TPU v7x, 32 devices: a whole 2x2x4 slice. The times are simulated.
32 devices in a mesh: dp: 4 (over z), w: 2 (over y), h: 4 (over x, core).
Axes of the slice: x: 2, y: 2, z: 4, core: 2. Of those that a mesh axis runs over, the one named last changes fastest.
Arguments:
- field: float32 [12, 64, 256, 512], P('dp', None, 'h', 'w')
- target: float32 [12, 64, 256, 512], P('dp', None, 'h', 'w')
- lat_weight: float32 [256], P('h')
- leg_fwd: float32 [128, 128, 256], P('w', None, 'h')
- leg_inv: float32 [128, 128, 256], P('w', None, 'h')
- spec_w: float32 [2, 128, 64, 64], replicated
- w_in: bfloat16 [64, 128], replicated
- w_out: bfloat16 [128, 64], replicated
Outputs:
- output 1: float32 [], replicated
- output 2: float32 [12, 64, 256, 512], P('dp', None, 'h', 'w')
- output 3: float32 [2, 128, 64, 64], P(None, 'h')
- output 4: float32 [64, 128], replicated
- output 5: float32 [128, 64], replicated
All inputs are finite; a program needn't handle non-finite values.
Results may differ from a plain program's by a relative error of at most 0.00126581.
Values sent between devices are 32-bit elements.
A program may use at most 1 GiB of HBM per device.

v0:
```python
import functools
import jax
import jax.numpy as jnp
from jax import lax
from jax.sharding import PartitionSpec as P

NORM_EPS = 1e-5
PRECISE = lax.Precision.HIGHEST


def precise_product(einsum_form, operand_a, operand_b):
    return jnp.einsum(einsum_form, operand_a, operand_b, precision=PRECISE, preferred_element_type=jnp.float32)


def lon_forward(grid_vals, num_modes):
    lon_spec = jnp.fft.rfft(grid_vals, axis=3, norm="ortho")[:, :, :, :num_modes]
    return jnp.stack([lon_spec.real, lon_spec.imag])


def lon_inverse(coeffs, lon_count):
    pad_width = ((0, 0), (0, 0), (0, 0), (0, lon_count // 2 + 1 - coeffs.shape[4]))
    padded = jnp.pad(lax.complex(coeffs[0], coeffs[1]), pad_width)
    return jnp.fft.irfft(padded, n=lon_count, axis=3, norm="ortho")


def spectral_mix(coeffs, kernel):
    einsum_form = "bilm,lio->bolm"
    real_part = precise_product(einsum_form, coeffs[0], kernel[0]) - precise_product(einsum_form, coeffs[1], kernel[1])
    imag_part = precise_product(einsum_form, coeffs[0], kernel[1]) + precise_product(einsum_form, coeffs[1], kernel[0])
    return jnp.stack([real_part, imag_part])


def spectral_input_grad(d_mixed, kernel):
    einsum_form = "bolm,lio->bilm"
    real_part = precise_product(einsum_form, d_mixed[0], kernel[0]) + precise_product(einsum_form, d_mixed[1], kernel[1])
    imag_part = precise_product(einsum_form, d_mixed[1], kernel[0]) - precise_product(einsum_form, d_mixed[0], kernel[1])
    return jnp.stack([real_part, imag_part])


def spectral_kernel_grad(coeffs, d_mixed):
    einsum_form = "bilm,bolm->lio"
    real_part = precise_product(einsum_form, coeffs[0], d_mixed[0]) + precise_product(einsum_form, coeffs[1], d_mixed[1])
    imag_part = precise_product(einsum_form, coeffs[0], d_mixed[1]) - precise_product(einsum_form, coeffs[1], d_mixed[0])
    return jnp.stack([real_part, imag_part])


def solution(mesh):
    dp_size = mesh.shape["dp"]
    w_size = mesh.shape["w"]
    h_size = mesh.shape["h"]
    grid_axes = ("h", "w")
    all_axes = ("dp", "h", "w")

    def degree_from_lat(spec_loc, table):
        part_sums = precise_product("mlt,xbctm->xbclm", table, spec_loc)
        return lax.psum_scatter(part_sums, "h", scatter_dimension=3, tiled=True)

    def lat_from_degree(coeffs, table):
        coeffs_all = lax.all_gather(coeffs, "h", axis=3, tiled=True)
        return precise_product("mlt,xbclm->xbctm", table, coeffs_all)

    def local_step(field, target, lat_weight, leg_fwd, leg_inv, spec_w, w_in, w_out):
        batch_loc, chan_count, lat_loc, lon_loc = field.shape
        lon_count = lon_loc * w_size
        num_modes = leg_fwd.shape[0] * w_size
        grid_points = lat_loc * h_size * lon_count
        total_points = batch_loc * dp_size * chan_count * grid_points
        chan_mean = lax.psum(jnp.sum(field, axis=(2, 3), keepdims=True), grid_axes) / grid_points
        centred = field - chan_mean
        variance = lax.psum(jnp.sum(centred * centred, axis=(2, 3), keepdims=True), grid_axes) / grid_points
        inv_std = lax.rsqrt(variance + NORM_EPS)
        normed = centred * inv_std
        lon_whole = lax.all_to_all(normed, "w", 1, 3, tiled=True)
        spec_half, fwd_pull = jax.vjp(functools.partial(lon_forward, num_modes=num_modes), lon_whole)
        spec_loc = lax.all_to_all(spec_half, "w", 4, 2, tiled=True)
        coeffs = degree_from_lat(spec_loc, leg_fwd)
        mixed = spectral_mix(coeffs, spec_w)
        back_loc = lat_from_degree(mixed, leg_inv)
        back_half = lax.all_to_all(back_loc, "w", 2, 4, tiled=True)
        y_half, inv_pull = jax.vjp(functools.partial(lon_inverse, lon_count=lon_count), back_half)
        y_grid = lax.all_to_all(y_half, "w", 3, 1, tiled=True)
        y_bf = y_grid.astype(jnp.bfloat16)
        hidden = jnp.einsum("bctp,cf->bftp", y_bf, w_in, preferred_element_type=jnp.float32)
        activation, gelu_pull = jax.vjp(jax.nn.gelu, hidden)
        act_bf = activation.astype(jnp.bfloat16)
        mlp_out = jnp.einsum("bftp,fc->bctp", act_bf, w_out, preferred_element_type=jnp.float32)
        residual = field + y_grid + mlp_out - target
        d_out = lat_weight[None, None, :, None] * residual
        loss = lax.psum(jnp.sum(d_out * residual), all_axes) / total_points
        d_out_bf = d_out.astype(jnp.bfloat16)
        grad_w_out = lax.psum(jnp.einsum("bftp,bctp->fc", act_bf, d_out_bf, preferred_element_type=jnp.float32), all_axes)
        d_act = jnp.einsum("bctp,fc->bftp", d_out_bf, w_out, preferred_element_type=jnp.float32)
        d_hidden = gelu_pull(d_act)[0].astype(jnp.bfloat16)
        grad_w_in = lax.psum(jnp.einsum("bctp,bftp->cf", y_bf, d_hidden, preferred_element_type=jnp.float32), all_axes)
        d_y = d_out + jnp.einsum("bftp,cf->bctp", d_hidden, w_in, preferred_element_type=jnp.float32)
        d_y_half = lax.all_to_all(d_y, "w", 1, 3, tiled=True)
        d_back_half = inv_pull(d_y_half)[0]
        d_back_loc = lax.all_to_all(d_back_half, "w", 4, 2, tiled=True)
        d_mixed = degree_from_lat(d_back_loc, leg_inv)
        grad_spec = lax.psum(spectral_kernel_grad(coeffs, d_mixed), ("dp", "w"))
        d_coeffs = spectral_input_grad(d_mixed, spec_w)
        d_spec_loc = lat_from_degree(d_coeffs, leg_fwd)
        d_spec_half = lax.all_to_all(d_spec_loc, "w", 2, 4, tiled=True)
        d_lon_whole = fwd_pull(d_spec_half)[0]
        d_normed = lax.all_to_all(d_lon_whole, "w", 3, 1, tiled=True)
        norm_stats = lax.psum(jnp.stack([jnp.sum(d_normed, axis=(2, 3), keepdims=True), jnp.sum(d_normed * normed, axis=(2, 3), keepdims=True)]), grid_axes) / grid_points
        d_field = d_out + inv_std * (d_normed - norm_stats[0] - normed * norm_stats[1])
        return loss, d_field, grad_spec, grad_w_in, grad_w_out

    grid_spec = P("dp", None, "h", "w")
    table_spec = P("w", None, "h")
    kernel_spec = P(None, "h", None, None)
    return jax.shard_map(local_step, mesh=mesh, in_specs=(grid_spec, grid_spec, P("h"), table_spec, table_spec, kernel_spec, P(), P()), out_specs=(P(), grid_spec, kernel_spec, P(), P()), check_vma=False)
```

profile of v0, /device:TPU:1, one launch (start us, length us, event | category | flops | bytes accessed | tf_op | source)
XLA Modules:
  0.0 4224.9 jit_solution(15567432658899933872)
XLA Ops:
  106.3 123.4 %all-to-all-done = f32[3,64,64,256]{3,2,0,1:T(8,128)} async-done(((f32[3,64,64,256]{3,2,0,1:T(8,128)}), f32[3,64,64,256]{3,2,0,1:T(8,128)}, u32[]{:S(2)}, u32[]{:S(2)}) %all-to-all-start) | async-done | bytes 12582944 | tf_op jit(solution)/shard_map/all_to_all | solution.py:73
  229.7 23.7 copy.201
  253.4 20.9 copy.202
  289.7 31.5 fusion.284
  321.2 35.2 fusion.62
  356.4 37.8 add_bitcast_fusion.2
  394.2 37.3 subtract_bitcast_fusion.1
  431.5 17.8 copy.307
  524.7 77.7 %all_to_all.118 = f32[2,1,786432]{2,1,0:T(1,128)} all-to-all(f32[2,1,786432]{2,1,0:T(1,128)} %reshape.95), channel_id=1, replica_groups=mesh['dp'=4,'w'=2,'h'=4] {'w'}, dimensions={0} | all-to-all | bytes 12582912 | tf_op jit(solution)/shard_map/all_to_all | solution.py:75
  602.9 23.2 reduce.8
  667.3 23.6 copy.212
  704.4 163.2 %reduce-scatter.5.cloned.1.call-done = f32[2,3,64,32,64]{4,2,1,0,3:T(8,128)} async-done(((f32[2,3,64,128,64]{4,2,1,0,3:T(8,128)}), f32[2,3,64,32,64]{4,2,1,0,3:T(8,128)}) %reduce-scatter.5.cloned.1.call-update) | async-done | bytes 3145744 | tf_op jit(solution)/shard_map/reduce_scatter | solution.py:56
  896.4 155.0 %all-gather.3.cloned.1.call-done = f32[2,3,64,128,64]{2,4,1,3,0:T(8,128)} async-done(((f32[2,3,64,32,64]{2,4,1,3,0:T(8,128)}), f32[2,3,64,128,64]{2,4,1,3,0:T(8,128)}) %all-gather.3.cloned.1.call-update) | async-done | bytes 12582928 | tf_op jit(solution)/shard_map/all_gather | solution.py:59
  1051.4 51.2 %fusion.79 = f32[2,3,64,64,64]{3,2,1,0,4:T(8,128)} fusion(f32[2,3,64,128,64]{2,4,1,3,0:T(8,128)} %all-gather.3.cloned.1.call-done, f32[64,128,64]{1,2,0:T(8,128)S(1)} %copy-done), kind=kOutput, calls=%fused_computation.127 | convolution fusion | flops 2415919104 | bytes 20971520 | tf_op jit(solution)/shard_map/mlt,xbclm->xbctm/dot_general | solution.py:12
  1139.1 69.4 %all-to-all-done.2 = f32[2,1,786432]{2,1,0:T(1,128)} async-done(((f32[2,1,786432]{2,1,0:T(1,128)}), f32[2,1,786432]{2,1,0:T(1,128)}, u32[]{:S(2)}, u32[]{:S(2)}) %all-to-all-start.2) | async-done | bytes 6291488 | tf_op jit(solution)/shard_map/all_to_all | solution.py:79
  1208.5 22.8 reduce.9
  1245.7 21.2 copy.406
  1355.1 23.4 copy.220
  1378.6 58.8 %fusion.21 = f32[3,32,64,4,128]{4,2,3,1,0:T(8,128)} fusion(f32[3,32,64,128,4]{2,1,4,3,0:T(8,128)} %bitcast.499), kind=kOutput, calls=%fused_computation.28 | convolution fusion | flops 4831920128 | bytes 25165824 | tf_op jit(solution)/shard_map/jvp(jit(fft)) | solution.py:23
  1449.4 23.4 copy.219
  1472.8 25.6 jvp_jit_fft__.802
  1504.4 60.5 %fusion.19 = f32[3,32,64,4,128]{4,2,3,1,0:T(8,128)} fusion(f32[3,32,64,128,4]{2,1,4,3,0:T(8,128)S(1)} %bitcast.502), kind=kOutput, calls=%fused_computation.26 | convolution fusion | flops 4831920128 | bytes 25165824 | tf_op jit(solution)/shard_map/jvp(jit(fft)) | solution.py:23
  1564.9 62.4 %fusion.281 = (f32[3,32,64,128,4]{3,2,4,1,0:T(8,128)}, f32[3,32,64,128,4]{3,2,4,1,0:T(8,128)}, f32[3,32,64,128,4]{3,2,4,1,0:T(8,128)}) fusion(f32[128,4]{0,1:T(4,128)S(1)} %get-tuple-element.73, f32[3,32,64,4,128]{4,2,3,1,0:T(8,128)} %fusion.19, f32[128,4]{0,1:T(4,128)S(1)} %get-tuple-element.72, f32[3,32,64,4,128]{4,2,3,1,0:T(8,128)} %fusion.21, ...), kind=kOutput, calls=%fused_computation.325 | convolution fusion | flops 4860215296 | bytes 75501568 | tf_op jit(solution)/shard_map/jvp(jit(fft)) | solution.py:23
  1627.3 35.3 fusion.56
  1662.7 27.0 fusion.52
  1689.7 43.3 %multiply_bitcast_fusion = f32[3,32,64,4,128]{4,3,2,1,0:T(4,128)} fusion(f32[3,32,64,128,4]{3,4,2,1,0:T(4,128)} %fusion.56, f32[3,32,64,128,4]{3,4,2,1,0:T(4,128)} %fusion.52, f32[3,32,64,128,4]{3,2,4,1,0:T(8,128)} %get-tuple-element.50), kind=kOutput, calls=%fused_computation.110 | convolution fusion | flops 166723664 | bytes 50331648 | tf_op jit(solution)/shard_map/jvp(jit(fft)) | solution.py:23
  1750.6 33.3 reshape.99
  1783.9 150.7 %all_to_all.119 = f32[2,1,1572864]{2,1,0:T(1,128)} all-to-all(f32[2,1,1572864]{2,1,0:T(1,128)} %reshape.99), channel_id=1, replica_groups=mesh['dp'=4,'w'=2,'h'=4] {'w'}, dimensions={0} | all-to-all | bytes 25165824 | tf_op jit(solution)/shard_map/all_to_all | solution.py:81
  1934.6 46.9 %reduce.10 = f32[2,1572864]{1,0:T(2,128)} reduce(f32[2,1,1572864]{2,1,0:T(1,128)} %all_to_all.119, f32[]{:T(128)} %broadcast.248), dimensions={1}, to_apply=%all_to_all.94.reduce_sub_computation | reduce | bytes 25165828 | tf_op jit(solution)/shard_map/all_to_all | solution.py:81
  1981.5 32.5 reshape.100
  2014.0 22.4 copy.228
  2056.7 32.7 fusion.35
  2089.4 25.8 fusion.6
  2157.6 134.9 %all-to-all-done.4 = f32[3,64,64,256]{3,2,0,1:T(8,128)} async-done(((f32[3,64,64,256]{3,2,0,1:T(8,128)}), f32[3,64,64,256]{3,2,0,1:T(8,128)}, u32[]{:S(2)}, u32[]{:S(2)}) %all-to-all-start.4) | async-done | bytes 12582944 | tf_op jit(solution)/shard_map/all_to_all | solution.py:96
  2304.5 23.6 copy.234
  2328.1 20.9 copy.235
  2364.5 31.2 fusion.278
  2395.7 35.3 fusion.50
  2430.9 37.3 subtract_bitcast_fusion
  2468.2 37.8 add_bitcast_fusion.1
  2506.1 17.9 copy.310
  2590.5 76.5 %all_to_all.120 = f32[2,1,786432]{2,1,0:T(1,128)} all-to-all(f32[2,1,786432]{2,1,0:T(1,128)} %reshape.101), channel_id=1, replica_groups=mesh['dp'=4,'w'=2,'h'=4] {'w'}, dimensions={0} | all-to-all | bytes 12582912 | tf_op jit(solution)/shard_map/all_to_all | solution.py:98
  2667.0 23.0 reduce.11
  2730.9 23.6 copy.244
  2754.6 176.2 %reduce-scatter.7.cloned.1.call-done = f32[2,3,64,32,64]{4,2,1,0,3:T(8,128)} async-done(((f32[2,3,64,128,64]{4,2,1,0,3:T(8,128)}), f32[2,3,64,32,64]{4,2,1,0,3:T(8,128)}) %reduce-scatter.7.cloned.1.call-update) | async-done | bytes 3145744 | tf_op jit(solution)/shard_map/reduce_scatter | solution.py:56
  2959.1 155.0 %all-gather.5.cloned.1.call-done = f32[2,3,64,128,64]{2,4,1,3,0:T(8,128)} async-done(((f32[2,3,64,32,64]{2,4,1,3,0:T(8,128)}), f32[2,3,64,128,64]{2,4,1,3,0:T(8,128)}) %all-gather.5.cloned.1.call-update) | async-done | bytes 12582928 | tf_op jit(solution)/shard_map/all_gather | solution.py:59
  3114.1 65.7 %fusion.82 = f32[2,3,64,64,64]{3,2,1,0,4:T(8,128)} fusion(f32[2,3,64,128,64]{2,4,1,3,0:T(8,128)} %all-gather.5.cloned.1.call-done, f32[64,128,64]{1,2,0:T(8,128)} %param.14), kind=kOutput, calls=%fused_computation.128 | convolution fusion | flops 2415919104 | bytes 20971520 | tf_op jit(solution)/shard_map/mlt,xbclm->xbctm/dot_general | solution.py:12
  3209.4 78.7 %all_to_all.121 = f32[2,1,786432]{2,1,0:T(1,128)} all-to-all(f32[2,1,786432]{2,1,0:T(1,128)} %reshape.103), channel_id=1, replica_groups=mesh['dp'=4,'w'=2,'h'=4] {'w'}, dimensions={0} | all-to-all | bytes 12582912 | tf_op jit(solution)/shard_map/all_to_all | solution.py:103
  3288.2 23.0 reduce.12
  3440.6 19.6 copy.250
  3460.2 58.6 %fusion.7 = f32[3,32,64,4,128]{4,2,3,1,0:T(8,128)} fusion(f32[3,32,64,128,4]{2,1,0,4,3:T(8,128)} %bitcast.503), kind=kOutput, calls=%fused_computation.11 | convolution fusion | flops 4831920128 | bytes 25165824 | tf_op jit(solution)/shard_map/transpose(jvp(jit(fft)))/jit(_rfft_transpose)/jit(fft) | solution.py:16
  3527.6 60.6 %fusion.9 = f32[3,32,64,4,128]{4,2,3,1,0:T(8,128)} fusion(f32[3,32,64,128,4]{2,1,0,4,3:T(8,128)S(1)} %bitcast.498), kind=kOutput, calls=%fused_computation.13 | convolution fusion | flops 4831920128 | bytes 25165824 | tf_op jit(solution)/shard_map/transpose(jvp(jit(fft)))/jit(_rfft_transpose)/jit(fft) | solution.py:16
  3588.3 25.3 jit_fft_.139
  3613.6 62.5 %fusion.275 = (f32[3,32,64,128,4]{3,2,4,1,0:T(8,128)}, f32[3,32,64,128,4]{3,2,4,1,0:T(8,128)}, f32[3,32,64,128,4]{3,2,4,1,0:T(8,128)}) fusion(f32[128,4]{0,1:T(4,128)S(1)} %copy-done.17, f32[3,32,64,4,128]{4,2,3,1,0:T(8,128)} %fusion.7, f32[128,4]{0,1:T(4,128)S(1)} %copy-done.19, f32[3,32,64,4,128]{4,2,3,1,0:T(8,128)} %fusion.9, ...), kind=kOutput, calls=%fused_computation.323 | convolution fusion | flops 4860215296 | bytes 75501568 | tf_op jit(solution)/shard_map/transpose(jvp(jit(fft)))/jit(_rfft_transpose)/jit(fft) | solution.py:16
  3676.1 35.8 fusion.42
  3711.9 27.0 fusion.40
  3738.9 42.0 add_bitcast_fusion
  3798.6 33.3 reshape.105
  3889.6 109.4 %all-to-all-done.7 = f32[2,1,1572864]{2,1,0:T(1,128)} async-done(((f32[2,1,1572864]{2,1,0:T(1,128)}), f32[2,1,1572864]{2,1,0:T(1,128)}, u32[]{:S(2)}, u32[]{:S(2)}) %all-to-all-start.7) | async-done | bytes 12582944 | tf_op jit(solution)/shard_map/all_to_all | solution.py:105
  3999.0 46.7 %reduce.13 = f32[2,1572864]{1,0:T(2,128)} reduce(f32[2,1,1572864]{2,1,0:T(1,128)} %all-to-all-done.7, f32[]{:T(128)} %broadcast.248), dimensions={1}, to_apply=%all_to_all.106.reduce_sub_computation | reduce | bytes 25165828 | tf_op jit(solution)/shard_map/all_to_all | solution.py:105
  4045.7 32.3 reshape.106
  4077.9 22.4 copy.259
  4134.3 22.0 multiply_add_fusion
  4156.3 40.3 all-reduce.18
  (198 shorter events, 970.7 us)
Async XLA Ops:
  7.2 1044.2 %copy-start = (f32[64,128,64]{1,2,0:T(8,128)S(1)}, f32[64,128,64]{1,2,0:T(8,128)}, u32[]{:S(2)}) copy-start(f32[64,128,64]{1,2,0:T(8,128)} %param.15) | copy-start | bytes 6291460
  27.6 40.4 copy-start.21
  50.9 17.0 copy-start.23
  84.7 145.0 %all-to-all-start = ((f32[3,64,64,256]{3,2,0,1:T(8,128)}), f32[3,64,64,256]{3,2,0,1:T(8,128)}, u32[]{:S(2)}, u32[]{:S(2)}) async-start(f32[3,64,64,256]{3,2,0,1:T(8,128)} %copy.200), calls=%async_computation | async-start | bytes 25165824 | tf_op jit(solution)/shard_map/all_to_all | solution.py:73
  93.1 774.5 %reduce-scatter.5.cloned.1.call-start = ((), (), s32[]{:S(2)}) async-start(), calls=%async_computation.10 | async-start | bytes 31457280 | tf_op jit(solution)/shard_map/reduce_scatter | solution.py:56
  93.2 196.5 %copy-start.12 = (f32[128,4]{0,1:T(4,128)}, f32[128,4]{0,1:T(4,128)S(1)}, u32[]{:S(2)}) copy-start(f32[128,4]{0,1:T(4,128)S(1)} %get-tuple-element.70) | copy-start | bytes 6148
  93.2 196.5 %copy-start.14 = (f32[128,4]{0,1:T(4,128)}, f32[128,4]{0,1:T(4,128)S(1)}, u32[]{:S(2)}) copy-start(f32[128,4]{0,1:T(4,128)S(1)} %get-tuple-element.71) | copy-start | bytes 6148
  640.4 11.5 copy-start.11
  690.8 0.7 copy-start.29
  690.9 360.5 %all-gather.3.cloned.1.call-start = ((), (), s32[]{:S(2)}) async-start(), calls=%async_computation.11 | async-start | bytes 31457280 | tf_op jit(solution)/shard_map/all_gather | solution.py:59
  700.7 186.3 %copy-start.7 = (f32[1,32,64,64]{3,2,1,0:T(8,128)}, f32[1,32,64,64]{3,2,1,0:T(8,128)S(1)}, u32[]{:S(2)}) copy-start(f32[1,32,64,64]{3,2,1,0:T(8,128)S(1)} %copy.317) | copy-start | bytes 1572868
  867.6 14.3 copy-start.3
  867.6 19.4 copy-start.9
  1132.8 75.8 %all-to-all-start.2 = ((f32[2,1,786432]{2,1,0:T(1,128)}), f32[2,1,786432]{2,1,0:T(1,128)}, u32[]{:S(2)}, u32[]{:S(2)}) async-start(f32[2,1,786432]{2,1,0:T(1,128)} %reshape.97), calls=%async_computation.3 | async-start | bytes 12582912 | tf_op jit(solution)/shard_map/all_to_all | solution.py:79
  1139.1 425.8 %copy-start.16 = (f32[128,4]{0,1:T(4,128)}, f32[128,4]{0,1:T(4,128)S(1)}, u32[]{:S(2)}) copy-start(f32[128,4]{0,1:T(4,128)S(1)} %get-tuple-element.72) | copy-start | bytes 6148
  1139.1 425.8 %copy-start.18 = (f32[128,4]{0,1:T(4,128)}, f32[128,4]{0,1:T(4,128)S(1)}, u32[]{:S(2)}) copy-start(f32[128,4]{0,1:T(4,128)S(1)} %get-tuple-element.73) | copy-start | bytes 6148
  1472.8 31.6 copy-start.1
  1627.3 35.3 copy-start.6
  2036.5 8.2 copy-start.20
  2044.7 12.0 copy-start.25
  2056.7 32.7 copy-start.26
  2148.8 143.8 %all-to-all-start.4 = ((f32[3,64,64,256]{3,2,0,1:T(8,128)}), f32[3,64,64,256]{3,2,0,1:T(8,128)}, u32[]{:S(2)}, u32[]{:S(2)}) async-start(f32[3,64,64,256]{3,2,0,1:T(8,128)} %copy.233), calls=%async_computation.5 | async-start | bytes 25165824 | tf_op jit(solution)/shard_map/all_to_all | solution.py:96
  2157.2 773.6 %reduce-scatter.7.cloned.1.call-start = ((), (), s32[]{:S(2)}) async-start(), calls=%async_computation.12 | async-start | bytes 31457280 | tf_op jit(solution)/shard_map/reduce_scatter | solution.py:56
  2349.1 15.4 copy-start.13
  2349.1 15.4 copy-start.15
  2552.3 10.7 slice-start.10
  2754.5 183.4 %copy-start.8 = (f32[1,32,64,64]{3,2,1,0:T(8,128)S(1)}, f32[1,32,64,64]{3,2,1,0:T(8,128)}, u32[]{:S(2)}) copy-start(f32[1,32,64,64]{3,2,1,0:T(8,128)} %copy-done.7) | copy-start | bytes 1572868
  2754.6 359.5 %all-gather.5.cloned.1.call-start = ((), (), s32[]{:S(2)}) async-start(), calls=%async_computation.13 | async-start | bytes 31457280 | tf_op jit(solution)/shard_map/all_gather | solution.py:59
  2930.8 14.1 copy-start.4
  2930.8 19.2 copy-start.10
  3338.5 11.3 copy-start.28
  3440.6 78.2 %slice-start = ((s8[25165824]{0:T(1024)(128)(4,1)}), s8[4194304]{0:T(1024)(128)(4,1)S(1)}, s32[]{:S(2)}) async-start(s8[25165824]{0:T(1024)(128)(4,1)} %bitcast.496), calls=%async_computation.15 | async-start | bytes 8388608
  3440.6 78.2 %slice-start.1 = ((s8[25165824]{0:T(1024)(128)(4,1)}), s8[4194304]{0:T(1024)(128)(4,1)S(1)}, s32[]{:S(2)}) async-start(s8[25165824]{0:T(1024)(128)(4,1)} %bitcast.496), calls=%async_computation.16 | async-start | bytes 8388608
  3440.6 78.2 %slice-start.2 = ((s8[25165824]{0:T(1024)(128)(4,1)}), s8[4194304]{0:T(1024)(128)(4,1)S(1)}, s32[]{:S(2)}) async-start(s8[25165824]{0:T(1024)(128)(4,1)} %bitcast.496), calls=%async_computation.17 | async-start | bytes 8388608
  3460.2 58.6 %slice-start.3 = ((s8[25165824]{0:T(1024)(128)(4,1)}), s8[4194304]{0:T(1024)(128)(4,1)S(1)}, s32[]{:S(2)}) async-start(s8[25165824]{0:T(1024)(128)(4,1)} %bitcast.496), calls=%async_computation.18 | async-start | bytes 8388608
  3460.2 58.6 %slice-start.4 = ((s8[25165824]{0:T(1024)(128)(4,1)}), s8[4194304]{0:T(1024)(128)(4,1)S(1)}, s32[]{:S(2)}) async-start(s8[25165824]{0:T(1024)(128)(4,1)} %bitcast.496), calls=%async_computation.19 | async-start | bytes 8388608
  3460.2 58.6 %slice-start.5 = ((s8[25165824]{0:T(1024)(128)(4,1)}), s8[4194304]{0:T(1024)(128)(4,1)S(1)}, s32[]{:S(2)}) async-start(s8[25165824]{0:T(1024)(128)(4,1)} %bitcast.496), calls=%async_computation.20 | async-start | bytes 8388608
  3588.3 25.3 copy-start.17
  3588.3 25.3 copy-start.19
  3676.1 35.8 copy-start.5
  3831.9 167.1 %all-to-all-start.7 = ((f32[2,1,1572864]{2,1,0:T(1,128)}), f32[2,1,1572864]{2,1,0:T(1,128)}, u32[]{:S(2)}, u32[]{:S(2)}) async-start(f32[2,1,1572864]{2,1,0:T(1,128)} %reshape.105), calls=%async_computation.9 | async-start | bytes 25165824 | tf_op jit(solution)/shard_map/all_to_all | solution.py:105
  3840.3 9.1 copy-start.27
  3840.3 373.5 %all-reduce.17.cloned.1.call-start = ((), (), s32[]{:S(2)}) async-start(), calls=%async_computation.14 | async-start | bytes 4194304 | tf_op jit(solution)/shard_map/psum | solution.py:100
  3840.4 25.7 slice-start.6
  3849.5 16.6 slice-start.7
  3866.1 18.0 slice-start.8
  3872.0 12.1 slice-start.9
  4100.4 8.2 copy-start.2
  4100.4 8.2 copy-start.22
  4100.4 8.2 copy-start.24
Sparse Core Ops, SparseCore 0:
  691.0 176.5 reduce-scatter.4
  896.5 154.8 all-gather.2
  2754.7 176.0 reduce-scatter.6
  2959.2 154.8 all-gather.4
  3889.7 116.2 all-reduce.16
where the time goes:
time: 4240 us; the launch traced here: 4220 us
  matrix products  1230 us (29%)
  waiting for transfers between devices  1090 us (26%)
  local copies, waits for them, and re-layouts  925 us (22%)
  other arithmetic  467 us (11%)
  blocking collectives  464 us (11%)
    another operation x12, matrix products, lon_forward(): jnp.fft.rfft(grid_vals, axis=3, norm='ortho')[:, :, :, :num_modes]  457 us
    another operation x11, matrix products, lon_inverse(): return jnp.fft.irfft(padded, n=lon_count, axis=3, norm='ortho')  444 us
    reduce_scatter x2, waiting for transfers between devices, degree_from_lat(): return lax.psum_scatter(part_sums, 'h', scatter_dimension=3, tiled=True)  339 us
    unnamed x99, local copies, waits for them, and re-layouts  320 us
    all_gather x2, waiting for transfers between devices, lat_from_degree(): coeffs_all = lax.all_gather(coeffs, 'h', axis=3, tiled=True)  310 us
    dot_general x16, matrix products, precise_product(): jnp.einsum(einsum_form, operand_a, operand_b, precision=PRECISE, preferre...  218 us
    all_to_all x1, blocking collectives, local_step(): y_grid = lax.all_to_all(y_half, 'w', 3, 1, tiled=True)  151 us
    another operation x10, local copies, waits for them, and re-layouts, lon_forward(): jnp.fft.rfft(grid_vals, axis=3, norm='ortho')[:, :, :, :num_modes]  138 us
  transfers between devices with their start and end apart: 9, of which 8 were waited for; matrix products, arithmetic and copies ran while one was open for 5% of the time, Pallas kernels for 0%

commit v1 on v0

v1 whole, which is shorter than its diff:
```python
import math
import numpy as np
import jax
import jax.numpy as jnp
from jax import lax
from jax.experimental import pallas as pl
from jax.experimental.pallas import tpu as pltpu
from jax.sharding import PartitionSpec as P

NORM_EPS = 1e-5
HI = lax.Precision.HIGHEST
F32 = jnp.float32
BF16 = jnp.bfloat16
MESH = pl.DeviceIdType.MESH
GELU_A = math.sqrt(2.0 / math.pi)
GELU_B = 0.044715

NB, CH, NT, NN = 3, 64, 64, 256
NM, NL = 128, 128
LON, LAT, BATCH = 512, 256, 12
POINTS = LON * LAT
TOTAL = POINTS * BATCH * CH
LANES = NB * 2 * CH
SUB, LN = 8, 128
T8 = NT // SUB
GROUPS = NM // SUB
PLANE = 8
H_OF_PAIR = (0, 0, 3, 3, 1, 1, 2, 2)
BLOCK = SUB * SUB
PLACES = GROUPS + 1
DATA = PLACES * BLOCK
STAT = DATA
GRAD = DATA + SUB
ROWS = GRAD + SUB
SPARE = BLOCK
STEP = 3 * BLOCK
COUNT = 6
NN_DIMS, NT_DIMS, TN_DIMS = ((1,), (0,)), ((1,), (1,)), ((0,), (0,))
SUM_STEPS = ((0, 2), (2, 5), (5, 8), (8, 11), (11, 14), (14, 16))
GATHER_STEPS = ((13, 16), (10, 13), (7, 10), (4, 7), (1, 4), (0, 1))

SMEM = pl.BlockSpec(memory_space=pltpu.SMEM)
VMEM = pl.BlockSpec(memory_space=pltpu.VMEM)
ANY = pl.BlockSpec(memory_space=pl.ANY)


def dot(a, b, dims=NN_DIMS):
    return lax.dot_general(a, b, (dims, ((), ())), precision=HI, preferred_element_type=F32)


def mxu(a, b, dims=NN_DIMS):
    return lax.dot_general(a, b, (dims, ((), ())), preferred_element_type=F32)


def call(kernel, outs, scratch=(), cid=None, **kw):
    extra = {} if cid is None else {"collective_id": cid, "has_side_effects": True}
    return pl.pallas_call(
        kernel,
        out_shape=tuple(jax.ShapeDtypeStruct(s, F32) for s in outs),
        scratch_shapes=list(scratch),
        compiler_params=pltpu.CompilerParams(vmem_limit_bytes=62 << 20, **extra),
        **kw,
    )


def vmem(*shape, dtype=F32):
    return pltpu.VMEM(shape, dtype)


def dma_sems(*shape):
    return pltpu.SemaphoreType.DMA(shape)


def rows(lo, hi):
    return pl.ds(lo, hi - lo)


def dft_matrix():
    theta = 2.0 * np.pi * ((np.arange(NN)[:, None] * np.arange(NM)[None, :]) % LON) / LON
    return (np.concatenate([np.cos(theta), -np.sin(theta)], axis=1) / math.sqrt(LON)).astype(np.float32)


def signed(base, half, weight):
    m = lax.broadcasted_iota(jnp.int32, base.shape, 1) % NM
    out = jnp.where((m % 2) * half == 1, -base, base)
    return jnp.where(m == 0, out, weight * out) if weight > 1 else out


def to_orders(lines, ft):
    z = dot(lines, ft).reshape(SUB, CH, NN)
    z = jnp.concatenate([z[:, :, :NM], z[:, :, NM:]], axis=1)
    return jnp.swapaxes(jnp.swapaxes(z, 1, 2), 0, 1)


def to_grid(orders, ft):
    u = jnp.swapaxes(jnp.swapaxes(orders, 0, 1), 1, 2)
    u = jnp.concatenate([u[:, :CH, :], u[:, CH:, :]], axis=2).reshape(SUB * CH, NN)
    return dot(u, ft)


def place_of_block(j):
    k = min(j, GROUPS - 1 - j)
    return H_OF_PAIR[k] // 2, H_OF_PAIR[k] % 2, k % 2


def sum_position(j, g):
    k = min(j, GROUPS - 1 - j)
    return 2 * g + 1 if j < SUB else jnp.where(g <= k, 2 * g, k + 1 + g)


def chunk(i, share):
    lo = i * STEP
    hi = lo + STEP if i < COUNT - 1 else ROWS
    return lo, lo + (hi - lo) * share // BLOCK * SUB, hi


class Place:
    def __init__(self):
        self.h, self.y, self.z = lax.axis_index("h"), lax.axis_index("w"), lax.axis_index("dp")
        self.x, self.c = self.h // 2, self.h % 2
        self.slot = 2 * self.h + self.y
        self.low = self.h < 2
        self.pair = jnp.where(self.low, 4 * self.h, 14 - 4 * self.h) + self.y
        self.sibling = {"h": 2 * self.x + 1 - self.c}
        self.xn = {"h": 2 * (1 - self.x) + self.c}
        self.yn = {"w": 1 - self.y}

    def plane(self, r):
        s = (self.slot + r) % PLANE
        return {"h": s // 2, "w": s % 2}

    def greet(self, others):
        barrier = pltpu.get_barrier_semaphore()
        for other in others:
            pl.semaphore_signal(barrier, inc=1, device_id=other, device_id_type=MESH)
        pl.semaphore_wait(barrier, len(others))


def send(src, dst, sems, i, to):
    return pltpu.make_async_remote_copy(
        src_ref=src, dst_ref=dst, send_sem=sems.at[0, i], recv_sem=sems.at[1, i], device_id=to, device_id_type=MESH
    )


CB = 16
PIECES = CH // CB
HALF_TABLE = (SUB, SUB, NT, NL)


def near_far(k):
    return pl.ds(pl.multiple_of(SUB * k, SUB), SUB), pl.ds(pl.multiple_of(SUB * (GROUPS - 1 - k), SUB), SUB)


def front_kernel(x_hbm, p_hbm, w_hbm, base_ref, z_hbm, p_peer, mu_ref, inv_ref, c0_ref, kern_ref,
                 xbuf, wbuf, p0, cols, pay, sbuf, zbuf, ftbuf, turned, own, s_x, s_w, s_z, s_p, s_st):
    place = Place()
    near, far = near_far(place.pair)

    def load_x(n):
        b, part = n // PIECES, pl.ds(n % PIECES * CB, CB)
        return pltpu.make_async_copy(x_hbm.at[b, part], xbuf.at[b, part], s_x.at[n])

    def load_w(i):
        return pltpu.make_async_copy(w_hbm.at[i], wbuf.at[i], s_w.at[i])

    def load_p0():
        return pltpu.make_async_copy(p_hbm.at[0, 0], p0, s_w.at[2])

    def give_p(g):
        return send(p_hbm.at[g], p_peer.at[g], s_p, g, place.yn)

    load_p0().start()
    for n in range(NB * PIECES):
        load_x(n).start()
    for i in range(2):
        load_w(i).start()
    others = range(1, PLANE)
    place.greet([place.plane(r) for r in others])

    @pl.loop(0, SUB)
    def _(g):
        give_p(g).start()

    cols[...] = jnp.zeros_like(cols)
    for n in range(NB * PIECES):
        load_x(n).wait()
        v = xbuf[n // PIECES, n % PIECES * CB:(n % PIECES + 1) * CB]
        mean = jnp.sum(jnp.sum(v, axis=1, keepdims=True), axis=2, keepdims=True) / (NT * NN)
        diff = v - mean
        m2 = jnp.sum(jnp.sum(diff * diff, axis=1, keepdims=True), axis=2, keepdims=True)
        lane = lax.broadcasted_iota(jnp.int32, (CB, 1, LN), 2)
        cols[pl.ds(n * CB, CB)] = jnp.where(lane < CH, mean, m2).reshape(CB, LN)
    wide = cols[...].T
    load_p0().wait()
    p1 = jnp.where(place.y == 0, jnp.sum(p0[...], axis=0, keepdims=True), 0.0)
    pay[...] = jnp.concatenate([
        wide[:1], wide[CH:CH + 1], jnp.concatenate([p1, p1], axis=1), jnp.zeros((SUB - 3, NN), F32)
    ], axis=0)

    def give_stats(r):
        return send(pay, sbuf.at[place.slot], s_st, r, place.plane(r))

    for r in others:
        give_stats(r).start()
    sbuf[place.slot] = pay[...]
    ftbuf[...] = signed(base_ref[...], place.y, 1)

    for i in range(2):
        load_w(i).wait()

    @pl.loop(0, CH)
    def _(i):
        turned[...] = jnp.concatenate([wbuf[0, i], wbuf[1, i]], axis=0).T
        own[i, :SUB] = turned[near]
        own[i, SUB:] = turned[far]

    top = jnp.swapaxes(own[...], 0, 1)
    kern_ref[:, :CH] = top
    kern_ref[:, CH:] = jnp.concatenate([-top[:, :, CH:], top[:, :, :CH]], axis=2)

    for r in others:
        give_stats(r).wait_recv()
    means, m2s, p1s = (jnp.concatenate([sbuf[s, n:n + 1] for s in range(PLANE)], axis=0) for n in range(3))
    mu = jnp.sum(means, axis=0, keepdims=True) / PLANE
    dev = means - mu
    var = (jnp.sum(m2s, axis=0, keepdims=True) + (NT * NN) * jnp.sum(dev * dev, axis=0, keepdims=True)) / POINTS
    c0 = math.sqrt(LON) * jnp.sum(p1s, axis=0, keepdims=True)
    mu_ref[...], inv_ref[...], turned[...] = (
        jnp.broadcast_to(v, (LN, NN)).T[:n] for v, n in ((mu, NB * CH), (lax.rsqrt(var + NORM_EPS), NB * CH), (c0, NL))
    )
    c0_ref[:SUB] = turned[near]
    c0_ref[SUB:] = turned[far]

    def store_z(n):
        t = pl.multiple_of(n % T8 * SUB, SUB)
        lanes = pl.multiple_of(n // T8 * LN, LN)
        return pltpu.make_async_copy(zbuf.at[n % 2], z_hbm.at[:, pl.ds(t, SUB), pl.ds(lanes, LN)], s_z.at[n % 2])

    @pl.loop(0, NB * T8)
    def _(n):
        @pl.when(n >= 2)
        def _():
            store_z(n - 2).wait()

        b = n // T8
        xt = jnp.swapaxes(xbuf[b, :, pl.ds(pl.multiple_of(n % T8 * SUB, SUB), SUB), :], 0, 1)
        chans = pl.ds(pl.multiple_of(b * CH, CH), CH)
        xn = (xt - mu_ref[chans, :1]) * inv_ref[chans, :1]
        zbuf[n % 2] = to_orders(xn.reshape(SUB * CH, NN), ftbuf[...])
        store_z(n).start()

    for n in range(2):
        store_z(NB * T8 - 2 + n).wait()
    for r in others:
        give_stats(r).wait_send()

    @pl.loop(0, SUB)
    def _(g):
        give_p(g).wait()


def front(x, p_own, spec_w, base, cid):
    return call(
        front_kernel,
        [(NM, NT, LANES), HALF_TABLE, (NB * CH, LN), (NB * CH, LN), (2 * SUB, LN), (2 * SUB, LN, LN)],
        [
            vmem(NB, CH, NT, NN), vmem(2, CH, CH, NL), vmem(NT, NL), vmem(NN, LN), vmem(SUB, NN), vmem(PLANE, SUB, NN),
            vmem(2, NM, SUB, LN), vmem(NN, NN), vmem(NL, LN), vmem(CH, 2 * SUB, LN),
            dma_sems(NB * PIECES), dma_sems(3), dma_sems(2), dma_sems(2, SUB), dma_sems(2, PLANE),
        ],
        cid=cid,
        in_specs=[ANY, ANY, ANY, VMEM],
        out_specs=(ANY, ANY, VMEM, VMEM, VMEM, VMEM),
        name="front",
    )(x, p_own, spec_w, base)


def table_loader(own, peer, tbuf, sems, y):
    def copy(src, g):
        return pltpu.make_async_copy(src.at[g % SUB], tbuf.at[g], sems.at[g])

    def start(g):
        @pl.when(g // SUB == y)
        def _():
            copy(own, g).start()

        @pl.when(g // SUB != y)
        def _():
            copy(peer, g).start()

    def wait(g):
        copy(own, g).wait()

    return start, wait


def quarters(lo, hi):
    return [(max(lo, 4 * k), min(hi, 4 * k + 4), k) for k in range(4) if max(lo, 4 * k) < min(hi, 4 * k + 4)]


def analyze_kernel(share, with_q, *refs):
    if with_q:
        t_own, t_peer, z_hbm, ext_ref, q_own, out_ref, q_peer, *rest = refs
    else:
        t_own, t_peer, z_hbm, ext_ref, out_ref, *rest = refs
    tbuf, zbuf, part, sib, rx, ry, fx, fy, s_t, s_z, s_q, s_sib, s_x, s_y, s_fx, s_fy = rest
    p = Place()
    x, c, y = p.x, p.c, p.y
    start_t, wait_t = table_loader(t_own, t_peer, tbuf, s_t, y)

    def load_z(g):
        return pltpu.make_async_copy(z_hbm.at[g], zbuf.at[g], s_z.at[g])

    @pl.loop(0, GROUPS)
    def _(g):
        start_t(g)
        load_z(g).start()

    p.greet([p.sibling, p.xn, p.yn])
    for d in range(PLANE):
        part[d // 4, d // 2 % 2, d % 2, STAT:GRAD] = ext_ref[SUB * d:SUB * (d + 1)]
        part[d // 4, d // 2 % 2, d % 2, GRAD:ROWS] = jnp.zeros((SUB, LANES), F32)

    def give_q(g):
        return send(q_own.at[g], q_peer.at[g], s_q, g, p.yn)

    def compute(lo, hi, k):
        @pl.loop(lo, hi)
        def _(g):
            wait_t(g)
            load_z(g).wait()
            for m in range(SUB):
                r = dot(tbuf[g, m].T[4 * SUB * k:], zbuf[g, m])
                for n in range(GROUPS - 4 * k):
                    j = 4 * k + n
                    row = sum_position(j, g) * BLOCK + SUB * m
                    if n < 4:
                        row = jnp.where(j >= g, row, ROWS)
                    xj, cj, yj = place_of_block(j)
                    part[xj, cj, yj, pl.ds(pl.multiple_of(row, SUB), SUB), :] = r[SUB * n:SUB * (n + 1)]

    def to_sibling(i):
        lo, _, hi = chunk(i, share)
        return send(part.at[:, 1 - c, :, rows(lo, hi)], sib.at[:, :, rows(lo, hi)], s_sib, i, p.sibling)

    def to_x(i):
        lo, mid, _ = chunk(i, share)
        return send(part.at[1 - x, c, :, rows(lo, mid)], rx.at[:, rows(lo, mid)], s_x, i, p.xn)

    def to_y(i):
        _, mid, hi = chunk(i, share)
        return send(part.at[:, c, 1 - y, rows(mid, hi)], ry.at[:, rows(mid, hi)], s_y, i, p.yn)

    def forward_y(i):
        lo, mid, _ = chunk(i, share)
        return send(part.at[x, c, 1 - y, rows(lo, mid)], fy.at[rows(lo, mid)], s_fy, i, p.yn)

    def forward_x(i):
        _, mid, hi = chunk(i, share)
        return send(part.at[1 - x, c, y, rows(mid, hi)], fx.at[rows(mid, hi)], s_fx, i, p.xn)

    def chip_sum(i):
        lo, _, hi = chunk(i, share)
        to_sibling(i).wait_recv()
        for a in range(2):
            for b in range(2):
                part[a, c, b, rows(lo, hi)] += sib[a, b, rows(lo, hi)]
        to_x(i).start()
        to_y(i).start()
        if with_q:
            give_q(i).start()

    def half_sum(i):
        lo, mid, hi = chunk(i, share)
        to_x(i).wait_recv()
        part[x, c, 1 - y, rows(lo, mid)] += rx[1 - y, rows(lo, mid)]
        forward_y(i).start()
        to_y(i).wait_recv()
        part[1 - x, c, y, rows(mid, hi)] += ry[1 - x, rows(mid, hi)]
        forward_x(i).start()
        out_ref[rows(lo, mid)] = part[x, c, y, rows(lo, mid)] + rx[y, rows(lo, mid)]
        out_ref[rows(mid, hi)] = part[x, c, y, rows(mid, hi)] + ry[x, rows(mid, hi)]

    def last_sum(i):
        lo, mid, hi = chunk(i, share)
        forward_y(i).wait_recv()
        out_ref[rows(lo, mid)] += fy[rows(lo, mid)]
        forward_x(i).wait_recv()
        out_ref[rows(mid, hi)] += fx[rows(mid, hi)]

    if with_q:
        for g in (COUNT, COUNT + 1):
            give_q(g).start()
    for i in range(COUNT):
        for step in quarters(*SUM_STEPS[i]):
            compute(*step)
        to_sibling(i).start()
        if i > 0:
            chip_sum(i - 1)
    chip_sum(COUNT - 1)
    for i in range(COUNT + 2):
        if i < COUNT:
            half_sum(i)
        if i > 1:
            last_sum(i - 2)
    for i in range(COUNT):
        for copy in (to_sibling, to_x, to_y, forward_x, forward_y):
            copy(i).wait_send()
    if with_q:
        for g in range(SUB):
            give_q(g).wait()


def analyze(table, z, ext, cid, q_own=None):
    with_q = q_own is not None
    share = 7 if with_q else 4
    half = vmem(ROWS, LANES)
    pair = vmem(2, ROWS, LANES)
    outs = call(
        lambda *refs: analyze_kernel(share, with_q, *refs),
        [(ROWS, LANES)] + [HALF_TABLE] * with_q,
        [
            vmem(GROUPS, SUB, NT, NL), vmem(GROUPS, SUB, NT, LANES), vmem(2, 2, 2, ROWS + SPARE, LANES), vmem(2, 2, ROWS, LANES),
            pair, pair, half, half,
            dma_sems(GROUPS), dma_sems(GROUPS), dma_sems(2, SUB),
        ] + [dma_sems(2, COUNT)] * 5,
        cid=cid,
        in_specs=[ANY, ANY, ANY, VMEM] + [ANY] * with_q,
        out_specs=(VMEM,) + (ANY,) * with_q,
        name=f"analyze_{cid}",
    )(*table, z.reshape(GROUPS, SUB, NT, LANES), ext, *([q_own] * with_q))
    return outs if with_q else outs[0]


def synth_kernel(with_grads, *refs):
    if with_grads:
        t_own, t_peer, own_ref, dk_ref, u_hbm, ext_ref, spec_ref, *rest = refs
        *rest, zin, kin, zg, s_zk, s_zg, s_kin, s_kz = rest
    else:
        t_own, t_peer, own_ref, u_hbm, ext_ref, *rest = refs
    tbuf, ubuf, ball, s_t, s_u, s_sib, s_x, s_y, s_dx, s_dy, s_sx, s_sy, s_sd = rest
    p = Place()
    x, c, y = p.x, p.c, p.y
    start_t, wait_t = table_loader(t_own, t_peer, tbuf, s_t, y)

    def store_u(g):
        return pltpu.make_async_copy(ubuf.at[g], u_hbm.at[g], s_u.at[g])

    @pl.loop(0, GROUPS)
    def _(g):
        start_t(g)

    friends = [p.sibling, p.xn, p.yn]
    if with_grads:
        above = [{"dp": (p.z + r) % 4} for r in range(1, 4)]
        partner = [{"h": 3 - p.h}, {"h": 3 - p.h, "w": 1 - y}]
        friends = friends + above + partner
    p.greet(friends)

    def own_to(i, sems, to):
        lo, _, hi = chunk(i, 4)
        src = own_ref if i < COUNT - 1 else ball.at[x, c, y]
        return send(src.at[rows(lo, hi)], ball.at[x, c, y, rows(lo, hi)], sems, i, to)

    def own_x(i):
        return own_to(i, s_x, p.xn)

    def own_y(i):
        return own_to(i, s_y, p.yn)

    def own_s(i):
        return own_to(i, s_sib, p.sibling)

    def relay(i, a, b, sems, to, lo, hi):
        return send(ball.at[a, c, b, rows(lo, hi)], ball.at[a, c, b, rows(lo, hi)], sems, i, to)

    def diagonal_y(i):
        lo, mid, _ = chunk(i, 4)
        return relay(i, 1 - x, y, s_dy, p.yn, lo, mid)

    def diagonal_x(i):
        _, mid, hi = chunk(i, 4)
        return relay(i, x, 1 - y, s_dx, p.xn, mid, hi)

    def sibling_x(i):
        lo, _, hi = chunk(i, 4)
        return relay(i, 1 - x, y, s_sx, p.sibling, lo, hi)

    def sibling_y(i):
        lo, _, hi = chunk(i, 4)
        return relay(i, x, 1 - y, s_sy, p.sibling, lo, hi)

    def sibling_d(i):
        lo, _, hi = chunk(i, 4)
        return relay(i, 1 - x, 1 - y, s_sd, p.sibling, lo, hi)

    def give(i):
        for copy in (own_x, own_y, own_s):
            copy(i).start()

    def pass_on(i):
        own_x(i).wait_recv()
        diagonal_y(i).start()
        own_y(i).wait_recv()
        diagonal_x(i).start()
        sibling_x(i).start()
        sibling_y(i).start()

    def collect(i):
        diagonal_y(i).wait_recv()
        diagonal_x(i).wait_recv()
        sibling_d(i).start()

    def complete(i):
        for copy in (own_s, sibling_x, sibling_y, sibling_d):
            copy(i).wait_recv()

    def compute(lo, hi, k):
        @pl.loop(0, hi - lo)
        def _(n):
            g = hi - 1 - n
            wait_t(g)
            for m in range(SUB):
                tiles = []
                for n in range(GROUPS - 4 * k):
                    j = 4 * k + n
                    row = (GROUPS - sum_position(j, g)) * BLOCK + SUB * m
                    if n < 4:
                        row = jnp.where(j >= g, row, ROWS)
                    xj, cj, yj = place_of_block(j)
                    tiles.append(ball[xj, cj, yj, pl.ds(pl.multiple_of(row, SUB), SUB), :])
                ubuf[g, m] = dot(tbuf[g, m][:, 4 * SUB * k:], jnp.concatenate(tiles, axis=0))
            store_u(g).start()

    if with_grads:
        quarter = pl.ds(2 * p.z, 2)

        def grads_z(r):
            return send(own_ref.at[GRAD:ROWS], zg.at[r], s_zg, r, above[r])

        def dk_z(r):
            return send(dk_ref.at[:, pl.ds(2 * ((p.z + 1 + r) % 4), 2)], zin.at[r], s_zk, r, above[r])

        stay = jnp.where(p.low, 0, 1)
        kept = jnp.where(p.low, p.pair, GROUPS - 1 - p.pair) % 4
        given = jnp.where(p.low, GROUPS - 1 - p.pair, p.pair) % 4

        def dk_plane(r):
            to = (p.yn, *partner)[r]
            src = kin.at[stay] if r == 0 else kin.at[1 - stay]
            return send(src, spec_ref.at[kept if r == 0 else given, quarter], s_kin, r, to)

        def dk_up(r):
            return send(spec_ref.at[:, quarter], spec_ref.at[:, quarter], s_kz, r, above[r])

        for r in range(3):
            grads_z(r).start()
            dk_z(r).start()

    give(0)
    give(1)
    ball[x, c, y, 0:ROWS] = own_ref[...]
    for d in range(PLANE):
        ball[d // 4, d // 2 % 2, d % 2, ROWS:] = jnp.zeros((SPARE, LANES), F32)
    for i in range(COUNT + 2):
        if i < COUNT:
            pass_on(i)
        if with_grads and i == 1:
            for r in range(3):
                grads_z(r).wait_recv()
                ball[x, c, y, GRAD:ROWS] += zg[r]
        if with_grads and i == 2:
            for r in range(3):
                dk_z(r).wait_recv()
            kin[...] = dk_ref[:, quarter] + zin[0] + zin[1] + zin[2]
            for r in range(3):
                dk_plane(r).start()
            spec_ref[kept, quarter] = kin[stay]
        if with_grads and i == 3:
            for r in range(3):
                dk_plane(r).wait_recv()
            for r in range(3):
                dk_up(r).start()
        if i < COUNT - 2:
            give(i + 2)
        if 0 < i < COUNT + 1:
            collect(i - 1)
        if i > 1:
            complete(i - 2)
            for step in reversed(quarters(*GATHER_STEPS[i - 2])):
                compute(*step)
    for d in range(PLANE):
        ext_ref[d] = ball[d // 4, d // 2 % 2, d % 2, STAT:ROWS]
    for i in range(COUNT):
        for copy in (own_x, own_y, own_s, diagonal_x, diagonal_y, sibling_x, sibling_y, sibling_d):
            copy(i).wait_send()
    if with_grads:
        for r in range(3):
            grads_z(r).wait_send()
            dk_z(r).wait_send()
            dk_plane(r).wait_send()
            dk_up(r).wait()

    @pl.loop(0, GROUPS)
    def _(g):
        store_u(g).wait()


def synth(table, own, cid, dk=None):
    with_grads = dk is not None
    quarter = vmem(2, 2, CH, LN)
    outs = call(
        lambda *refs: synth_kernel(with_grads, *refs),
        [(GROUPS, SUB, NT, LANES), (PLANE, 2 * SUB, LANES)] + [(4, SUB, CH, LN)] * with_grads,
        [
            vmem(GROUPS, SUB, NT, NL), vmem(GROUPS, SUB, NT, LANES), vmem(2, 2, 2, ROWS + SPARE, LANES),
            dma_sems(GROUPS), dma_sems(GROUPS),
        ] + [dma_sems(2, COUNT)] * 8
        + [vmem(3, 2, 2, CH, LN), quarter, vmem(3, SUB, LANES)] * with_grads
        + [dma_sems(2, 3)] * 4 * with_grads,
        cid=cid,
        in_specs=[ANY, ANY, VMEM] + [VMEM] * with_grads,
        out_specs=(ANY, VMEM) + (VMEM,) * with_grads,
        name=f"synth_{cid}",
    )(*table, own, *([dk] * with_grads))
    return (outs[0].reshape(NM, NT, LANES), *outs[1:])


MIX = PLACES * SUB


def by_degree(v):
    t = jnp.swapaxes(v.reshape(MIX, SUB, LANES), 0, 1)
    return jnp.concatenate([t[:, :, LN * b:LN * (b + 1)] for b in range(NB)], axis=1)


def samples(v):
    return [v[MIX * b:MIX * (b + 1)] for b in range(NB)]


def put_degrees(ref, parts):
    t = jnp.stack([jnp.concatenate(samples(r), axis=1) for r in parts])
    t = jnp.swapaxes(t, 0, 1).reshape(DATA, LANES)
    for n in range(PLACES):
        ref[BLOCK * (GROUPS - n):BLOCK * (PLACES - n)] = t[BLOCK * n:BLOCK * (n + 1)]


def near_mask():
    place = lax.broadcasted_iota(jnp.int32, (NB * MIX, LN), 0) % MIX // SUB
    return (place % 2 == 1) & (place < 2 * (Place().pair + 1))


def mix_kernel(a_ref, kern_ref, b_ref):
    a = by_degree(a_ref[:DATA])
    near = near_mask()
    put_degrees(b_ref, [jnp.where(near, dot(a[l], kern_ref[l]), dot(a[l], kern_ref[SUB + l])) for l in range(SUB)])
    b_ref[DATA:] = jnp.zeros((ROWS - DATA, LANES), F32)


def mix(a, kern):
    return call(mix_kernel, [(ROWS, LANES)], in_specs=[VMEM, VMEM], out_specs=(VMEM,), name="mix")(a, kern)[0]


def mixb_kernel(a_ref, db_ref, kern_ref, c0_ref, da_ref, dk_ref):
    a = by_degree(a_ref[:DATA])
    db = by_degree(db_ref[:DATA])
    near = near_mask()
    parts = []
    total = jnp.zeros((NB * MIX, LN), F32)
    s0 = jnp.zeros((1, LANES), F32)
    for l in range(SUB):
        da = jnp.where(near, dot(db[l], kern_ref[l], NT_DIMS), dot(db[l], kern_ref[SUB + l], NT_DIMS))
        parts.append(da)
        total = total + da * a[l]
        near_row, far_row = (jnp.concatenate([v[n:n + 1] for v in samples(da)], axis=1) for n in (SUB, 0))
        s0 = s0 + near_row * c0_ref[l:l + 1, :1] + far_row * c0_ref[SUB + l:SUB + l + 1, :1]
        for i, part in enumerate((jnp.where(near, a[l], 0.0), jnp.where(near, 0.0, a[l]))):
            g = dot(part, db[l], TN_DIMS)
            low = g[CH:]
            dk_ref[i, l] = g[:CH] + jnp.concatenate([low[:, CH:], -low[:, :CH]], axis=1)
    put_degrees(da_ref, parts)
    s1 = jnp.concatenate([jnp.sum(v, axis=0, keepdims=True) for v in samples(total)], axis=1)
    da_ref[STAT:GRAD] = jnp.concatenate([s0, s1, jnp.zeros((SUB - 2, LANES), F32)], axis=0)
    da_ref[GRAD:] = db_ref[STAT:GRAD]


def mixb(a, db, kern, c0):
    outs = [(ROWS, LANES), (2, SUB, CH, LN)]
    return call(mixb_kernel, outs, in_specs=[VMEM] * len("adkc"), out_specs=(VMEM, VMEM), name="mixb")(a, db, kern, c0)


GRID_SPEC = pl.BlockSpec((1, CH, SUB, NN), lambda b, t: (b, 0, t, 0))
LINES_SPEC = pl.BlockSpec((1, SUB, CH, NN), lambda b, t: (b, t, 0, 0))
CHAN_SPEC = pl.BlockSpec((CH, LN), lambda b, t: (b, 0))
ORDER_SPEC = pl.BlockSpec((NM, SUB, LN), lambda b, t: (0, t, b))
WIDE = SUB * NN


def whole(*shape):
    return pl.BlockSpec(shape, lambda b, t: (0,) * len(shape))


def first_step():
    return (pl.program_id(0) == 0) & (pl.program_id(1) == 0)


def mlp_kernel(u_ref, x_ref, tgt_ref, q_ref, base_ref, w1_ref, w2t_ref, dout_ref, dz_ref, grads_ref,
               gt_ref, g_ref, line_ref, yb_ref, h_ref, act_ref, db_ref, dh_ref):
    @pl.when(first_step())
    def _():
        grads_ref[...] = jnp.zeros_like(grads_ref)
        gt_ref[...] = signed(base_ref[...], Place().y, 2)
        g_ref[...] = gt_ref[...].T

    y = to_grid(u_ref[...], g_ref[...]).reshape(SUB, CH, NN)
    r0 = jnp.swapaxes(x_ref[0] - tgt_ref[0], 0, 1)

    def wide(v):
        return jnp.concatenate([v[t] for t in range(SUB)], axis=1)

    line_ref[...] = wide(r0 + y)
    yb_ref[...] = wide(y).astype(BF16)
    h_ref[...] = mxu(w1_ref[...], yb_ref[...], TN_DIMS)
    for t in range(SUB):
        cols = slice(NN * t, NN * (t + 1))
        h = h_ref[:, cols]
        h2 = h * h
        th = jnp.tanh(h * (GELU_A + (GELU_A * GELU_B) * h2))
        cdf = 0.5 + 0.5 * th
        act_ref[:, cols] = (h * cdf).astype(BF16)
        h_ref[:, cols] = cdf + (0.5 * h) * (1.0 - th * th) * (GELU_A + (3.0 * GELU_A * GELU_B) * h2)
    res = line_ref[...] + mxu(w2t_ref[...], act_ref[...])
    first = pl.program_id(1) * SUB
    qw = jnp.concatenate([jnp.full((1, NN), q_ref[first + t], F32) for t in range(SUB)], axis=1)
    d = qw * res
    line_ref[...] = d
    db_ref[...] = d.astype(BF16)
    loss = jnp.sum((d * res).reshape(SUB, SUB, WIDE), axis=0)
    grads_ref[0:SUB, 2 * LN:] += sum(loss[:, LN * i:LN * (i + 1)] for i in range(WIDE // LN))
    for t in range(SUB):
        dout_ref[0, t] = line_ref[:, NN * t:NN * (t + 1)]
    dh_ref[...] = (mxu(w2t_ref[...], db_ref[...], TN_DIMS) * h_ref[...]).astype(BF16)
    grads_ref[:, :LN] += mxu(yb_ref[...], dh_ref[...], NT_DIMS)
    grads_ref[:, LN:2 * LN] += mxu(db_ref[...], act_ref[...], NT_DIMS)
    dy = line_ref[...] + mxu(w1_ref[...], dh_ref[...])
    dys = jnp.concatenate([dy[:, NN * t:NN * (t + 1)] for t in range(SUB)], axis=0)
    dz_ref[...] = to_orders(dys, gt_ref[...])


def mlp(u, x, target, q, base, w1, w2t):
    hid = 2 * CH
    return call(
        mlp_kernel,
        [(NB, NT, CH, NN), (NM, NT, LANES), (CH, LANES)],
        [
            vmem(NN, NN), vmem(NN, NN), vmem(CH, WIDE), vmem(CH, WIDE, dtype=BF16), vmem(hid, WIDE),
            vmem(hid, WIDE, dtype=BF16), vmem(CH, WIDE, dtype=BF16), vmem(hid, WIDE, dtype=BF16),
        ],
        grid=(NB, T8),
        in_specs=[
            ORDER_SPEC, GRID_SPEC, GRID_SPEC, SMEM, whole(NN, NN), whole(CH, hid), whole(CH, hid),
        ],
        out_specs=(LINES_SPEC, ORDER_SPEC, whole(CH, LANES)),
        name="mlp",
    )(u, x, target, q, base, w1, w2t)


def final_kernel(u_ref, x_ref, dout_ref, mu_ref, inv_ref, ext_ref, spec_ref, base_ref, out_ref, gspec_ref, gw1_ref, gw2t_ref, loss_ref,
                 g_ref, s0_ref, s1_ref):
    @pl.when(first_step())
    def _():
        g_ref[...] = signed(base_ref[...], Place().y, 1).T
        gspec_ref[0] = spec_ref[:, :, :CH]
        gspec_ref[1] = spec_ref[:, :, CH:]
        grads = ext_ref[:, SUB:].reshape(CH, LANES)
        gw1_ref[...] = grads[:, :LN]
        gw2t_ref[...] = grads[:, LN:2 * LN]
        loss = jnp.sum(jnp.sum(grads[:SUB, 2 * LN:], axis=0, keepdims=True), axis=1, keepdims=True) / TOTAL
        loss_ref[...] = jnp.broadcast_to(loss, (SUB, LN))
        sums = sum(ext_ref[n, :SUB] for n in range(PLANE)) / POINTS
        for b in range(NB):
            chans, lanes = slice(CH * b, CH * (b + 1)), slice(LN * b, LN * (b + 1))
            s0, s1 = (jnp.broadcast_to(sums[n:n + 1, lanes], (LN, LN)).T for n in range(2))
            s0_ref[chans] = s0[:CH]
            s1_ref[chans] = s1[:CH] + s1[CH:]

    dn = to_grid(u_ref[...], g_ref[...]).reshape(SUB, CH, NN)
    xt = jnp.swapaxes(x_ref[0], 0, 1)
    chans = pl.ds(pl.multiple_of(pl.program_id(0) * CH, CH), CH)
    inv = inv_ref[:, :1]
    normed = (xt - mu_ref[:, :1]) * inv
    r = dout_ref[0] + inv * (dn - s0_ref[chans, :1] - normed * s1_ref[chans, :1])
    out_ref[0] = jnp.swapaxes(r, 0, 1)


def final(u, x, dout, mu, inv, ext, spec, base):
    hid = 2 * CH
    degrees = NL // 4
    return call(
        final_kernel,
        [(NB, CH, NT, NN), (2, degrees, CH, CH), (CH, hid), (CH, hid), (SUB, LN)],
        [vmem(NN, NN), vmem(NB * CH, LN), vmem(NB * CH, LN)],
        grid=(NB, T8),
        in_specs=[
            ORDER_SPEC, GRID_SPEC, LINES_SPEC, CHAN_SPEC, CHAN_SPEC,
            whole(PLANE, 2 * SUB, LANES), whole(degrees, CH, LN), whole(NN, NN),
        ],
        out_specs=(GRID_SPEC, whole(2, degrees, CH, CH), whole(CH, hid), whole(CH, hid), whole(SUB, LN)),
        name="final",
    )(u, x, dout, mu, inv, ext, spec.reshape(degrees, CH, LN), base)


def solution(mesh):
    def local_step(x, target, q, leg_fwd, leg_inv, spec_w, w1, w2):
        base = jnp.asarray(dft_matrix())
        p_own, q_own = (jnp.swapaxes(v, 1, 2).reshape(HALF_TABLE) for v in (leg_fwd, leg_inv))
        z, p_peer, mu, inv, c0, kern = front(x, p_own, jnp.moveaxis(spec_w, 1, 3), base, 0)
        a, q_peer = analyze((p_own, p_peer), z, jnp.zeros((CH, LANES), F32), 1, q_own)
        b = mix(a, kern)
        u, _ = synth((q_own, q_peer), b, 2)
        dout, dz, grads = mlp(u, x, target, q, base, w1, w2.T)
        db = analyze((q_own, q_peer), dz, grads, 3)
        da, dk = mixb(a, db, kern, c0)
        du, ext, spec = synth((p_own, p_peer), da, 4, dk)
        d_field, grad_spec, gw1, gw2t, loss = final(du, x, dout, mu, inv, ext, spec, base)
        return loss[0, 0], d_field, grad_spec, gw1, gw2t.T

    grid_spec = P("dp", None, "h", "w")
    table_spec = P("w", None, "h")
    return jax.shard_map(
        local_step,
        mesh=mesh,
        in_specs=(grid_spec, grid_spec, P("h"), table_spec, table_spec, P(), P(), P()),
        out_specs=(P(), grid_spec, P(None, "h", None, None), P(), P()),
        check_vma=False,
    )
```

time: 4240 us -> 512 us (0.12)
  the two profiles are of different devices: /device:TPU:1 before, /device:TPU:0 now
where the time goes in v1:
time: 512 us; the launch traced here: 503 us
  Pallas kernels  500 us (98%)
    pallas_call x2, Pallas kernels, analyze(): call(lambda *refs: analyze_kernel(share, with_q, *refs), [(ROWS, LANES)]...  161 us
    pallas_call x2, Pallas kernels, synth(): call(lambda *refs: synth_kernel(with_grads, *refs), [(GROUPS, SUB, NT, LA...  139 us
    pallas_call x1, Pallas kernels, front(): call(front_kernel, [(NM, NT, LANES), HALF_TABLE, (NB * CH, LN), (NB * CH,...  74.9 us
    pallas_call x1, Pallas kernels, mlp(): call(mlp_kernel, [(NB, NT, CH, NN), (NM, NT, LANES), (CH, LANES)], [vmem(...  70.9 us
    pallas_call x1, Pallas kernels, final(): call(final_kernel, [(NB, CH, NT, NN), (2, degrees, CH, CH), (CH, hid), (C...  33 us
    pallas_call x1, Pallas kernels, mixb(): call(mixb_kernel, outs, in_specs=[VMEM] * len('adkc'), out_specs=(VMEM, V...  13.2 us

profile of v1, /device:TPU:0, one launch (start us, length us, event | category | flops | bytes accessed | tf_op | source)
XLA Modules:
  0.0 503.0 jit_solution(13811037090280578443)
XLA Ops:
  0.6 74.9 %front.1 = (f32[128,64,384]{2,1,0:T(8,128)}, f32[8,8,64,128]{3,2,1,0:T(8,128)}, f32[192,128]{1,0:T(8,128)}, f32[192,128]{1,0:T(8,128)}, f32[16,128]{1,0:T(8,128)}, /*index=5*/f32[16,128,128]{2,1,0:T(8,128)}) custom-call(f32[3,64,64,256]{3,2,1,0:T(8,128)} %x_ref.3, f32[8,8,64,128]{3,2,1,0:T(8,128)} %bitcast.18, f32[2,64,64,128]{3,2,1,0:T(8,128)} %bitcast.25, ...), custom_call_target="tpu_custom_call" | custom-call | tf_op jit(solution)/shard_map/front/pallas_call | solution.py:263
  75.5 0.6 broadcast_in_dim.3.refs_3_
  76.2 93.6 %analyze_1.1 = (f32[1104,384]{1,0:T(8,128)}, f32[8,8,64,128]{3,2,1,0:T(8,128)}) custom-call(f32[8,8,64,128]{3,2,1,0:T(8,128)} %bitcast.19, f32[8,8,64,128]{3,2,1,0:T(8,128)} %get-tuple-element.27.refs_1_, f32[16,8,64,384]{3,2,1,0:T(8,128)} %bitcast.21, f32[64,384]{1,0:T(8,128)} %broadcast_in_dim.3.refs_3_, f32[8,8,64,128]{3,2,1,0:T(8,128)} %bitcast.15), custom_call_target="tpu_custom_call" | custom-call | tf_op jit(solution)/shard_map/analyze_1/pallas_call | solution.py:419
  169.8 8.5 %mix.1.refs_2_ = f32[1104,384]{1,0:T(8,128)} custom-call(f32[1104,384]{1,0:T(8,128)} %get-tuple-element.29.a_ref, f32[16,128,128]{2,1,0:T(8,128)} %get-tuple-element.31.kern_ref), custom_call_target="tpu_custom_call" | custom-call | tf_op jit(solution)/shard_map/mix/pallas_call | solution.py:661
  178.3 67.0 %synth_2.1 = (f32[16,8,64,384]{3,2,1,0:T(8,128)}, f32[8,16,384]{2,1,0:T(8,128)}) custom-call(f32[8,8,64,128]{3,2,1,0:T(8,128)} %bitcast.16, f32[8,8,64,128]{3,2,1,0:T(8,128)} %get-tuple-element.30.refs_1_, f32[1104,384]{1,0:T(8,128)} %mix.1.refs_2_), custom_call_target="tpu_custom_call" | custom-call | tf_op jit(solution)/shard_map/synth_2/pallas_call | solution.py:612
  245.2 70.9 %mlp.1 = (f32[3,64,64,256]{3,2,1,0:T(8,128)}, f32[128,64,384]{2,1,0:T(8,128)}, f32[64,384]{1,0:T(8,128)}) custom-call(f32[128,64,384]{2,1,0:T(8,128)} %bitcast.24, f32[3,64,64,256]{3,2,1,0:T(8,128)} %x_ref.3, f32[3,64,64,256]{3,2,1,0:T(8,128)} %tgt_ref.1, f32[64]{0:T(128)} %q_ref.1, f32[256,256]{1,0:T(8,128)} %constant.4.clone.base_ref, ...), custom_call_target="tpu_custom_call" | custom-call | tf_op jit(solution)/shard_map/mlp/pallas_call | solution.py:752
  316.1 67.1 %analyze_3.1.db_ref = f32[1104,384]{1,0:T(8,128)} custom-call(f32[8,8,64,128]{3,2,1,0:T(8,128)} %bitcast.17, f32[8,8,64,128]{3,2,1,0:T(8,128)} %get-tuple-element.30.refs_1_, f32[16,8,64,384]{3,2,1,0:T(8,128)} %bitcast.22, f32[64,384]{1,0:T(8,128)} %get-tuple-element.34.refs_3_), custom_call_target="tpu_custom_call" | custom-call | tf_op jit(solution)/shard_map/analyze_3/pallas_call | solution.py:419
  383.2 13.2 %mixb.1 = (f32[1104,384]{1,0:T(8,128)}, f32[2,8,64,128]{3,2,1,0:T(8,128)}) custom-call(f32[1104,384]{1,0:T(8,128)} %get-tuple-element.29.a_ref, f32[1104,384]{1,0:T(8,128)} %analyze_3.1.db_ref, f32[16,128,128]{2,1,0:T(8,128)} %get-tuple-element.31.kern_ref, f32[16,128]{1,0:T(8,128)} %get-tuple-element.35.c0_ref), custom_call_target="tpu_custom_call" | custom-call | tf_op jit(solution)/shard_map/mixb/pallas_call | solution.py:689
  396.4 71.9 %synth_4.1 = (f32[16,8,64,384]{3,2,1,0:T(8,128)}, f32[8,16,384]{2,1,0:T(8,128)}, f32[4,8,64,128]{3,2,1,0:T(8,128)}) custom-call(f32[8,8,64,128]{3,2,1,0:T(8,128)} %bitcast.20, f32[8,8,64,128]{3,2,1,0:T(8,128)} %get-tuple-element.27.refs_1_, f32[1104,384]{1,0:T(8,128)} %get-tuple-element.36.refs_2_, f32[2,8,64,128]{3,2,1,0:T(8,128)} %get-tuple-element.37.refs_3_), custom_call_target="tpu_custom_call" | custom-call | tf_op jit(solution)/shard_map/synth_4/pallas_call | solution.py:612
  468.3 33.0 %final.1 = (f32[3,64,64,256]{3,2,1,0:T(8,128)}, f32[2,32,64,64]{3,2,1,0:T(8,128)}, f32[64,128]{1,0:T(8,128)}, f32[64,128]{1,0:T(8,128)}, f32[8,128]{1,0:T(8,128)}) custom-call(f32[128,64,384]{2,1,0:T(8,128)} %bitcast.23, f32[3,64,64,256]{3,2,1,0:T(8,128)} %x_ref.3, f32[3,64,64,256]{3,2,1,0:T(8,128)} %get-tuple-element.39.dout_ref, ...), custom_call_target="tpu_custom_call" | custom-call | tf_op jit(solution)/shard_map/final/pallas_call | solution.py:799
  501.3 1.2 slice.3

commit v2 on v1

v2 whole, which is shorter than its diff:
```python
import math
import numpy as np
import jax
import jax.numpy as jnp
from jax import lax
from jax.experimental import pallas as pl
from jax.experimental.pallas import tpu as pltpu
from jax.sharding import PartitionSpec as P

NORM_EPS = 1e-5
HI = lax.Precision.HIGHEST
F32 = jnp.float32
BF16 = jnp.bfloat16
MESH = pl.DeviceIdType.MESH
GELU_A = math.sqrt(2.0 / math.pi)
GELU_B = 0.044715

NB, CH, NT, NN = 3, 64, 64, 256
NM, NL = 128, 128
LON, LAT, BATCH = 512, 256, 12
POINTS = LON * LAT
TOTAL = POINTS * BATCH * CH
LANES = NB * 2 * CH
SUB, LN = 8, 128
T8 = NT // SUB
GROUPS = NM // SUB
PLANE = 8
H_OF_PAIR = (0, 0, 3, 3, 1, 1, 2, 2)
BLOCK = SUB * SUB
PLACES = GROUPS + 1
DATA = PLACES * BLOCK
STAT = DATA
GRAD = DATA + SUB
ROWS = GRAD + SUB
SPARE = BLOCK
SLOTS = (2, 2, 2)
COUNT = 6
AT_ONCE = 4
UNROLL = 2
LATE = SUB // 2
NN_DIMS, NT_DIMS, TN_DIMS = ((1,), (0,)), ((1,), (1,)), ((0,), (0,))
SUM_ENDS = (2, 5, 8, 11, 14, 16, 17)
GATHER_ENDS = (3, 6, 9, 12, 15, 17)
MIX_AFTER = (2, 3, 4, 6)

SMEM = pl.BlockSpec(memory_space=pltpu.SMEM)
VMEM = pl.BlockSpec(memory_space=pltpu.VMEM)
ANY = pl.BlockSpec(memory_space=pl.ANY)


def dot(a, b, dims=NN_DIMS):
    return lax.dot_general(a, b, (dims, ((), ())), precision=HI, preferred_element_type=F32)


def mxu(a, b, dims=NN_DIMS):
    return lax.dot_general(a, b, (dims, ((), ())), preferred_element_type=F32)


def call(kernel, outs, scratch=(), cid=None, **kw):
    extra = {} if cid is None else {"collective_id": cid, "has_side_effects": True}
    return pl.pallas_call(
        kernel,
        out_shape=tuple(jax.ShapeDtypeStruct(s, F32) for s in outs),
        scratch_shapes=list(scratch),
        compiler_params=pltpu.CompilerParams(vmem_limit_bytes=62 << 20, **extra),
        **kw,
    )


def vmem(*shape, dtype=F32):
    return pltpu.VMEM(shape, dtype)


def dma_sems(*shape):
    return pltpu.SemaphoreType.DMA(shape)


def rows(lo, hi):
    return pl.ds(lo, hi - lo)


def dft_matrix():
    theta = 2.0 * np.pi * ((np.arange(NN)[:, None] * np.arange(NM)[None, :]) % LON) / LON
    return (np.concatenate([np.cos(theta), -np.sin(theta)], axis=1) / math.sqrt(LON)).astype(np.float32)


def signed(base, half, weight):
    m = lax.broadcasted_iota(jnp.int32, base.shape, 1) % NM
    out = jnp.where((m % 2) * half == 1, -base, base)
    return jnp.where(m == 0, out, weight * out) if weight > 1 else out


def to_orders(lines, ft):
    z = dot(lines, ft).reshape(SUB, CH, NN)
    z = jnp.concatenate([z[:, :, :NM], z[:, :, NM:]], axis=1)
    return jnp.swapaxes(z, 1, 2)


def to_grid(orders, ft):
    u = jnp.swapaxes(orders, 1, 2)
    u = jnp.concatenate([u[:, :CH, :], u[:, CH:, :]], axis=2).reshape(SUB * CH, NN)
    return dot(u, ft)


def place_of_block(j):
    k = min(j, GROUPS - 1 - j)
    return H_OF_PAIR[k] // 2, H_OF_PAIR[k] % 2, k % 2


def slot_index(d):
    return d // 4, d // 2 % 2, d % 2


def sum_position(j, g):
    k = min(j, GROUPS - 1 - j)
    return 2 * g + 1 if j < SUB else jnp.where(g <= k, 2 * g, k + 1 + g)


def start_of(i, ends):
    return ends[i - 1] if i > 0 else 0


def chunk(i, share, ends):
    lo = start_of(i, ends) * BLOCK
    hi = ends[i] * BLOCK if ends[i] < PLACES else ROWS
    return lo, lo + (hi - lo) * share // BLOCK * SUB, hi


class Place:
    def __init__(self):
        self.h, self.y, self.z = lax.axis_index("h"), lax.axis_index("w"), lax.axis_index("dp")
        self.x, self.c = self.h // 2, self.h % 2
        self.slot = 2 * self.h + self.y
        self.low = self.h < 2
        self.pair = jnp.where(self.low, 4 * self.h, 14 - 4 * self.h) + self.y
        self.sibling = {"h": 2 * self.x + 1 - self.c}
        self.xn = {"h": 2 * (1 - self.x) + self.c}
        self.yn = {"w": 1 - self.y}

    def plane(self, r):
        s = (self.slot + r) % PLANE
        return {"h": s // 2, "w": s % 2}

    def greet(self, others):
        barrier = pltpu.get_barrier_semaphore()
        for other in others:
            pl.semaphore_signal(barrier, inc=1, device_id=other, device_id_type=MESH)
        pl.semaphore_wait(barrier, len(others))


def send(src, dst, sems, i, to):
    return pltpu.make_async_remote_copy(
        src_ref=src, dst_ref=dst, send_sem=sems.at[0, i], recv_sem=sems.at[1, i], device_id=to, device_id_type=MESH
    )


CB = 16
PIECES = CH // CB
HALF_TABLE = (SUB, SUB, NT, NL)


def near_far(k):
    return pl.ds(pl.multiple_of(SUB * k, SUB), SUB), pl.ds(pl.multiple_of(SUB * (GROUPS - 1 - k), SUB), SUB)


def front_kernel(x_hbm, p_hbm, w_hbm, base_ref, z_hbm, p_peer, mu_ref, inv_ref, c0_ref, kern_ref,
                 xbuf, wbuf, pbuf, cols, pay, sbuf, zbuf, ftbuf, turned, own, s_x, s_w, s_z, s_p, s_st):
    place = Place()
    near, far = near_far(place.pair)

    def load_x(n):
        b, part = n // PIECES, pl.ds(n % PIECES * CB, CB)
        return pltpu.make_async_copy(x_hbm.at[b, part], xbuf.at[b, part], s_x.at[n])

    def load_w(i):
        return pltpu.make_async_copy(w_hbm.at[i], wbuf.at[i], s_w.at[i])

    def load_p(g):
        return pltpu.make_async_copy(p_hbm.at[g], pbuf.at[g], s_p.at[2, g])

    def give_p(g):
        return send(pbuf.at[g], p_peer.at[g], s_p, g, place.yn)

    @pl.loop(0, SUB)
    def _(g):
        load_p(g).start()

    @pl.loop(0, NB * PIECES)
    def _(n):
        load_x(n).start()

    for i in range(2):
        load_w(i).start()
    others = range(1, PLANE)
    place.greet([place.plane(r) for r in others])

    def offer(lo, hi):
        @pl.loop(lo, hi)
        def _(g):
            load_p(g).wait()
            give_p(g).start()

    offer(0, 1)
    cols[...] = jnp.zeros_like(cols)

    @pl.loop(0, NB * PIECES)
    def _(n):
        load_x(n).wait()
        v = xbuf[n // PIECES, pl.ds(n % PIECES * CB, CB)]
        mean = jnp.sum(jnp.sum(v, axis=1, keepdims=True), axis=2, keepdims=True) / (NT * NN)
        diff = v - mean
        m2 = jnp.sum(jnp.sum(diff * diff, axis=1, keepdims=True), axis=2, keepdims=True)
        lane = lax.broadcasted_iota(jnp.int32, (CB, 1, LN), 2)
        cols[pl.ds(pl.multiple_of(n * CB, CB), CB)] = jnp.where(lane < CH, mean, m2).reshape(CB, LN)
    wide = cols[...].T
    p1 = jnp.where(place.y == 0, jnp.sum(pbuf[0, 0], axis=0, keepdims=True), 0.0)
    pay[...] = jnp.concatenate([
        *(wide[n:n + 1] for n in (0, CH)), jnp.concatenate([p1, p1], axis=1), jnp.zeros((SUB - 3, NN), F32)
    ], axis=0)

    def give_stats(r):
        return send(pay, sbuf.at[place.slot], s_st, r, place.plane(r))

    for r in others:
        give_stats(r).start()
    offer(1, SUB)
    sbuf[place.slot] = pay[...]
    ftbuf[...] = signed(base_ref[...], place.y, 1)

    for i in range(2):
        load_w(i).wait()

    @pl.loop(0, CH)
    def _(i):
        turned[...] = jnp.concatenate([wbuf[n, i] for n in range(2)], axis=0).T
        own[i, :SUB] = turned[near]
        own[i, SUB:] = turned[far]

    top = jnp.swapaxes(own[...], 0, 1)
    kern_ref[:, :CH] = top
    kern_ref[:, CH:] = jnp.concatenate([-top[:, :, CH:], top[:, :, :CH]], axis=2)

    for r in others:
        give_stats(r).wait_recv()
    means, m2s, p1s = (jnp.concatenate([sbuf[s, n:n + 1] for s in range(PLANE)], axis=0) for n in range(3))
    mu = jnp.sum(means, axis=0, keepdims=True) / PLANE
    dev = means - mu
    var = (jnp.sum(m2s, axis=0, keepdims=True) + (NT * NN) * jnp.sum(dev * dev, axis=0, keepdims=True)) / POINTS
    c0 = math.sqrt(LON) * jnp.sum(p1s, axis=0, keepdims=True)
    mu_ref[...], inv_ref[...], turned[...] = (
        jnp.broadcast_to(v, (LN, NN)).T[:n] for v, n in ((mu, NB * CH), (lax.rsqrt(var + NORM_EPS), NB * CH), (c0, NL))
    )
    c0_ref[:SUB] = turned[near]
    c0_ref[SUB:] = turned[far]

    def store_z(n):
        t = pl.multiple_of(n % T8 * SUB, SUB)
        lanes = pl.multiple_of(n // T8 * LN, LN)
        return pltpu.make_async_copy(zbuf.at[n % 2], z_hbm.at[pl.ds(t, SUB), :, pl.ds(lanes, LN)], s_z.at[n % 2])

    @pl.loop(0, NB * T8)
    def _(n):
        @pl.when(n >= 2)
        def _():
            store_z(n - 2).wait()

        b = n // T8
        xt = jnp.swapaxes(xbuf[b, :, pl.ds(pl.multiple_of(n % T8 * SUB, SUB), SUB), :], 0, 1)
        chans = pl.ds(pl.multiple_of(b * CH, CH), CH)
        xn = (xt - mu_ref[chans, :1]) * inv_ref[chans, :1]
        zbuf[n % 2] = to_orders(xn.reshape(SUB * CH, NN), ftbuf[...])
        store_z(n).start()

    for n in range(2):
        store_z(NB * T8 - 2 + n).wait()
    for r in others:
        give_stats(r).wait_send()

    @pl.loop(0, SUB)
    def _(g):
        give_p(g).wait()


def front(x, p_own, spec_w, base, cid):
    return call(
        front_kernel,
        [(NT, NM, LANES), HALF_TABLE, (NB * CH, LN), (NB * CH, LN), (2 * SUB, LN), (2 * SUB, LN, LN)],
        [
            vmem(NB, CH, NT, NN), vmem(2, CH, CH, NL), vmem(*HALF_TABLE), vmem(NN, LN), vmem(SUB, NN), vmem(PLANE, SUB, NN),
            vmem(2, SUB, NM, LN), vmem(NN, NN), vmem(NL, LN), vmem(CH, 2 * SUB, LN),
            dma_sems(NB * PIECES), dma_sems(2), dma_sems(2), dma_sems(3, SUB), dma_sems(2, PLANE),
        ],
        cid=cid,
        in_specs=[ANY, ANY, ANY, VMEM],
        out_specs=(ANY, ANY, VMEM, VMEM, VMEM, VMEM),
        name="front",
    )(x, p_own, spec_w, base)


def table_loader(own, peers, tbuf, sems, y):
    def copy(src, at, g):
        return pltpu.make_async_copy(src.at[at], tbuf.at[g], sems.at[g])

    def start(g):
        at = g % SUB
        away = g // SUB != y

        @pl.when(g // SUB == y)
        def _():
            copy(own, at, g).start()

        first = 0
        for src, count in peers:
            if src is not None:
                @pl.when(away & (at >= first) & (at < first + count))
                def _(src=src, first=first):
                    copy(src, at - first, g).start()
            first += count

    def wait(g):
        copy(own, 0, g).wait()

    return start, wait


def quarters(lo, hi):
    return [(max(lo, 4 * k), min(hi, 4 * k + 4), k) for k in range(4) if max(lo, 4 * k) < min(hi, 4 * k + 4)]


def by_degree(ref, v):
    n = v.shape[0] // SUB
    t = jnp.swapaxes(v.reshape(n, SUB, LANES), 0, 1)
    for b in range(NB):
        ref[:, n * b:n * (b + 1)] = t[:, :, LN * b:LN * (b + 1)]


def put_degrees(ref, parts, first, count):
    n = count * SUB
    t = jnp.concatenate([parts[:, n * b:n * (b + 1)] for b in range(NB)], axis=2)
    t = jnp.swapaxes(t, 0, 1)
    for i in range(count):
        to = BLOCK * (GROUPS - first - i)
        ref[to:to + BLOCK] = t[SUB * i:SUB * (i + 1)].reshape(BLOCK, LANES)


def near_mask(first, count, pair):
    place = first + lax.broadcasted_iota(jnp.int32, (NB * count * SUB, LN), 0) % (count * SUB) // SUB
    return (place % 2 == 1) & (place < 2 * (pair + 1))


def mix_places(first, count, pair, a_ref, kern_ref, b_ref, a, b):
    rows_in = a_ref[BLOCK * first:BLOCK * (first + count)]
    n = NB * count * SUB
    by_degree(a, rows_in)
    near = near_mask(first, count, pair)

    @pl.loop(0, SUB, unroll=UNROLL)
    def _(l):
        al = a[l, :n]
        b[l, :n] = jnp.where(near, dot(al, kern_ref[l]), dot(al, kern_ref[SUB + l]))

    put_degrees(b_ref, b, first, count)


def mix_back_places(first, count, pair, a_ref, db_ref, kern_ref, c0_ref, da_ref, dk_ref, s_ref, a, db, da):
    at = slice(BLOCK * first, BLOCK * (first + count))
    n = count * SUB
    by_degree(a, a_ref[at])
    by_degree(db, db_ref[at])
    near = near_mask(first, count, pair)

    @pl.loop(0, SUB, unroll=UNROLL)
    def _(l):
        al, dl = a[l, :NB * n], db[l, :NB * n]
        v = jnp.where(near, dot(dl, kern_ref[l], NT_DIMS), dot(dl, kern_ref[SUB + l], NT_DIMS))
        da[l, :NB * n] = v
        product = v * al
        s_ref[1:2] += jnp.concatenate([jnp.sum(product[n * i:n * (i + 1)], axis=0, keepdims=True) for i in range(NB)], axis=1)
        if first == 0:
            for row, c0 in ((SUB, l), (0, SUB + l)):
                c0 = jnp.concatenate([c0_ref[pl.ds(c0, 1)]] * NB, axis=1)
                s_ref[0:1] += c0 * jnp.concatenate([v[n * i + row:n * i + row + 1] for i in range(NB)], axis=1)
        for i, part in enumerate((jnp.where(near, al, 0.0), jnp.where(near, 0.0, al))):
            g = dot(part, dl, TN_DIMS)
            low = g[CH:]
            dk_ref[i, l] += g[:CH] + jnp.concatenate([low[:, CH:], -low[:, :CH]], axis=1)

    put_degrees(da_ref, da, first, count)


def analyze_kernel(share, with_q, *refs):
    if with_q:
        t_own, t_peer, z_hbm, q_own, kern_ref, out_ref, mix_ref, q_peer, a_deg, b_deg, qbuf, *rest = refs
        peers = [(t_peer, SUB)]
    else:
        t_own, t_low, t_high, z_hbm, ext_ref, kern_ref, a_ref, c0_ref, mix_ref, dk_ref, a_deg, b_deg, out_ref, s_ref, da_deg, *rest = refs
        peers = [(t_low, LATE), (t_high, SUB - LATE)]
        dk_ref[...] = jnp.zeros_like(dk_ref)
        s_ref[...] = jnp.zeros_like(s_ref)
    tbuf, zbuf, turned, part, sib, rx, ry, fx, fy, s_t, s_z, s_q, s_sib, s_x, s_y, s_fx, s_fy = rest
    count = len(SUM_ENDS)
    p = Place()
    x, c, y = p.x, p.c, p.y
    start_t, wait_t = table_loader(t_own, peers, tbuf, s_t, y)

    def load_z(g):
        return pltpu.make_async_copy(z_hbm.at[:, pl.ds(pl.multiple_of(SUB * g, SUB), SUB)], zbuf.at[g], s_z.at[g])

    @pl.loop(0, GROUPS)
    def _(g):
        start_t(g)
        load_z(g).start()

    p.greet([p.sibling, p.xn, p.yn])
    for d in range(PLANE):
        spare = part.at[slot_index(d)]
        spare[STAT:ROWS] = jnp.zeros((ROWS - STAT, LANES), F32)
        if not with_q:
            spare[STAT:GRAD] = ext_ref[SUB * d:SUB * (d + 1)]

    def load_q(g):
        return pltpu.make_async_copy(q_own.at[LATE + g], qbuf.at[g], s_q.at[2, g])

    def give_q(g):
        return send(qbuf.at[g], q_peer.at[g], s_q, g, p.yn)

    def compute(lo, hi, k):
        @pl.loop(lo, hi)
        def _(g):
            wait_t(g)
            load_z(g).wait()
            turned[...] = jnp.swapaxes(zbuf[g], 0, 1)

            at_once = AT_ONCE if k < 2 else 2

            @pl.loop(0, SUB, step=at_once)
            def _(some):
                for m in range(at_once):
                    m = some + m
                    r = dot(tbuf[g, m].T[4 * SUB * k:], turned[m])
                    for n in range(GROUPS - 4 * k):
                        j = 4 * k + n
                        row = sum_position(j, g) * BLOCK + SUB * m
                        if n < 4:
                            row = jnp.where(j >= g, row, ROWS)
                        xj, cj, yj = place_of_block(j)
                        part[xj, cj, yj, pl.ds(pl.multiple_of(row, SUB), SUB), :] = r[SUB * n:SUB * (n + 1)]

    def to_sibling(i):
        lo, _, hi = chunk(i, share, SUM_ENDS)
        return send(part.at[:, 1 - c, :, rows(lo, hi)], sib.at[:, :, rows(lo, hi)], s_sib, i, p.sibling)

    def to_x(i):
        lo, mid, _ = chunk(i, share, SUM_ENDS)
        return send(part.at[1 - x, c, :, rows(lo, mid)], rx.at[:, rows(lo, mid)], s_x, i, p.xn)

    def to_y(i):
        _, mid, hi = chunk(i, share, SUM_ENDS)
        return send(part.at[:, c, 1 - y, rows(mid, hi)], ry.at[:, rows(mid, hi)], s_y, i, p.yn)

    def forward_y(i):
        lo, mid, _ = chunk(i, share, SUM_ENDS)
        return send(part.at[x, c, 1 - y, rows(lo, mid)], fy.at[rows(lo, mid)], s_fy, i, p.yn)

    def forward_x(i):
        _, mid, hi = chunk(i, share, SUM_ENDS)
        return send(part.at[1 - x, c, y, rows(mid, hi)], fx.at[rows(mid, hi)], s_fx, i, p.xn)

    def chip_sum(i):
        lo, _, hi = chunk(i, share, SUM_ENDS)
        to_sibling(i).wait_recv()

        @pl.loop(lo, hi, step=2 * SUB)
        def _(row):
            some = pl.ds(pl.multiple_of(row, SUB), 2 * SUB)
            for a in range(2):
                for b in range(2):
                    part[a, c, b, some] += sib[a, b, some]

        to_x(i).start()
        to_y(i).start()
        if with_q and i < LATE:
            give_q(i).start()

    def half_sum(i):
        lo, mid, hi = chunk(i, share, SUM_ENDS)
        to_x(i).wait_recv()
        part[x, c, 1 - y, rows(lo, mid)] += rx[1 - y, rows(lo, mid)]
        forward_y(i).start()
        to_y(i).wait_recv()
        part[1 - x, c, y, rows(mid, hi)] += ry[1 - x, rows(mid, hi)]
        forward_x(i).start()
        out_ref[rows(lo, mid)] = part[x, c, y, rows(lo, mid)] + rx[y, rows(lo, mid)]
        out_ref[rows(mid, hi)] = part[x, c, y, rows(mid, hi)] + ry[x, rows(mid, hi)]

    def last_sum(i):
        lo, mid, hi = chunk(i, share, SUM_ENDS)
        forward_y(i).wait_recv()
        out_ref[rows(lo, mid)] += fy[rows(lo, mid)]
        forward_x(i).wait_recv()
        out_ref[rows(mid, hi)] += fx[rows(mid, hi)]

    def mixed(first, end):
        places = end - first
        if with_q:
            mix_places(first, places, p.pair, out_ref, kern_ref, mix_ref, a_deg, b_deg)
        else:
            mix_back_places(first, places, p.pair, a_ref, out_ref, kern_ref, c0_ref, mix_ref, dk_ref, s_ref, a_deg, b_deg, da_deg)

    if with_q:
        for g in range(LATE):
            load_q(g).start()
        for g in range(LATE):
            load_q(g).wait()
    for i in range(count + LAST_LAG):
        if i < count:
            for step in quarters(max(start_of(i, SUM_ENDS) - 1, 0), SUM_ENDS[i] - 1):
                compute(*step)
            to_sibling(i).start()
        if 0 < i <= count:
            chip_sum(i - 1)
        if HALF_LAG <= i < count + HALF_LAG:
            half_sum(i - HALF_LAG)
        if i >= LAST_LAG:
            last_sum(i - LAST_LAG)
            if i - LAST_LAG in MIX_AFTER:
                n = MIX_AFTER.index(i - LAST_LAG)
                mixed(SUM_ENDS[MIX_AFTER[n - 1]] if n > 0 else 0, SUM_ENDS[MIX_AFTER[n]])
    if with_q:
        mix_ref[STAT:] = jnp.zeros((ROWS - STAT, LANES), F32)
    else:
        mix_ref[STAT:GRAD] = s_ref[...]
        mix_ref[GRAD:] = out_ref[STAT:GRAD]
    for i in range(count):
        for copy in (to_sibling, to_x, to_y, forward_x, forward_y):
            copy(i).wait_send()
    if with_q:
        for g in range(LATE):
            give_q(g).wait()


HALF_LAG, LAST_LAG = 2, 4
MOST = 8


def analyze(table, z, cid, kern, q_own=None, back=()):
    with_q = q_own is not None
    share = 6 if with_q else 4
    piece = (LATE, *HALF_TABLE[1:])
    half = vmem(ROWS, LANES)
    pair = vmem(2, ROWS, LANES)
    degrees = vmem(SUB, NB * MOST * SUB, LN)
    if with_q:
        ins, places, outs = (q_own, kern), [ANY, VMEM], [(ROWS, LANES), (ROWS, LANES), piece]
        out_places, more = (VMEM, VMEM, ANY), [vmem(*piece)]
    else:
        ext, a, c0 = back
        ins, places, outs = (ext, kern, a, c0), [VMEM] * 4, [(ROWS, LANES), (2, SUB, CH, LN)]
        out_places, more = (VMEM, VMEM), [half, vmem(SUB, LANES), degrees]
    return call(
        lambda *refs: analyze_kernel(share, with_q, *refs),
        outs,
        [degrees, degrees] + more + [
            vmem(GROUPS, SUB, NT, NL), vmem(GROUPS, NT, SUB, LANES), vmem(SUB, NT, LANES), vmem(*SLOTS, ROWS + SPARE, LANES),
            vmem(*SLOTS[1:], ROWS, LANES), pair, pair, half, half,
            dma_sems(GROUPS), dma_sems(GROUPS), dma_sems(3, LATE),
        ] + [dma_sems(2, len(SUM_ENDS))] * 5,
        cid=cid,
        in_specs=[ANY] * len(table) + [ANY] + places,
        out_specs=out_places,
        name=f"analyze_{cid}",
    )(*table, z, *ins)


def synth_kernel(with_grads, *refs):
    if with_grads:
        t_own, t_peer, own_ref, dk_ref, u_hbm, ext_ref, spec_ref, *rest = refs
        *rest, zin, kin, zg, s_zk, s_zg, s_kin, s_kz = rest
        peers, share = [(t_peer, SUB)], 4
    else:
        t_own, t_peer, own_ref, u_hbm, q_low, *rest = refs
        *rest, s_q, s_low = rest
        peers, share = [(None, LATE), (t_peer, SUB - LATE)], 2
    tbuf, ubuf, turned, ball, s_t, s_u, s_sib, s_x, s_y, s_dx, s_dy, s_sx, s_sy, s_sd = rest
    p = Place()
    x, c, y = p.x, p.c, p.y
    start_t, wait_local = table_loader(t_own, peers, tbuf, s_t, y)

    def store_u(g):
        return pltpu.make_async_copy(ubuf.at[g], u_hbm.at[:, pl.ds(pl.multiple_of(SUB * g, SUB), SUB)], s_u.at[g])

    @pl.loop(0, GROUPS)
    def _(g):
        start_t(g)

    friends = [p.sibling, p.xn, p.yn]
    if with_grads:
        above = [{"dp": (p.z + r) % 4} for r in range(1, 4)]
        partner = [{"h": 3 - p.h}, {"h": 3 - p.h, "w": 1 - y}]
        friends = friends + above + partner
    p.greet(friends)

    def own_to(i, sems, to):
        lo, _, hi = chunk(i, share, GATHER_ENDS)
        src = own_ref if i < COUNT - 1 else ball.at[x, c, y]
        return send(src.at[rows(lo, hi)], ball.at[x, c, y, rows(lo, hi)], sems, i, to)

    def own_x(i):
        return own_to(i, s_x, p.xn)

    def own_y(i):
        return own_to(i, s_y, p.yn)

    def own_s(i):
        return own_to(i, s_sib, p.sibling)

    def relay(i, a, b, sems, to, lo, hi):
        return send(ball.at[a, c, b, rows(lo, hi)], ball.at[a, c, b, rows(lo, hi)], sems, i, to)

    def diagonal_y(i):
        lo, mid, _ = chunk(i, share, GATHER_ENDS)
        return relay(i, 1 - x, y, s_dy, p.yn, lo, mid)

    def diagonal_x(i):
        _, mid, hi = chunk(i, share, GATHER_ENDS)
        return relay(i, x, 1 - y, s_dx, p.xn, mid, hi)

    def sibling_x(i):
        lo, _, hi = chunk(i, share, GATHER_ENDS)
        return relay(i, 1 - x, y, s_sx, p.sibling, lo, hi)

    def sibling_y(i):
        lo, _, hi = chunk(i, share, GATHER_ENDS)
        return relay(i, x, 1 - y, s_sy, p.sibling, lo, hi)

    def sibling_d(i):
        lo, _, hi = chunk(i, share, GATHER_ENDS)
        return relay(i, 1 - x, 1 - y, s_sd, p.sibling, lo, hi)

    def give_q(g):
        return send(tbuf.at[SUB * y + g], tbuf.at[SUB * y + g], s_q, g, p.yn)

    def store_low(g):
        return pltpu.make_async_copy(tbuf.at[SUB * (1 - y) + g], q_low.at[g], s_low.at[g])

    def wait_t(g):
        if with_grads:
            wait_local(g)
        else:
            at = g % SUB

            @pl.when(at >= LATE)
            def _():
                wait_local(g)

            @pl.when((at < LATE) & (g // SUB != y))
            def _():
                give_q(at).wait_recv()
                store_low(at).start()

    def give(i):
        for copy in (own_x, own_y, own_s):
            copy(i).start()

    def pass_on(i):
        own_x(i).wait_recv()
        diagonal_y(i).start()
        own_y(i).wait_recv()
        diagonal_x(i).start()
        sibling_x(i).start()
        sibling_y(i).start()

    def collect(i):
        diagonal_y(i).wait_recv()
        diagonal_x(i).wait_recv()
        sibling_d(i).start()

    def complete(i):
        for copy in (own_s, sibling_x, sibling_y, sibling_d):
            copy(i).wait_recv()

    def compute(lo, hi, k):
        @pl.loop(0, hi - lo)
        def _(n):
            g = hi - 1 - n
            wait_t(g)

            at_once = AT_ONCE if k < 2 else 2

            @pl.loop(0, SUB, step=at_once)
            def _(some):
                for m in range(at_once):
                    m = some + m
                    tiles = []
                    for n in range(GROUPS - 4 * k):
                        j = 4 * k + n
                        row = (GROUPS - sum_position(j, g)) * BLOCK + SUB * m
                        if n < 4:
                            row = jnp.where(j >= g, row, ROWS)
                        xj, cj, yj = place_of_block(j)
                        tiles.append(ball[xj, cj, yj, pl.ds(pl.multiple_of(row, SUB), SUB), :])
                    turned[m] = dot(tbuf[g, m][:, 4 * SUB * k:], jnp.concatenate(tiles, axis=0))

            ubuf[g] = jnp.swapaxes(turned[...], 0, 1)
            store_u(g).start()

    if with_grads:
        quarter = pl.ds(2 * p.z, 2)

        def grads_z(r):
            return send(own_ref.at[GRAD:ROWS], zg.at[r], s_zg, r, above[r])

        def dk_z(r):
            return send(dk_ref.at[:, pl.ds(2 * ((p.z + 1 + r) % 4), 2)], zin.at[r], s_zk, r, above[r])

        stay = jnp.where(p.low, 0, 1)
        kept = jnp.where(p.low, p.pair, GROUPS - 1 - p.pair) % 4
        given = jnp.where(p.low, GROUPS - 1 - p.pair, p.pair) % 4

        def dk_plane(r):
            to = (p.yn, *partner)[r]
            src = kin.at[stay] if r == 0 else kin.at[1 - stay]
            return send(src, spec_ref.at[kept if r == 0 else given, quarter], s_kin, r, to)

        def dk_up(r):
            return send(spec_ref.at[:, quarter], spec_ref.at[:, quarter], s_kz, r, above[r])

        for r in range(3):
            grads_z(r).start()
            dk_z(r).start()

    give(0)
    if not with_grads:
        for g in range(LATE):
            wait_local(SUB * y + LATE - 1 - g)
        give_q(LATE - 1).start()
    give(1)
    ball[x, c, y, 0:ROWS] = own_ref[...]
    for d in range(PLANE):
        ball[*slot_index(d), ROWS:] = jnp.zeros((SPARE, LANES), F32)
    for i in range(COUNT + 2):
        if i < COUNT:
            pass_on(i)
        if not with_grads and i < LATE - 1:
            give_q(LATE - 2 - i).start()
        if with_grads and i == 1:
            for r in range(3):
                grads_z(r).wait_recv()
                ball[x, c, y, GRAD:ROWS] += zg[r]
        if with_grads and i == 2:
            for r in range(3):
                dk_z(r).wait_recv()
            kin[...] = dk_ref[:, quarter] + zin[0] + zin[1] + zin[2]
            for r in range(3):
                dk_plane(r).start()
            spec_ref[kept, quarter] = kin[stay]
        if with_grads and i == 3:
            for r in range(3):
                dk_plane(r).wait_recv()
            for r in range(3):
                dk_up(r).start()
        if i < COUNT - 2:
            give(i + 2)
        if 0 < i < COUNT:
            collect(i - 1)
        if i > 1:
            complete(i - 2)
            for step in reversed(quarters(max(GROUPS - GATHER_ENDS[i - 2], 0), GROUPS - start_of(i - 2, GATHER_ENDS))):
                compute(*step)
        if i == COUNT:
            collect(i - 1)
    if with_grads:
        for d in range(PLANE):
            ext_ref[d] = ball[*slot_index(d), STAT:ROWS]
    else:
        for g in range(LATE):
            give_q(g).wait_send()
            store_low(g).wait()
    for i in range(COUNT):
        for copy in (own_x, own_y, own_s, diagonal_x, diagonal_y, sibling_x, sibling_y, sibling_d):
            copy(i).wait_send()
    if with_grads:
        for r in range(3):
            grads_z(r).wait_send()
            dk_z(r).wait_send()
            dk_plane(r).wait_send()
            dk_up(r).wait()

    @pl.loop(0, GROUPS)
    def _(g):
        store_u(g).wait()


def synth(table, own, cid, dk=None):
    with_grads = dk is not None
    quarter = vmem(*SLOTS[1:], CH, LN)
    if with_grads:
        more = [(PLANE, 2 * SUB, LANES), (4, SUB, CH, LN)]
        scratch = [vmem(NB, *SLOTS[1:], CH, LN), quarter, vmem(NB, SUB, LANES)] + [dma_sems(2, NB)] * 4
    else:
        more = [(LATE, *HALF_TABLE[1:])]
        scratch = [dma_sems(2, LATE), dma_sems(LATE)]
    return call(
        lambda *refs: synth_kernel(with_grads, *refs),
        [(NT, NM, LANES)] + more,
        [
            vmem(GROUPS, SUB, NT, NL), vmem(GROUPS, NT, SUB, LANES), vmem(SUB, NT, LANES), vmem(*SLOTS, ROWS + SPARE, LANES),
            dma_sems(GROUPS), dma_sems(GROUPS),
        ] + [dma_sems(2, COUNT)] * 8 + scratch,
        cid=cid,
        in_specs=[ANY, ANY, VMEM] + [VMEM] * with_grads,
        out_specs=(ANY, VMEM, VMEM) if with_grads else (ANY, ANY),
        name=f"synth_{cid}",
    )(*table, own, *([dk] * with_grads))


def blocks(nt):
    return (
        pl.BlockSpec((1, CH, nt, NN), lambda b, t: (b, 0, t, 0)),
        pl.BlockSpec((1, nt, CH, NN), lambda b, t: (b, t, 0, 0)),
        pl.BlockSpec((nt, NM, LN), lambda b, t: (t, 0, b)),
    )


CHAN_SPEC = pl.BlockSpec((CH, LN), lambda b, t: (b, 0))
FINAL_T = 4 * SUB
WIDE = SUB * NN


def whole(*shape):
    return pl.BlockSpec(shape, lambda b, t: (0,) * len(shape))


def first_step():
    return (pl.program_id(0) == 0) & (pl.program_id(1) == 0)


def mlp_kernel(u_ref, x_ref, tgt_ref, q_ref, base_ref, w1_ref, w2t_ref, dout_ref, dz_ref, grads_ref,
               gt_ref, g_ref, line_ref, yb_ref, h_ref, act_ref, db_ref, dh_ref):
    @pl.when(first_step())
    def _():
        grads_ref[...] = jnp.zeros_like(grads_ref)
        gt_ref[...] = signed(base_ref[...], Place().y, 2)
        g_ref[...] = gt_ref[...].T

    y = to_grid(u_ref[...], g_ref[...]).reshape(SUB, CH, NN)
    r0 = jnp.swapaxes(x_ref[0] - tgt_ref[0], 0, 1)

    def wide(v):
        return jnp.concatenate([v[t] for t in range(SUB)], axis=1)

    line_ref[...] = wide(r0 + y)
    yb_ref[...] = wide(y).astype(BF16)
    h_ref[...] = mxu(w1_ref[...], yb_ref[...], TN_DIMS)
    for t in range(SUB):
        cols = slice(NN * t, NN * (t + 1))
        h = h_ref[:, cols]
        h2 = h * h
        th = jnp.tanh(h * (GELU_A + (GELU_A * GELU_B) * h2))
        cdf = 0.5 + 0.5 * th
        act_ref[:, cols] = (h * cdf).astype(BF16)
        h_ref[:, cols] = cdf + (0.5 * h) * (1.0 - th * th) * (GELU_A + (3.0 * GELU_A * GELU_B) * h2)
    res = line_ref[...] + mxu(w2t_ref[...], act_ref[...])
    first = pl.program_id(1) * SUB
    qw = jnp.concatenate([jnp.full((1, NN), q_ref[first + t], F32) for t in range(SUB)], axis=1)
    d = qw * res
    line_ref[...] = d
    db_ref[...] = d.astype(BF16)
    loss = jnp.sum((d * res).reshape(SUB, SUB, WIDE), axis=0)
    grads_ref[0:SUB, 2 * LN:] += sum(loss[:, LN * i:LN * (i + 1)] for i in range(WIDE // LN))
    for t in range(SUB):
        dout_ref[0, t] = line_ref[:, NN * t:NN * (t + 1)]
    dh_ref[...] = (mxu(w2t_ref[...], db_ref[...], TN_DIMS) * h_ref[...]).astype(BF16)
    grads_ref[:, :LN] += mxu(yb_ref[...], dh_ref[...], NT_DIMS)
    grads_ref[:, LN:2 * LN] += mxu(db_ref[...], act_ref[...], NT_DIMS)
    dy = line_ref[...] + mxu(w1_ref[...], dh_ref[...])
    dys = jnp.concatenate([dy[:, NN * t:NN * (t + 1)] for t in range(SUB)], axis=0)
    dz_ref[...] = to_orders(dys, gt_ref[...])


def mlp(u, x, target, q, base, w1, w2t):
    hid = 2 * CH
    grid, lines, orders = blocks(SUB)
    return call(
        mlp_kernel,
        [(NB, NT, CH, NN), (NT, NM, LANES), (CH, LANES)],
        [
            vmem(NN, NN), vmem(NN, NN), vmem(CH, WIDE), vmem(CH, WIDE, dtype=BF16), vmem(hid, WIDE),
            vmem(hid, WIDE, dtype=BF16), vmem(CH, WIDE, dtype=BF16), vmem(hid, WIDE, dtype=BF16),
        ],
        grid=(NB, T8),
        in_specs=[
            orders, grid, grid, SMEM, whole(NN, NN), whole(CH, hid), whole(CH, hid),
        ],
        out_specs=(lines, orders, whole(CH, LANES)),
        name="mlp",
    )(u, x, target, q, base, w1, w2t)


def final_kernel(u_ref, x_ref, dout_ref, mu_ref, inv_ref, ext_ref, spec_ref, base_ref, out_ref, gspec_ref, gw1_ref, gw2t_ref, loss_ref,
                 g_ref, s0_ref, s1_ref):
    @pl.when(first_step())
    def _():
        g_ref[...] = signed(base_ref[...], Place().y, 1).T
        gspec_ref[0] = spec_ref[:, :, :CH]
        gspec_ref[1] = spec_ref[:, :, CH:]
        grads = ext_ref[:, SUB:].reshape(CH, LANES)
        gw1_ref[...] = grads[:, :LN]
        gw2t_ref[...] = grads[:, LN:2 * LN]
        loss = jnp.sum(jnp.sum(grads[:SUB, 2 * LN:], axis=0, keepdims=True), axis=1, keepdims=True) / TOTAL
        loss_ref[...] = loss
        sums = sum(ext_ref[n, :SUB] for n in range(PLANE)) / POINTS
        for b in range(NB):
            chans, lanes = slice(CH * b, CH * (b + 1)), slice(LN * b, LN * (b + 1))
            s0, s1 = (jnp.broadcast_to(sums[n:n + 1, lanes], (LN, LN)).T for n in range(2))
            s0_ref[chans] = s0[:CH]
            s1_ref[chans] = s1[:CH] + s1[CH:]

    chans = pl.ds(pl.multiple_of(pl.program_id(0) * CH, CH), CH)
    inv = inv_ref[:, :1]
    slope = inv_ref[...] * inv_ref[...] * s1_ref[chans]

    @pl.loop(0, FINAL_T // SUB)
    def _(k):
        ts = pl.ds(pl.multiple_of(SUB * k, SUB), SUB)
        dn = to_grid(u_ref[ts], g_ref[...]).reshape(SUB, CH, NN)
        r = jnp.swapaxes(dout_ref[0, ts] + inv * (dn - s0_ref[chans, :1]), 0, 1)
        for c in range(CH):
            for n in range(NN // LN):
                lanes = slice(LN * n, LN * (n + 1))
                out_ref[0, c, ts, lanes] = r[c, :, lanes] - (x_ref[0, c, ts, lanes] - mu_ref[c:c + 1]) * slope[c:c + 1]


def final(u, x, dout, mu, inv, ext, spec, base):
    hid = 2 * CH
    degrees = NL // 4
    grid, lines, orders = blocks(FINAL_T)
    return call(
        final_kernel,
        [(NB, CH, NT, NN), (2, degrees, CH, CH), (CH, hid), (CH, hid), (1, 1)],
        [vmem(NN, NN), vmem(NB * CH, LN), vmem(NB * CH, LN)],
        grid=(NB, NT // FINAL_T),
        in_specs=[
            orders, grid, lines, CHAN_SPEC, CHAN_SPEC,
            whole(PLANE, 2 * SUB, LANES), whole(degrees, CH, LN), whole(NN, NN),
        ],
        out_specs=(grid, whole(2, degrees, CH, CH), whole(CH, hid), whole(CH, hid), whole(1, 1)),
        name="final",
    )(u, x, dout, mu, inv, ext, spec.reshape(degrees, CH, LN), base)


def solution(mesh):
    def local_step(x, target, q, leg_fwd, leg_inv, spec_w, w1, w2):
        base = jnp.asarray(dft_matrix())
        p_own, q_own = (jnp.swapaxes(v, 1, 2).reshape(HALF_TABLE) for v in (leg_fwd, leg_inv))
        z, p_peer, mu, inv, c0, kern = front(x, p_own, jnp.moveaxis(spec_w, 1, 3), base, 0)
        a, b, q_high = analyze((p_own, p_peer), z, 1, kern, q_own=q_own)
        u, q_low = synth((q_own, q_high), b, 2)
        dout, dz, grads = mlp(u, x, target, q, base, w1, w2.T)
        da, dk = analyze((q_own, q_low, q_high), dz, 3, kern, back=(grads, a, c0))
        du, ext, spec = synth((p_own, p_peer), da, 4, dk)
        d_field, grad_spec, gw1, gw2t, loss = final(du, x, dout, mu, inv, ext, spec, base)
        return loss.reshape(()), d_field, grad_spec, gw1, gw2t.T

    grid_spec = P("dp", None, "h", "w")
    table_spec = P("w", None, "h")
    return jax.shard_map(
        local_step,
        mesh=mesh,
        in_specs=(grid_spec, grid_spec, P("h"), table_spec, table_spec, P(), P(), P()),
        out_specs=(P(), grid_spec, P(None, "h", None, None), P(), P()),
        check_vma=False,
    )
```

time: 512 us -> 474 us (0.926)
  the two profiles are of different devices: /device:TPU:0 before, /device:TPU:1 now
where the time goes in v2:
time: 474 us
  Pallas kernels  473 us (100%)
    pallas_call x2, Pallas kernels, analyze(): call(lambda *refs: analyze_kernel(share, with_q, *refs), outs, [degrees,...  164 us
    pallas_call x2, Pallas kernels, synth(): call(lambda *refs: synth_kernel(with_grads, *refs), [(NT, NM, LANES)] + m...  159 us
    pallas_call x1, Pallas kernels, mlp(): call(mlp_kernel, [(NB, NT, CH, NN), (NT, NM, LANES), (CH, LANES)], [vmem(...  70.8 us
    pallas_call x1, Pallas kernels, front(): call(front_kernel, [(NT, NM, LANES), HALF_TABLE, (NB * CH, LN), (NB * CH,...  52.9 us
    pallas_call x1, Pallas kernels, final(): call(final_kernel, [(NB, CH, NT, NN), (2, degrees, CH, CH), (CH, hid), (C...  25.7 us

profile of v2, /device:TPU:1, one launch (start us, length us, event | category | flops | bytes accessed | tf_op | source)
XLA Modules:
  0.0 474.1 jit_solution(17542247992138967902)
XLA Ops:
  0.6 52.9 %front.1 = (f32[64,128,384]{2,1,0:T(8,128)}, f32[8,8,64,128]{3,2,1,0:T(8,128)}, f32[192,128]{1,0:T(8,128)}, f32[192,128]{1,0:T(8,128)}, f32[16,128]{1,0:T(8,128)}, /*index=5*/f32[16,128,128]{2,1,0:T(8,128)}) custom-call(f32[3,64,64,256]{3,2,1,0:T(8,128)} %x_ref.3, f32[8,8,64,128]{3,2,1,0:T(8,128)} %bitcast.14, f32[2,64,64,128]{3,2,1,0:T(8,128)} %bitcast.17, ...), custom_call_target="tpu_custom_call" | custom-call | tf_op jit(solution)/shard_map/front/pallas_call | solution.py:285
  53.5 88.8 %analyze_1.1 = (f32[1104,384]{1,0:T(8,128)}, f32[1104,384]{1,0:T(8,128)}, f32[4,8,64,128]{3,2,1,0:T(8,128)}) custom-call(f32[8,8,64,128]{3,2,1,0:T(8,128)} %bitcast.15, f32[8,8,64,128]{3,2,1,0:T(8,128)} %get-tuple-element.29.refs_1_, f32[64,128,384]{2,1,0:T(8,128)} %get-tuple-element.30.refs_2_, f32[8,8,64,128]{3,2,1,0:T(8,128)} %bitcast.11, ...), custom_call_target="tpu_custom_call" | custom-call | tf_op jit(solution)/shard_map/analyze_1/pallas_call | solution.py:560
  142.4 83.9 %synth_2.1 = (f32[64,128,384]{2,1,0:T(8,128)}, f32[4,8,64,128]{3,2,1,0:T(8,128)}) custom-call(f32[8,8,64,128]{3,2,1,0:T(8,128)} %bitcast.12, f32[4,8,64,128]{3,2,1,0:T(8,128)} %get-tuple-element.32.refs_1_.refs_2_, f32[1104,384]{1,0:T(8,128)} %get-tuple-element.33.refs_2_), custom_call_target="tpu_custom_call" | custom-call | tf_op jit(solution)/shard_map/synth_2/pallas_call | solution.py:803
  226.3 70.8 %mlp.1 = (f32[3,64,64,256]{3,2,1,0:T(8,128)}, f32[64,128,384]{2,1,0:T(8,128)}, f32[64,384]{1,0:T(8,128)}) custom-call(f32[64,128,384]{2,1,0:T(8,128)} %get-tuple-element.35.u_ref, f32[3,64,64,256]{3,2,1,0:T(8,128)} %x_ref.3, f32[3,64,64,256]{3,2,1,0:T(8,128)} %tgt_ref.1, f32[64]{0:T(128)} %q_ref.1, f32[256,256]{1,0:T(8,128)} %constant.2.clone.base_ref, ...), custom_call_target="tpu_custom_call" | custom-call | tf_op jit(solution)/shard_map/mlp/pallas_call | solution.py:884
  297.1 75.6 %analyze_3.1 = (f32[1104,384]{1,0:T(8,128)}, f32[2,8,64,128]{3,2,1,0:T(8,128)}) custom-call(f32[8,8,64,128]{3,2,1,0:T(8,128)} %bitcast.13, f32[4,8,64,128]{3,2,1,0:T(8,128)} %get-tuple-element.34.refs_1_, f32[4,8,64,128]{3,2,1,0:T(8,128)} %get-tuple-element.32.refs_1_.refs_2_, f32[64,128,384]{2,1,0:T(8,128)} %get-tuple-element.36.refs_3_, ...), custom_call_target="tpu_custom_call" | custom-call | tf_op jit(solution)/shard_map/analyze_3/pallas_call | solution.py:560
  372.7 75.5 %synth_4.1 = (f32[64,128,384]{2,1,0:T(8,128)}, f32[8,16,384]{2,1,0:T(8,128)}, f32[4,8,64,128]{3,2,1,0:T(8,128)}) custom-call(f32[8,8,64,128]{3,2,1,0:T(8,128)} %bitcast.16, f32[8,8,64,128]{3,2,1,0:T(8,128)} %get-tuple-element.29.refs_1_, f32[1104,384]{1,0:T(8,128)} %get-tuple-element.40.refs_2_, f32[2,8,64,128]{3,2,1,0:T(8,128)} %get-tuple-element.41.refs_3_), custom_call_target="tpu_custom_call" | custom-call | tf_op jit(solution)/shard_map/synth_4/pallas_call | solution.py:803
  448.2 25.7 %final.1 = (f32[3,64,64,256]{3,2,1,0:T(8,128)}, f32[2,32,64,64]{3,2,1,0:T(8,128)}, f32[64,128]{1,0:T(8,128)}, f32[64,128]{1,0:T(8,128)}, f32[1,1]{1,0:T(1,128)}) custom-call(f32[64,128,384]{2,1,0:T(8,128)} %get-tuple-element.42.u_ref, f32[3,64,64,256]{3,2,1,0:T(8,128)} %x_ref.3, f32[3,64,64,256]{3,2,1,0:T(8,128)} %get-tuple-element.43.dout_ref, ...), custom_call_target="tpu_custom_call" | custom-call | tf_op jit(solution)/shard_map/final/pallas_call | solution.py:938

commit v3 on v2

v3 whole, which is shorter than its diff:
```python
import math
import numpy as np
import jax
import jax.numpy as jnp
from jax import lax
from jax.experimental import pallas as pl
from jax.experimental.pallas import tpu as pltpu
from jax.sharding import PartitionSpec as P

NORM_EPS = 1e-5
HI = lax.Precision.HIGHEST
F32 = jnp.float32
BF16 = jnp.bfloat16
MESH = pl.DeviceIdType.MESH
GELU_A = math.sqrt(2.0 / math.pi)
GELU_B = 0.044715

ROW, COL = 0, 1
NB, CH, NT, NN = 3, 64, 64, 256
NM, NL = 128, 128
LON, LAT, BATCH = 512, 256, 12
POINTS = LON * LAT
TOTAL = POINTS * BATCH * CH
LANES = NB * 2 * CH
SUB, LN = 8, 128
T8 = NT // SUB
GROUPS = NM // SUB
PLANE = 8
H_OF_PAIR = (0, 0, 3, 3, 1, 1, 2, 2)
BLOCK = SUB * SUB
PLACES = GROUPS + 1
DATA = PLACES * BLOCK
STAT = DATA
GRAD = DATA + SUB
ROWS = GRAD + SUB
SPARE = BLOCK
SLOTS = (2, 2, 2)
AT_ONCE = 4
UNROLL = 2
LATE = 2
EARLY = SUB - LATE
NN_DIMS, NT_DIMS, TN_DIMS = ((1,), (0,)), ((1,), (1,)), ((0,), (0,))
SUM_ENDS = (2, 5, 8, 11, 14, 16, 17)
GATHER_ENDS = (3, 6, 9, 12, 15, 17)
MIX_AFTER = (2, 3, 4, 6)

SMEM = pl.BlockSpec(memory_space=pltpu.SMEM)
VMEM = pl.BlockSpec(memory_space=pltpu.VMEM)
ANY = pl.BlockSpec(memory_space=pl.ANY)


def dot(a, b, dims=NN_DIMS):
    return lax.dot_general(a, b, (dims, ((), ())), precision=HI, preferred_element_type=F32)


def mxu(a, b, dims=NN_DIMS):
    return lax.dot_general(a, b, (dims, ((), ())), preferred_element_type=F32)


def call(kernel, outs, scratch=(), cid=None, **kw):
    extra = {} if cid is None else {"collective_id": cid, "has_side_effects": True}
    return pl.pallas_call(
        kernel,
        out_shape=tuple(jax.ShapeDtypeStruct(s, F32) for s in outs),
        scratch_shapes=list(scratch),
        compiler_params=pltpu.CompilerParams(vmem_limit_bytes=62 << 20, **extra),
        **kw,
    )


def vmem(*shape, dtype=F32):
    return pltpu.VMEM(shape, dtype)


def dma_sems(*shape):
    return pltpu.SemaphoreType.DMA(shape)


def row_sum(v):
    return jnp.sum(v, axis=ROW, keepdims=True)


def block_sum(v):
    return jnp.sum(jnp.sum(v, axis=COL, keepdims=True), axis=COL + 1, keepdims=True)


def turn(v):
    return jnp.swapaxes(v, ROW, COL)


def rows(lo, hi):
    return pl.ds(lo, hi - lo)


def dft_matrix():
    theta = 2.0 * np.pi * ((np.arange(NN)[:, None] * np.arange(NM)[None, :]) % LON) / LON
    return (np.concatenate([np.cos(theta), -np.sin(theta)], axis=COL) / math.sqrt(LON)).astype(np.float32)


def signed(base, half, weight):
    m = lax.broadcasted_iota(jnp.int32, base.shape, 1) % NM
    out = jnp.where((m % 2) * half == 1, -base, base)
    return jnp.where(m == 0, out, weight * out) if weight > 1 else out


def to_orders(lines, ft):
    z = dot(lines, ft).reshape(SUB, CH, NN)
    z = jnp.concatenate([z[:, :, :NM], z[:, :, NM:]], axis=COL)
    return jnp.swapaxes(z, 1, 2)


def to_grid(orders, ft):
    u = jnp.swapaxes(orders, 1, 2)
    u = jnp.concatenate([u[:, :CH, :], u[:, CH:, :]], axis=2).reshape(SUB * CH, NN)
    return dot(u, ft)


def place_of_block(j):
    k = min(j, GROUPS - 1 - j)
    return H_OF_PAIR[k] // 2, H_OF_PAIR[k] % 2, k % 2


def slot_index(d):
    return d // 4, d // 2 % 2, d % 2


def sum_position(j, g):
    k = min(j, GROUPS - 1 - j)
    return 2 * g + 1 if j < SUB else jnp.where(g <= k, 2 * g, k + 1 + g)


def start_of(i, ends):
    return ends[i - 1] if i > 0 else 0


def chunk(i, share, ends):
    lo = start_of(i, ends) * BLOCK
    hi = ends[i] * BLOCK if ends[i] < PLACES else ROWS
    return lo, lo + (hi - lo) * share // BLOCK * SUB, hi


class Place:
    def __init__(self):
        self.h, self.y, self.z = lax.axis_index("h"), lax.axis_index("w"), lax.axis_index("dp")
        self.x, self.c = self.h // 2, self.h % 2
        self.slot = 2 * self.h + self.y
        self.low = self.h < 2
        self.pair = jnp.where(self.low, 4 * self.h, 14 - 4 * self.h) + self.y
        self.ox, self.oy = 1 - self.x, 1 - self.y
        self.sibling = {"h": 2 * self.x + 1 - self.c}
        self.xn = {"h": 2 * self.ox + self.c}
        self.yn = {"w": self.oy}

    def plane(self, r):
        s = (self.slot + r) % PLANE
        return {"h": s // 2, "w": s % 2}

    def greet(self, others):
        barrier = pltpu.get_barrier_semaphore()
        for other in others:
            pl.semaphore_signal(barrier, inc=1, device_id=other, device_id_type=MESH)
        pl.semaphore_wait(barrier, len(others))


def send(src, dst, sems, i, to):
    return pltpu.make_async_remote_copy(
        src_ref=src, dst_ref=dst, send_sem=sems.at[0, i], recv_sem=sems.at[1, i], device_id=to, device_id_type=MESH
    )


CB = 16
PIECES = CH // CB
HALF_TABLE = (SUB, SUB, NT, NL)


def near_far(k):
    return pl.ds(pl.multiple_of(SUB * k, SUB), SUB), pl.ds(pl.multiple_of(SUB * (GROUPS - 1 - k), SUB), SUB)


def front_kernel(x_hbm, p_hbm, w_hbm, base_ref, z_hbm, p_peer, mu_ref, inv_ref, c0_ref, kern_ref,
                 xbuf, wbuf, pbuf, cols, pay, sbuf, zbuf, ftbuf, turned, own, s_x, s_w, s_z, s_p, s_st):
    place = Place()
    near, far = near_far(place.pair)

    def load_x(n):
        b, part = n // PIECES, pl.ds(n % PIECES * CB, CB)
        return pltpu.make_async_copy(x_hbm.at[b, part], xbuf.at[b, part], s_x.at[n])

    def load_w(i):
        return pltpu.make_async_copy(w_hbm.at[i], wbuf.at[i], s_w.at[i])

    def load_p(g):
        return pltpu.make_async_copy(p_hbm.at[g], pbuf.at[g], s_p.at[2, g])

    def give_p(g):
        return send(pbuf.at[g], p_peer.at[g], s_p, g, place.yn)

    @pl.loop(0, SUB)
    def _(g):
        load_p(g).start()

    @pl.loop(0, NB * PIECES)
    def _(n):
        load_x(n).start()

    for i in range(2):
        load_w(i).start()
    others = range(1, PLANE)
    place.greet([place.plane(r) for r in others])

    def offer(lo, hi):
        @pl.loop(lo, hi)
        def _(g):
            load_p(g).wait()
            give_p(g).start()

    offer(0, 1)
    cols[...] = jnp.zeros_like(cols)

    @pl.loop(0, NB * PIECES)
    def _(n):
        load_x(n).wait()
        v = xbuf[n // PIECES, pl.ds(n % PIECES * CB, CB)]
        mean = block_sum(v) / (NT * NN)
        diff = v - mean
        m2 = block_sum(diff * diff)
        lane = lax.broadcasted_iota(jnp.int32, (CB, 1, LN), 2)
        cols[pl.ds(pl.multiple_of(n * CB, CB), CB)] = jnp.where(lane < CH, mean, m2).reshape(CB, LN)
    wide = cols[...].T
    p1 = jnp.where(place.y == 0, row_sum(pbuf[0, 0]), 0.0)
    pay[...] = jnp.concatenate([
        *(wide[n:n + 1] for n in (0, CH)), jnp.concatenate([p1, p1], axis=COL), jnp.zeros((SUB - 3, NN), F32)
    ], axis=ROW)

    def give_stats(r):
        return send(pay, sbuf.at[place.slot], s_st, r, place.plane(r))

    for r in others:
        give_stats(r).start()
    offer(1, SUB)
    sbuf[place.slot] = pay[...]
    ftbuf[...] = signed(base_ref[...], place.y, 1)

    for i in range(2):
        load_w(i).wait()

    @pl.loop(0, CH)
    def _(i):
        turned[...] = jnp.concatenate([wbuf[n, i] for n in range(2)], axis=ROW).T
        own[i, :SUB] = turned[near]
        own[i, SUB:] = turned[far]

    top = turn(own[...])
    kern_ref[:, :CH] = top
    kern_ref[:, CH:] = jnp.concatenate([-top[:, :, CH:], top[:, :, :CH]], axis=2)

    for r in others:
        give_stats(r).wait_recv()
    means, m2s, p1s = (jnp.concatenate([sbuf[s, n:n + 1] for s in range(PLANE)], axis=ROW) for n in range(3))
    mu = row_sum(means) / PLANE
    dev = means - mu
    var = (row_sum(m2s) + (NT * NN) * row_sum(dev * dev)) / POINTS
    c0 = math.sqrt(LON) * row_sum(p1s)
    mu_ref[...], inv_ref[...], turned[...] = (
        jnp.broadcast_to(v, (LN, NN)).T[:n] for v, n in ((mu, NB * CH), (lax.rsqrt(var + NORM_EPS), NB * CH), (c0, NL))
    )
    c0_ref[:SUB] = turned[near]
    c0_ref[SUB:] = turned[far]

    def store_z(n):
        t = pl.multiple_of(n % T8 * SUB, SUB)
        lanes = pl.multiple_of(n // T8 * LN, LN)
        return pltpu.make_async_copy(zbuf.at[n % 2], z_hbm.at[pl.ds(t, SUB), :, pl.ds(lanes, LN)], s_z.at[n % 2])

    @pl.loop(0, NB * T8)
    def _(n):
        @pl.when(n >= 2)
        def _():
            store_z(n - 2).wait()

        b = n // T8
        xt = turn(xbuf[b, :, pl.ds(pl.multiple_of(n % T8 * SUB, SUB), SUB), :])
        chans = pl.ds(pl.multiple_of(b * CH, CH), CH)
        xn = (xt - mu_ref[chans, :1]) * inv_ref[chans, :1]
        zbuf[n % 2] = to_orders(xn.reshape(SUB * CH, NN), ftbuf[...])
        store_z(n).start()

    for n in range(2):
        store_z(NB * T8 - 2 + n).wait()
    for r in others:
        give_stats(r).wait_send()

    @pl.loop(0, SUB)
    def _(g):
        give_p(g).wait()


def front(x, p_own, spec_w, base, cid):
    return call(
        front_kernel,
        [(NT, NM, LANES), HALF_TABLE, (NB * CH, LN), (NB * CH, LN), (2 * SUB, LN), (2 * SUB, LN, LN)],
        [
            vmem(NB, CH, NT, NN), vmem(2, CH, CH, NL), vmem(*HALF_TABLE), vmem(NN, LN), vmem(SUB, NN), vmem(PLANE, SUB, NN),
            vmem(2, SUB, NM, LN), vmem(NN, NN), vmem(NL, LN), vmem(CH, 2 * SUB, LN),
            dma_sems(NB * PIECES), dma_sems(2), dma_sems(2), dma_sems(3, SUB), dma_sems(2, PLANE),
        ],
        cid=cid,
        in_specs=[ANY, ANY, ANY, VMEM],
        out_specs=(ANY, ANY, VMEM, VMEM, VMEM, VMEM),
        name="front",
    )(x, p_own, spec_w, base)


def table_loader(own, peers, tbuf, sems, y):
    def copy(src, at, g):
        return pltpu.make_async_copy(src.at[at], tbuf.at[g], sems.at[g])

    def start(g):
        at = g % SUB
        away = g // SUB != y

        @pl.when(g // SUB == y)
        def _():
            copy(own, at, g).start()

        first = 0
        for src, count in peers:
            if src is not None:
                @pl.when(away & (at >= first) & (at < first + count))
                def _(src=src, first=first):
                    copy(src, at - first, g).start()
            first += count

    def wait(g):
        copy(own, 0, g).wait()

    return start, wait


def quarters(lo, hi):
    return [(max(lo, 4 * k), min(hi, 4 * k + 4), k) for k in range(4) if max(lo, 4 * k) < min(hi, 4 * k + 4)]


def by_degree(ref, v):
    n = v.shape[0] // SUB
    t = turn(v.reshape(n, SUB, LANES))
    for b in range(NB):
        ref[:, n * b:n * (b + 1)] = t[:, :, LN * b:LN * (b + 1)]


def put_degrees(ref, parts, first, count):
    n = count * SUB
    t = jnp.concatenate([parts[:, n * b:n * (b + 1)] for b in range(NB)], axis=2)
    t = turn(t)
    for i in range(count):
        to = BLOCK * (GROUPS - first - i)
        ref[to:to + BLOCK] = t[SUB * i:SUB * (i + 1)].reshape(BLOCK, LANES)


def near_mask(first, count, pair):
    place = first + lax.broadcasted_iota(jnp.int32, (NB * count * SUB, LN), 0) % (count * SUB) // SUB
    return (place % 2 == 1) & (place < 2 * (pair + 1))


def mix_places(first, count, pair, a_ref, kern_ref, b_ref, a, b):
    rows_in = a_ref[BLOCK * first:BLOCK * (first + count)]
    n = NB * count * SUB
    by_degree(a, rows_in)
    near = near_mask(first, count, pair)

    @pl.loop(0, SUB, unroll=UNROLL)
    def _(l):
        al = a[l, :n]
        b[l, :n] = jnp.where(near, dot(al, kern_ref[l]), dot(al, kern_ref[SUB + l]))

    put_degrees(b_ref, b, first, count)


def mix_back_places(first, count, pair, a_ref, db_ref, kern_ref, c0_ref, da_ref, dk_ref, s_ref, a, db, da):
    at = slice(BLOCK * first, BLOCK * (first + count))
    n = count * SUB
    by_degree(a, a_ref[at])
    by_degree(db, db_ref[at])
    near = near_mask(first, count, pair)

    @pl.loop(0, SUB, unroll=UNROLL)
    def _(l):
        al, dl = a[l, :NB * n], db[l, :NB * n]
        v = jnp.where(near, dot(dl, kern_ref[l], NT_DIMS), dot(dl, kern_ref[SUB + l], NT_DIMS))
        da[l, :NB * n] = v
        product = v * al
        s_ref[1:2] += jnp.concatenate([row_sum(product[n * i:n * (i + 1)]) for i in range(NB)], axis=COL)
        if first == 0:
            for row, c0 in ((SUB, l), (0, SUB + l)):
                c0 = jnp.concatenate([c0_ref[pl.ds(c0, 1)]] * NB, axis=COL)
                s_ref[0:1] += c0 * jnp.concatenate([v[n * i + row:n * i + row + 1] for i in range(NB)], axis=COL)
        for i, part in enumerate((jnp.where(near, al, 0.0), jnp.where(near, 0.0, al))):
            g = dot(part, dl, TN_DIMS)
            low = g[CH:]
            dk_ref[i, l] += g[:CH] + jnp.concatenate([low[:, CH:], -low[:, :CH]], axis=COL)

    put_degrees(da_ref, da, first, count)


def analyze_kernel(share, with_q, *refs):
    if with_q:
        t_own, t_peer, z_hbm, q_own, kern_ref, out_ref, mix_ref, q_peer, a_deg, b_deg, qbuf, *rest = refs
        peers = [(t_peer, SUB)]
    else:
        t_own, t_low, t_high, z_hbm, ext_ref, kern_ref, a_ref, c0_ref, mix_ref, dk_ref, a_deg, b_deg, out_ref, s_ref, da_deg, *rest = refs
        peers = [(t_low, LATE), (t_high, EARLY)]
        dk_ref[...] = jnp.zeros_like(dk_ref)
        s_ref[...] = jnp.zeros_like(s_ref)
    tbuf, zbuf, turned, part, sib, rx, ry, fx, fy, s_t, s_z, s_q, s_sib, s_x, s_y, s_fx, s_fy = rest
    count = len(SUM_ENDS)
    p = Place()
    x, c, y = p.x, p.c, p.y
    start_t, wait_t = table_loader(t_own, peers, tbuf, s_t, y)

    def load_z(g):
        return pltpu.make_async_copy(z_hbm.at[:, pl.ds(pl.multiple_of(SUB * g, SUB), SUB)], zbuf.at[g], s_z.at[g])

    @pl.loop(0, GROUPS)
    def _(g):
        start_t(g)
        load_z(g).start()

    p.greet([p.sibling, p.xn, p.yn])
    for d in range(PLANE):
        spare = part.at[slot_index(d)]
        spare[STAT:ROWS] = jnp.zeros((ROWS - STAT, LANES), F32)
        if not with_q:
            spare[STAT:GRAD] = ext_ref[SUB * d:SUB * (d + 1)]

    def load_q(g):
        return pltpu.make_async_copy(q_own.at[LATE + g], qbuf.at[g], s_q.at[2, g])

    def give_q(g):
        return send(qbuf.at[g], q_peer.at[g], s_q, g, p.yn)

    def compute(lo, hi, k):
        @pl.loop(lo, hi)
        def _(g):
            wait_t(g)
            load_z(g).wait()
            turned[...] = turn(zbuf[g])

            at_once = AT_ONCE if k < 2 else 2

            @pl.loop(0, SUB, step=at_once)
            def _(some):
                for m in range(at_once):
                    m = some + m
                    r = dot(tbuf[g, m].T[4 * SUB * k:], turned[m])
                    for n in range(GROUPS - 4 * k):
                        j = 4 * k + n
                        row = sum_position(j, g) * BLOCK + SUB * m
                        if n < 4:
                            row = jnp.where(j >= g, row, ROWS)
                        xj, cj, yj = place_of_block(j)
                        part[xj, cj, yj, pl.ds(pl.multiple_of(row, SUB), SUB), :] = r[SUB * n:SUB * (n + 1)]

    def to_sibling(i):
        lo, _, hi = chunk(i, share, SUM_ENDS)
        return send(part.at[:, 1 - c, :, rows(lo, hi)], sib.at[:, :, rows(lo, hi)], s_sib, i, p.sibling)

    def to_x(i):
        lo, mid, _ = chunk(i, share, SUM_ENDS)
        return send(part.at[p.ox, c, :, rows(lo, mid)], rx.at[:, rows(lo, mid)], s_x, i, p.xn)

    def to_y(i):
        _, mid, hi = chunk(i, share, SUM_ENDS)
        return send(part.at[:, c, p.oy, rows(mid, hi)], ry.at[:, rows(mid, hi)], s_y, i, p.yn)

    def forward_y(i):
        lo, mid, _ = chunk(i, share, SUM_ENDS)
        return send(part.at[x, c, p.oy, rows(lo, mid)], fy.at[rows(lo, mid)], s_fy, i, p.yn)

    def forward_x(i):
        _, mid, hi = chunk(i, share, SUM_ENDS)
        return send(part.at[p.ox, c, y, rows(mid, hi)], fx.at[rows(mid, hi)], s_fx, i, p.xn)

    def chip_sum(i):
        lo, _, hi = chunk(i, share, SUM_ENDS)
        to_sibling(i).wait_recv()

        @pl.loop(lo, hi, step=2 * SUB)
        def _(row):
            some = pl.ds(pl.multiple_of(row, SUB), 2 * SUB)
            for a in range(2):
                for b in range(2):
                    part[a, c, b, some] += sib[a, b, some]

        to_x(i).start()
        to_y(i).start()
        if with_q and i < EARLY:
            give_q(i).start()

    def half_sum(i):
        lo, mid, hi = chunk(i, share, SUM_ENDS)
        to_x(i).wait_recv()
        part[x, c, p.oy, rows(lo, mid)] += rx[p.oy, rows(lo, mid)]
        forward_y(i).start()
        to_y(i).wait_recv()
        part[p.ox, c, y, rows(mid, hi)] += ry[p.ox, rows(mid, hi)]
        forward_x(i).start()
        out_ref[rows(lo, mid)] = part[x, c, y, rows(lo, mid)] + rx[y, rows(lo, mid)]
        out_ref[rows(mid, hi)] = part[x, c, y, rows(mid, hi)] + ry[x, rows(mid, hi)]

    def last_sum(i):
        lo, mid, hi = chunk(i, share, SUM_ENDS)
        forward_y(i).wait_recv()
        out_ref[rows(lo, mid)] += fy[rows(lo, mid)]
        forward_x(i).wait_recv()
        out_ref[rows(mid, hi)] += fx[rows(mid, hi)]

    def mixed(first, end):
        places = end - first
        if with_q:
            mix_places(first, places, p.pair, out_ref, kern_ref, mix_ref, a_deg, b_deg)
        else:
            mix_back_places(first, places, p.pair, a_ref, out_ref, kern_ref, c0_ref, mix_ref, dk_ref, s_ref, a_deg, b_deg, da_deg)

    if with_q:
        for g in range(EARLY):
            load_q(g).start()
        for g in range(EARLY):
            load_q(g).wait()
    for i in range(count + LAST_LAG):
        if i < count:
            for step in quarters(max(start_of(i, SUM_ENDS) - 1, 0), SUM_ENDS[i] - 1):
                compute(*step)
            to_sibling(i).start()
        if 0 < i <= count:
            chip_sum(i - 1)
        if HALF_LAG <= i < count + HALF_LAG:
            half_sum(i - HALF_LAG)
        if i >= LAST_LAG:
            last_sum(i - LAST_LAG)
            if i - LAST_LAG in MIX_AFTER:
                n = MIX_AFTER.index(i - LAST_LAG)
                mixed(SUM_ENDS[MIX_AFTER[n - 1]] if n > 0 else 0, SUM_ENDS[MIX_AFTER[n]])
    if with_q:
        mix_ref[STAT:] = jnp.zeros((ROWS - STAT, LANES), F32)
    else:
        mix_ref[STAT:GRAD] = s_ref[...]
        mix_ref[GRAD:] = out_ref[STAT:GRAD]
    for i in range(count):
        for copy in (to_sibling, to_x, to_y, forward_x, forward_y):
            copy(i).wait_send()
    if with_q:
        for g in range(EARLY):
            give_q(g).wait()


HALF_LAG, LAST_LAG = 2, 4
MOST = 8


def analyze(table, z, cid, kern, q_own=None, back=()):
    with_q = q_own is not None
    share = 7 if with_q else 4
    piece = (EARLY, *HALF_TABLE[1:])
    half = vmem(ROWS, LANES)
    pair = vmem(2, ROWS, LANES)
    degrees = vmem(SUB, NB * MOST * SUB, LN)
    if with_q:
        ins, places, outs = (q_own, kern), [ANY, VMEM], [(ROWS, LANES), (ROWS, LANES), piece]
        out_places, more = (VMEM, VMEM, ANY), [vmem(*piece)]
    else:
        ext, a, c0 = back
        ins, places, outs = (ext, kern, a, c0), [VMEM] * 4, [(ROWS, LANES), (2, SUB, CH, LN)]
        out_places, more = (VMEM, VMEM), [half, vmem(SUB, LANES), degrees]
    return call(
        lambda *refs: analyze_kernel(share, with_q, *refs),
        outs,
        [degrees, degrees] + more + [
            vmem(GROUPS, SUB, NT, NL), vmem(GROUPS, NT, SUB, LANES), vmem(SUB, NT, LANES), vmem(*SLOTS, ROWS + SPARE, LANES),
            vmem(*SLOTS[1:], ROWS, LANES), pair, pair, half, half,
            dma_sems(GROUPS), dma_sems(GROUPS), dma_sems(3, EARLY),
        ] + [dma_sems(2, len(SUM_ENDS))] * 5,
        cid=cid,
        in_specs=[ANY] * len(table) + [ANY] + places,
        out_specs=out_places,
        name=f"analyze_{cid}",
    )(*table, z, *ins)


class Gather:
    def __init__(self, p, own_ref, ball, sems):
        self.p, self.own_ref, self.ball, self.sems = p, own_ref, ball, sems

    def relay(self, piece, n, to, a, b, part, src=None):
        i, lo, mid, hi, lanes = piece
        at = (rows(lo, hi), rows(lo, mid), rows(mid, hi))[part]
        here = self.ball.at[a, self.p.c, b, at, lanes]
        return send(here if src is None else src.at[at, lanes], here, self.sems[n], i, to)

    def own(self, piece, n, to):
        return self.relay(piece, n, to, self.p.x, self.p.y, 0, self.own_ref)

    def own_x(self, piece):
        return self.own(piece, 0, self.p.xn)

    def own_y(self, piece):
        return self.own(piece, 1, self.p.yn)

    def own_s(self, piece):
        return self.own(piece, 2, self.p.sibling)

    def diagonal_y(self, piece):
        return self.relay(piece, 3, self.p.yn, self.p.ox, self.p.y, 1)

    def diagonal_x(self, piece):
        return self.relay(piece, 4, self.p.xn, self.p.x, self.p.oy, 2)

    def sibling_x(self, piece):
        return self.relay(piece, 5, self.p.sibling, self.p.ox, self.p.y, 0)

    def sibling_y(self, piece):
        return self.relay(piece, 6, self.p.sibling, self.p.x, self.p.oy, 0)

    def sibling_d(self, piece):
        return self.relay(piece, 7, self.p.sibling, self.p.ox, self.p.oy, 0)

    def give(self, piece):
        for copy in (self.own_x, self.own_y, self.own_s):
            copy(piece).start()

    def pass_on(self, piece):
        self.own_x(piece).wait_recv()
        self.diagonal_y(piece).start()
        self.own_y(piece).wait_recv()
        self.diagonal_x(piece).start()
        self.sibling_x(piece).start()
        self.sibling_y(piece).start()

    def collect(self, piece):
        self.diagonal_y(piece).wait_recv()
        self.diagonal_x(piece).wait_recv()
        self.sibling_d(piece).start()

    def complete(self, piece):
        for copy in (self.own_s, self.sibling_x, self.sibling_y, self.sibling_d):
            copy(piece).wait_recv()

    def finish(self, piece):
        for copy in (
            self.own_x, self.own_y, self.own_s, self.diagonal_y, self.diagonal_x,
            self.sibling_x, self.sibling_y, self.sibling_d,
        ):
            copy(piece).wait_send()


def inverse_sums(tbuf, ball, turned, g, k, lanes, at_once):
    @pl.loop(0, SUB, step=at_once)
    def _(some):
        for m in range(at_once):
            m = some + m
            tiles = []
            for n in range(GROUPS - 4 * k):
                j = 4 * k + n
                row = (GROUPS - sum_position(j, g)) * BLOCK + SUB * m
                if n < 4:
                    row = jnp.where(j >= g, row, ROWS)
                xj, cj, yj = place_of_block(j)
                tiles.append(ball[xj, cj, yj, pl.ds(pl.multiple_of(row, SUB), SUB), lanes])
            turned[m] = dot(tbuf[g, m][:, 4 * SUB * k:], jnp.concatenate(tiles, axis=ROW))


ALL = pl.ds(0, LANES)


def synth_kernel(t_own, t_peer, own_ref, dk_ref, u_hbm, ext_ref, spec_ref, tbuf, ubuf, turned, ball, zin, kin, zg,
                 s_t, s_u, s_zk, s_zg, s_kin, s_kz, *sems):
    p = Place()
    x, c, y = p.x, p.c, p.y
    start_t, wait_t = table_loader(t_own, [(t_peer, SUB)], tbuf, s_t, y)
    count = len(GATHER_ENDS)

    def store_u(g):
        return pltpu.make_async_copy(ubuf.at[g], u_hbm.at[:, pl.ds(pl.multiple_of(SUB * g, SUB), SUB)], s_u.at[g])

    @pl.loop(0, GROUPS)
    def _(g):
        start_t(g)

    above = [{"dp": (p.z + r) % 4} for r in range(1, 4)]
    partner = [{"h": 3 - p.h}, {"h": 3 - p.h, "w": p.oy}]
    p.greet([p.sibling, p.xn, p.yn, *above, *partner])

    early = Gather(p, own_ref, ball, sems)
    late = Gather(p, ball.at[x, c, y], ball, sems)

    def piece(i):
        return i, *chunk(i, 4, GATHER_ENDS), ALL

    def gather(i):
        return late if i == count - 1 else early

    quarter = pl.ds(2 * p.z, 2)

    def grads_z(r):
        return send(own_ref.at[GRAD:ROWS], zg.at[r], s_zg, r, above[r])

    def dk_z(r):
        return send(dk_ref.at[:, pl.ds(2 * ((p.z + 1 + r) % 4), 2)], zin.at[r], s_zk, r, above[r])

    stay = jnp.where(p.low, 0, 1)
    kept = jnp.where(p.low, p.pair, GROUPS - 1 - p.pair) % 4
    given = jnp.where(p.low, GROUPS - 1 - p.pair, p.pair) % 4

    def dk_plane(r):
        to = (p.yn, *partner)[r]
        src = kin.at[stay] if r == 0 else kin.at[1 - stay]
        return send(src, spec_ref.at[kept if r == 0 else given, quarter], s_kin, r, to)

    def dk_up(r):
        return send(spec_ref.at[:, quarter], spec_ref.at[:, quarter], s_kz, r, above[r])

    def compute(lo, hi, k):
        @pl.loop(0, hi - lo)
        def _(n):
            g = hi - 1 - n
            wait_t(g)
            inverse_sums(tbuf, ball, turned, g, k, ALL, AT_ONCE)
            ubuf[g] = turn(turned[...])
            store_u(g).start()

    for r in range(3):
        grads_z(r).start()
        dk_z(r).start()
    for i in range(2):
        gather(i).give(piece(i))
    ball[x, c, y, 0:ROWS] = own_ref[...]
    for d in range(PLANE):
        ball[*slot_index(d), ROWS:] = jnp.zeros((SPARE, LANES), F32)
    for i in range(count + 2):
        if i < count:
            gather(i).pass_on(piece(i))
        if i == 1:
            for r in range(3):
                grads_z(r).wait_recv()
                ball[x, c, y, GRAD:ROWS] += zg[r]
        if i == 2:
            for r in range(3):
                dk_z(r).wait_recv()
            kin[...] = dk_ref[:, quarter] + zin[0] + zin[1] + zin[2]
            for r in range(3):
                dk_plane(r).start()
            spec_ref[kept, quarter] = kin[stay]
        if i == 3:
            for r in range(3):
                dk_plane(r).wait_recv()
            for r in range(3):
                dk_up(r).start()
        if i < count - 2:
            gather(i + 2).give(piece(i + 2))
        if 0 < i < count:
            gather(i - 1).collect(piece(i - 1))
        if i > 1:
            gather(i - 2).complete(piece(i - 2))
            for step in reversed(quarters(max(GROUPS - GATHER_ENDS[i - 2], 0), GROUPS - start_of(i - 2, GATHER_ENDS))):
                compute(*step)
        if i == count:
            gather(i - 1).collect(piece(i - 1))
    for d in range(PLANE):
        ext_ref[d] = ball[*slot_index(d), STAT:ROWS]
    for i in range(count):
        gather(i).finish(piece(i))
    for r in range(3):
        grads_z(r).wait_send()
        dk_z(r).wait_send()
        dk_plane(r).wait_send()
        dk_up(r).wait()

    @pl.loop(0, GROUPS)
    def _(g):
        store_u(g).wait()


def synth(table, own, cid, dk):
    quarter = (*SLOTS[1:], CH, LN)
    return call(
        synth_kernel,
        [(NT, NM, LANES), (PLANE, 2 * SUB, LANES), (4, SUB, CH, LN)],
        [
            vmem(GROUPS, SUB, NT, NL), vmem(GROUPS, NT, SUB, LANES), vmem(SUB, NT, LANES), vmem(*SLOTS, ROWS + SPARE, LANES),
            vmem(NB, *quarter), vmem(*quarter), vmem(NB, SUB, LANES), dma_sems(GROUPS), dma_sems(GROUPS),
        ] + [dma_sems(2, NB)] * 4 + [dma_sems(2, len(GATHER_ENDS))] * 8,
        cid=cid,
        in_specs=[ANY, ANY, VMEM, VMEM],
        out_specs=(ANY, VMEM, VMEM),
        name=f"synth_{cid}",
    )(*table, own, dk)


WIDE = SUB * NN
BT = 2 * SUB
PER = NT // BT
FIRST = 9 * BLOCK


def grid_stage(n, orders, x, tgt, q_ref, weights, dout, dz, grads_ref, scratch):
    g_ref, gt_ref, w1_ref, w2t_ref = weights
    some = range(BT // SUB)
    ts = [slice(SUB * k, SUB * (k + 1)) for k in some]

    def columns(t):
        return slice(NN * t, NN * (t + 1))

    def wide(v):
        return jnp.concatenate([v[t] for t in range(SUB)], axis=COL)

    line, yb, hid, act, db, dh = ([ref.at[k] for k in some] for ref in scratch)
    for k in some:
        y = to_grid(orders[k][...], g_ref[...]).reshape(SUB, CH, NN)
        r0 = turn(x[:, ts[k]] - tgt[:, ts[k]])
        line[k][...] = wide(r0 + y)
        yb[k][...] = wide(y).astype(BF16)
    for k in some:
        hid[k][...] = mxu(w1_ref[...], yb[k][...], TN_DIMS)
        for t in range(SUB):
            h = hid[k][:, columns(t)]
            h2 = h * h
            th = jnp.tanh(h * (GELU_A + (GELU_A * GELU_B) * h2))
            cdf = 0.5 + 0.5 * th
            act[k][:, columns(t)] = (h * cdf).astype(BF16)
            hid[k][:, columns(t)] = cdf + (0.5 * h) * (1.0 - th * th) * (GELU_A + (3.0 * GELU_A * GELU_B) * h2)
    for k in some:
        res = line[k][...] + mxu(w2t_ref[...], act[k][...])
        first = n % PER * BT + SUB * k
        d = jnp.concatenate([jnp.full((1, NN), q_ref[first + t], F32) for t in range(SUB)], axis=COL) * res
        line[k][...] = d
        db[k][...] = d.astype(BF16)
        loss = jnp.sum((d * res).reshape(SUB, SUB, WIDE), axis=ROW)
        grads_ref[:SUB, 2 * LN:] += sum(loss[:, LN * i:LN * (i + 1)] for i in range(WIDE // LN))
        for t in range(SUB):
            dout[SUB * k + t] = line[k][:, columns(t)]
    for k in some:
        dh[k][...] = (mxu(w2t_ref[...], db[k][...], TN_DIMS) * hid[k][...]).astype(BF16)
        grads_ref[:, :LN] += mxu(yb[k][...], dh[k][...], NT_DIMS)
        grads_ref[:, LN:2 * LN] += mxu(db[k][...], act[k][...], NT_DIMS)
    for k in some:
        dy = line[k][...] + mxu(w1_ref[...], dh[k][...])
        dys = jnp.concatenate([dy[:, columns(t)] for t in range(SUB)], axis=ROW)
        dz[ts[k]] = to_orders(dys, gt_ref[...])


def forward_kernel(t_own, t_high, own_ref, x_hbm, tgt_hbm, q_ref, base_ref, w1_ref, w2t_ref, dout_hbm, dz_hbm, q_low, grads_ref,
                   tbuf, ubuf, turned, ball, xbuf, tgtbuf, dbuf, zbuf, g_ref, gt_ref, line, yb, hid, act, db, dh,
                   s_t, s_in, s_out, s_q, s_low, *sems):
    p = Place()
    y = p.y
    start_t, wait_local = table_loader(t_own, [(None, LATE), (t_high, EARLY)], tbuf, s_t, y)
    gather = Gather(p, own_ref, ball, sems)
    share = 2

    def lanes(s):
        return pl.ds(pl.multiple_of(LN * s, LN), LN)

    def piece(s, half):
        lo, hi = ((0, FIRST), (FIRST, ROWS))[half]
        return 2 * s + half, lo, lo + (hi - lo) * share // BLOCK * SUB, hi, lanes(s)

    def each(step, s):
        for half in range(2):
            step(piece(s, half))

    def block(n):
        return n // PER, pl.ds(pl.multiple_of(n % PER * BT, BT), BT)

    def loads(n):
        b, t = block(n)
        return [
            pltpu.make_async_copy(src.at[b, :, t], dst.at[n % 2], s_in.at[i, n % 2])
            for i, (src, dst) in enumerate(((x_hbm, xbuf), (tgt_hbm, tgtbuf)))
        ]

    def stores(n):
        b, t = block(n)
        return [
            pltpu.make_async_copy(dbuf.at[n % 2], dout_hbm.at[b, t], s_out.at[0, n % 2]),
            pltpu.make_async_copy(zbuf.at[n % 2], dz_hbm.at[t, :, lanes(b)], s_out.at[1, n % 2]),
        ]

    def give_q(g):
        return send(tbuf.at[SUB * y + g], tbuf.at[SUB * y + g], s_q, g, p.yn)

    def store_low(g):
        return pltpu.make_async_copy(tbuf.at[SUB * p.oy + g], q_low.at[g], s_low.at[g])

    @pl.loop(0, GROUPS)
    def _(g):
        start_t(g)

    p.greet([p.sibling, p.xn, p.yn])
    gather.give(piece(0, 0))
    for g in reversed(range(LATE)):
        wait_local(SUB * y + g)
        give_q(g).start()
        if g == LATE - 1:
            gather.give(piece(0, 1))
    for copy in loads(0):
        copy.start()
    ball[p.x, p.c, y, :ROWS] = own_ref[...]
    for d in range(PLANE):
        ball[*slot_index(d), ROWS:] = jnp.zeros((SPARE, LANES), F32)
    grads_ref[...] = jnp.zeros_like(grads_ref)
    gt_ref[...] = signed(base_ref[...], y, 2)
    g_ref[...] = gt_ref[...].T
    each(gather.pass_on, 0)
    each(gather.give, 1)
    each(gather.collect, 0)

    @pl.loop(0, NB)
    def _(s):
        each(gather.complete, s)
        for k in reversed(range(4)):
            @pl.loop(0, 4)
            def _(n):
                g = 4 * k + 3 - n
                at = g % SUB

                @pl.when((s == 0) & (at >= LATE))
                def _():
                    wait_local(g)

                @pl.when((s == 0) & (at < LATE) & (g // SUB != y))
                def _():
                    give_q(at).wait_recv()
                    store_low(at).start()

                inverse_sums(tbuf, ball, turned, g, k, lanes(s), SUB)
                ubuf[:, pl.ds(pl.multiple_of(SUB * g, SUB), SUB)] = turn(turned[...])

        @pl.when(s + 1 < NB)
        def _():
            each(gather.pass_on, s + 1)

        @pl.when(s + 2 < NB)
        def _():
            each(gather.give, s + 2)

        @pl.loop(0, PER)
        def _(i):
            n = s * PER + i
            for copy in loads(n):
                copy.wait()

            @pl.when(n + 1 < NB * PER)
            def _():
                for copy in loads(n + 1):
                    copy.start()

            @pl.when(n > 1)
            def _():
                for copy in stores(n - 2):
                    copy.wait()

            orders = [ubuf.at[pl.ds(pl.multiple_of(i * BT + SUB * k, SUB), SUB)] for k in range(BT // SUB)]
            grid_stage(
                n, orders, xbuf.at[n % 2], tgtbuf.at[n % 2], q_ref, (g_ref, gt_ref, w1_ref, w2t_ref),
                dbuf.at[n % 2], zbuf.at[n % 2], grads_ref, (line, yb, hid, act, db, dh),
            )
            for copy in stores(n):
                copy.start()

            @pl.when((i == 1) & (s + 1 < NB))
            def _():
                each(gather.collect, s + 1)

    for n in range(2):
        for copy in stores(NB * PER - 2 + n):
            copy.wait()

    @pl.loop(0, NB)
    def _(s):
        each(gather.finish, s)

    for g in range(LATE):
        give_q(g).wait_send()
        store_low(g).wait()


def forward(table, own, x, target, q, base, w1, w2t, cid):
    hid = 2 * CH
    grid, two = (2, CH, BT, NN), BT // SUB
    return call(
        forward_kernel,
        [(NB, NT, CH, NN), (NT, NM, LANES), (LATE, *HALF_TABLE[1:]), (CH, LANES)],
        [
            vmem(GROUPS, SUB, NT, NL), vmem(NT, NM, LN), vmem(SUB, NT, LN), vmem(*SLOTS, ROWS + SPARE, LANES),
            vmem(*grid), vmem(*grid), vmem(2, BT, CH, NN), vmem(2, BT, NM, LN), vmem(NN, NN), vmem(NN, NN),
            vmem(two, CH, WIDE), vmem(two, CH, WIDE, dtype=BF16), vmem(two, hid, WIDE), vmem(two, hid, WIDE, dtype=BF16),
            vmem(two, CH, WIDE, dtype=BF16), vmem(two, hid, WIDE, dtype=BF16),
            dma_sems(GROUPS), dma_sems(2, 2), dma_sems(2, 2), dma_sems(2, LATE), dma_sems(LATE),
        ] + [dma_sems(2, 2 * NB)] * 8,
        cid=cid,
        in_specs=[ANY, ANY, VMEM, ANY, ANY, SMEM, VMEM, VMEM, VMEM],
        out_specs=(ANY, ANY, ANY, VMEM),
        name="forward",
    )(*table, own, x, target, q, base, w1, w2t)


def blocks(nt):
    return (
        pl.BlockSpec((1, CH, nt, NN), lambda b, t: (b, 0, t, 0)),
        pl.BlockSpec((1, nt, CH, NN), lambda b, t: (b, t, 0, 0)),
        pl.BlockSpec((nt, NM, LN), lambda b, t: (t, 0, b)),
    )


CHAN_SPEC = pl.BlockSpec((CH, LN), lambda b, t: (b, 0))
FINAL_T = 4 * SUB

def whole(*shape):
    return pl.BlockSpec(shape, lambda b, t: (0,) * len(shape))


def first_step():
    return (pl.program_id(0) == 0) & (pl.program_id(1) == 0)


def final_kernel(u_ref, x_ref, dout_ref, mu_ref, inv_ref, ext_ref, spec_ref, base_ref, out_ref, gspec_ref, gw1_ref, gw2t_ref, loss_ref,
                 g_ref, s0_ref, s1_ref):
    @pl.when(first_step())
    def _():
        g_ref[...] = signed(base_ref[...], Place().y, 1).T
        gspec_ref[0] = spec_ref[:, :, :CH]
        gspec_ref[1] = spec_ref[:, :, CH:]
        grads = ext_ref[:, SUB:].reshape(CH, LANES)
        gw1_ref[...] = grads[:, :LN]
        gw2t_ref[...] = grads[:, LN:2 * LN]
        loss = block_sum(grads[None, :SUB, 2 * LN:])[0] / TOTAL
        loss_ref[...] = loss
        sums = sum(ext_ref[n, :SUB] for n in range(PLANE)) / POINTS
        for b in range(NB):
            chans, lanes = slice(CH * b, CH * (b + 1)), slice(LN * b, LN * (b + 1))
            s0, s1 = (jnp.broadcast_to(sums[n:n + 1, lanes], (LN, LN)).T for n in range(2))
            s0_ref[chans] = s0[:CH]
            s1_ref[chans] = s1[:CH] + s1[CH:]

    chans = pl.ds(pl.multiple_of(pl.program_id(0) * CH, CH), CH)
    inv = inv_ref[:, :1]
    slope = inv_ref[...] * inv_ref[...] * s1_ref[chans]

    @pl.loop(0, FINAL_T // SUB)
    def _(k):
        ts = pl.ds(pl.multiple_of(SUB * k, SUB), SUB)
        dn = to_grid(u_ref[ts], g_ref[...]).reshape(SUB, CH, NN)
        r = turn(dout_ref[0, ts] + inv * (dn - s0_ref[chans, :1]))
        for c in range(CH):
            for n in range(NN // LN):
                lanes = slice(LN * n, LN * (n + 1))
                out_ref[0, c, ts, lanes] = r[c, :, lanes] - (x_ref[0, c, ts, lanes] - mu_ref[c:c + 1]) * slope[c:c + 1]


def final(u, x, dout, mu, inv, ext, spec, base):
    hid = 2 * CH
    degrees = NL // 4
    grid, lines, orders = blocks(FINAL_T)
    return call(
        final_kernel,
        [(NB, CH, NT, NN), (2, degrees, CH, CH), (CH, hid), (CH, hid), (1, 1)],
        [vmem(NN, NN), vmem(NB * CH, LN), vmem(NB * CH, LN)],
        grid=(NB, NT // FINAL_T),
        in_specs=[
            orders, grid, lines, CHAN_SPEC, CHAN_SPEC,
            whole(PLANE, 2 * SUB, LANES), whole(degrees, CH, LN), whole(NN, NN),
        ],
        out_specs=(grid, whole(2, degrees, CH, CH), whole(CH, hid), whole(CH, hid), whole(1, 1)),
        name="final",
    )(u, x, dout, mu, inv, ext, spec.reshape(degrees, CH, LN), base)


def solution(mesh):
    def local_step(x, target, q, leg_fwd, leg_inv, spec_w, w1, w2):
        base = jnp.asarray(dft_matrix())
        p_own, q_own = (jnp.swapaxes(v, 1, 2).reshape(HALF_TABLE) for v in (leg_fwd, leg_inv))
        z, p_peer, mu, inv, c0, kern = front(x, p_own, jnp.moveaxis(spec_w, 1, 3), base, 0)
        a, b, q_high = analyze((p_own, p_peer), z, 1, kern, q_own=q_own)
        dout, dz, q_low, grads = forward((q_own, q_high), b, x, target, q, base, w1, w2.T, 2)
        da, dk = analyze((q_own, q_low, q_high), dz, 3, kern, back=(grads, a, c0))
        du, ext, spec = synth((p_own, p_peer), da, 4, dk)
        d_field, grad_spec, gw1, gw2t, loss = final(du, x, dout, mu, inv, ext, spec, base)
        return loss.reshape(()), d_field, grad_spec, gw1, gw2t.T

    grid_spec = P("dp", None, "h", "w")
    table_spec = P("w", None, "h")
    return jax.shard_map(
        local_step,
        mesh=mesh,
        in_specs=(grid_spec, grid_spec, P("h"), table_spec, table_spec, P(), P(), P()),
        out_specs=(P(), grid_spec, P(None, "h", None, None), P(), P()),
        check_vma=False,
    )
```

time: 474 us -> 449 us (0.947)
  Pallas kernels: 473 us -> 448 us
    pallas_call x3 -> x2, Pallas kernels: 230 us -> 198 us  [the longest x1 121 us: forward(): call(forward_kernel, [(NB, NT, CH, NN), (NT, NM, LANES), (LATE, *HALF_TAB...]
    pallas_call x2, Pallas kernels: 164 us -> 171 us  [analyze(): call(lambda *refs: analyze_kernel(share, with_q, *refs), outs, [degrees,...]
where the time goes in v3:
time: 449 us; the launch traced here: 448 us
  Pallas kernels  448 us (100%)
    pallas_call x2, Pallas kernels, analyze(): call(lambda *refs: analyze_kernel(share, with_q, *refs), outs, [degrees,...  171 us
    pallas_call x1, Pallas kernels, forward(): call(forward_kernel, [(NB, NT, CH, NN), (NT, NM, LANES), (LATE, *HALF_TAB...  121 us
    pallas_call x1, Pallas kernels, synth(): call(synth_kernel, [(NT, NM, LANES), (PLANE, 2 * SUB, LANES), (4, SUB, CH...  77.2 us
    pallas_call x1, Pallas kernels, front(): call(front_kernel, [(NT, NM, LANES), HALF_TABLE, (NB * CH, LN), (NB * CH,...  52.9 us
    pallas_call x1, Pallas kernels, final(): call(final_kernel, [(NB, CH, NT, NN), (2, degrees, CH, CH), (CH, hid), (C...  26 us

profile of v3, /device:TPU:1, one launch (start us, length us, event | category | flops | bytes accessed | tf_op | source)
XLA Modules:
  0.0 448.4 jit_solution(15785114701828770705)
XLA Ops:
  0.6 52.9 %front.1 = (f32[64,128,384]{2,1,0:T(8,128)}, f32[8,8,64,128]{3,2,1,0:T(8,128)}, f32[192,128]{1,0:T(8,128)}, f32[192,128]{1,0:T(8,128)}, f32[16,128]{1,0:T(8,128)}, /*index=5*/f32[16,128,128]{2,1,0:T(8,128)}) custom-call(f32[3,64,64,256]{3,2,1,0:T(8,128)} %x_ref.1, f32[8,8,64,128]{3,2,1,0:T(8,128)} %bitcast.14, f32[2,64,64,128]{3,2,1,0:T(8,128)} %bitcast.17, ...), custom_call_target="tpu_custom_call" | custom-call | tf_op jit(solution)/shard_map/front/pallas_call | solution.py:299
  53.5 95.7 %analyze_1.1 = (f32[1104,384]{1,0:T(8,128)}, f32[1104,384]{1,0:T(8,128)}, f32[6,8,64,128]{3,2,1,0:T(8,128)}) custom-call(f32[8,8,64,128]{3,2,1,0:T(8,128)} %bitcast.15, f32[8,8,64,128]{3,2,1,0:T(8,128)} %get-tuple-element.28.refs_1_.t_peer, f32[64,128,384]{2,1,0:T(8,128)} %get-tuple-element.29.refs_2_, f32[8,8,64,128]{3,2,1,0:T(8,128)} %bitcast.11, ...), custom_call_target="tpu_custom_call" | custom-call | tf_op jit(solution)/shard_map/analyze_1/pallas_call | solution.py:574
  149.3 120.8 %forward.1 = (f32[3,64,64,256]{3,2,1,0:T(8,128)}, f32[64,128,384]{2,1,0:T(8,128)}, f32[2,8,64,128]{3,2,1,0:T(8,128)}, f32[64,384]{1,0:T(8,128)}) custom-call(f32[8,8,64,128]{3,2,1,0:T(8,128)} %bitcast.12, f32[6,8,64,128]{3,2,1,0:T(8,128)} %get-tuple-element.31.t_high.refs_2_, f32[1104,384]{1,0:T(8,128)} %get-tuple-element.32.own_ref, ...), custom_call_target="tpu_custom_call" | custom-call | tf_op jit(solution)/shard_map/forward/pallas_call | solution.py:989
  270.1 74.8 %analyze_3.1 = (f32[1104,384]{1,0:T(8,128)}, f32[2,8,64,128]{3,2,1,0:T(8,128)}) custom-call(f32[8,8,64,128]{3,2,1,0:T(8,128)} %bitcast.13, f32[2,8,64,128]{3,2,1,0:T(8,128)} %get-tuple-element.33.refs_1_, f32[6,8,64,128]{3,2,1,0:T(8,128)} %get-tuple-element.31.t_high.refs_2_, f32[64,128,384]{2,1,0:T(8,128)} %get-tuple-element.34.refs_3_, ...), custom_call_target="tpu_custom_call" | custom-call | tf_op jit(solution)/shard_map/analyze_3/pallas_call | solution.py:574
  345.0 77.2 %synth_4.1 = (f32[64,128,384]{2,1,0:T(8,128)}, f32[8,16,384]{2,1,0:T(8,128)}, f32[4,8,64,128]{3,2,1,0:T(8,128)}) custom-call(f32[8,8,64,128]{3,2,1,0:T(8,128)} %bitcast.16, f32[8,8,64,128]{3,2,1,0:T(8,128)} %get-tuple-element.28.refs_1_.t_peer, f32[1104,384]{1,0:T(8,128)} %get-tuple-element.38.own_ref, f32[2,8,64,128]{3,2,1,0:T(8,128)} %get-tuple-element.39.dk_ref), custom_call_target="tpu_custom_call" | custom-call | tf_op jit(solution)/shard_map/synth_4/pallas_call | solution.py:784
  422.2 26.0 %final.1 = (f32[3,64,64,256]{3,2,1,0:T(8,128)}, f32[2,32,64,64]{3,2,1,0:T(8,128)}, f32[64,128]{1,0:T(8,128)}, f32[64,128]{1,0:T(8,128)}, f32[1,1]{1,0:T(1,128)}) custom-call(f32[64,128,384]{2,1,0:T(8,128)} %get-tuple-element.40.u_ref, f32[3,64,64,256]{3,2,1,0:T(8,128)} %x_ref.1, f32[3,64,64,256]{3,2,1,0:T(8,128)} %get-tuple-element.41.dout_ref, ...), custom_call_target="tpu_custom_call" | custom-call | tf_op jit(solution)/shard_map/final/pallas_call | solution.py:1063

commit v4 on v3

--- a/solution.py
+++ b/solution.py
@@ -18,6 +18,9 @@
 ROW, COL = 0, 1
 NB, CH, NT, NN = 3, 64, 64, 256
 NM, NL = 128, 128
+DFT_STEP = 16
+BUFFERS = 2
+HALF = 0.5
 LON, LAT, BATCH = 512, 256, 12
 POINTS = LON * LAT
 TOTAL = POINTS * BATCH * CH
@@ -25,7 +28,8 @@
 SUB, LN = 8, 128
 T8 = NT // SUB
 GROUPS = NM // SUB
-PLANE = 8
+PLANE, Z = 8, 4
+PAIRS = SUB // 2
 H_OF_PAIR = (0, 0, 3, 3, 1, 1, 2, 2)
 BLOCK = SUB * SUB
 PLACES = GROUPS + 1
@@ -42,7 +46,7 @@
 NN_DIMS, NT_DIMS, TN_DIMS = ((1,), (0,)), ((1,), (1,)), ((0,), (0,))
 SUM_ENDS = (2, 5, 8, 11, 14, 16, 17)
 GATHER_ENDS = (3, 6, 9, 12, 15, 17)
-MIX_AFTER = (2, 3, 4, 6)
+MIX_AFTER = (1, 3, 4, 5, 6), (2, 4, 6)
 
 SMEM = pl.BlockSpec(memory_space=pltpu.SMEM)
 VMEM = pl.BlockSpec(memory_space=pltpu.VMEM)
@@ -84,6 +88,10 @@
     return jnp.sum(jnp.sum(v, axis=COL, keepdims=True), axis=COL + 1, keepdims=True)
 
 
+def col(v):
+    return v[:, :1]
+
+
 def turn(v):
     return jnp.swapaxes(v, ROW, COL)
 
@@ -92,14 +100,22 @@
     return pl.ds(lo, hi - lo)
 
 
-def dft_matrix():
-    theta = 2.0 * np.pi * ((np.arange(NN)[:, None] * np.arange(NM)[None, :]) % LON) / LON
-    return (np.concatenate([np.cos(theta), -np.sin(theta)], axis=COL) / math.sqrt(LON)).astype(np.float32)
-
-
-def signed(base, half, weight):
-    m = lax.broadcasted_iota(jnp.int32, base.shape, 1) % NM
-    out = jnp.where((m % 2) * half == 1, -base, base)
+def dft_tables():
+    small = np.arange(DFT_STEP)[:, None] * np.arange(NM)[None]
+    coarse, fine = (np.exp(-2j * np.pi * (v % LON) / LON) for v in (DFT_STEP * small, small))
+    coarse = coarse / math.sqrt(LON)
+    return np.stack([coarse.real, coarse.imag, fine.real, fine.imag]).astype(np.float32)
+
+
+def signed(tables, half, weight):
+    fine_re, fine_im = tables[2], tables[3]
+    lines = []
+    for n in range(DFT_STEP):
+        re, im = tables[0, n:n + 1], tables[1, n:n + 1]
+        lines.append(jnp.concatenate([re * fine_re - im * fine_im, re * fine_im + im * fine_re], axis=COL))
+    out = jnp.concatenate(lines, axis=ROW)
+    m = lax.broadcasted_iota(jnp.int32, out.shape, 1) % NM
+    out = jnp.where((m % 2) * half == 1, -out, out)
     return jnp.where(m == 0, out, weight * out) if weight > 1 else out
 
 
@@ -136,7 +152,7 @@
 def chunk(i, share, ends):
     lo = start_of(i, ends) * BLOCK
     hi = ends[i] * BLOCK if ends[i] < PLACES else ROWS
-    return lo, lo + (hi - lo) * share // BLOCK * SUB, hi
+    return lo, lo + (hi - lo) * share // (2 * BLOCK) * SUB, hi
 
 
 class Place:
@@ -170,15 +186,16 @@
 
 CB = 16
 PIECES = CH // CB
-HALF_TABLE = (SUB, SUB, NT, NL)
+RAW_TABLE = (SUB, SUB, NT, NL)
+HALF_TABLE = (SUB, PAIRS, NL, LN)
 
 
 def near_far(k):
     return pl.ds(pl.multiple_of(SUB * k, SUB), SUB), pl.ds(pl.multiple_of(SUB * (GROUPS - 1 - k), SUB), SUB)
 
 
-def front_kernel(x_hbm, p_hbm, w_hbm, base_ref, z_hbm, p_peer, mu_ref, inv_ref, c0_ref, kern_ref,
-                 xbuf, wbuf, pbuf, cols, pay, sbuf, zbuf, ftbuf, turned, own, s_x, s_w, s_z, s_p, s_st):
+def front_kernel(x_hbm, p_hbm, q_hbm, w_hbm, base_ref, z_hbm, p_own, p_peer, q_own, mu_ref, inv_ref, c0_ref, kern_ref,
+                 xbuf, wbuf, pbuf, qbuf, ppack, qpack, zeros, cols, pay, sbuf, zbuf, ftbuf, turned, own, s_x, s_w, s_z, s_p, s_q, s_st):
     place = Place()
     near, far = near_far(place.pair)
 
@@ -192,8 +209,24 @@
     def load_p(g):
         return pltpu.make_async_copy(p_hbm.at[g], pbuf.at[g], s_p.at[2, g])
 
+    def load_q(g):
+        return pltpu.make_async_copy(q_hbm.at[g], qbuf.at[g], s_q.at[0, g])
+
+    def store_p(g):
+        return pltpu.make_async_copy(ppack.at[g], p_own.at[g], s_q.at[1, g])
+
+    def store_q(g):
+        return pltpu.make_async_copy(qpack.at[g], q_own.at[g], s_q.at[2, g])
+
     def give_p(g):
-        return send(pbuf.at[g], p_peer.at[g], s_p, g, place.yn)
+        return send(ppack.at[g, :, used(g)], p_peer.at[g, :, used(g)], s_p, g, place.yn)
+
+    def clear_p(g):
+        return pltpu.make_async_copy(zeros.at[:, unused(g)], p_peer.at[g, :, unused(g)], s_q.at[3, g])
+
+    def pack(src, dst, g):
+        for i in range(PAIRS):
+            dst[g, i] = jnp.concatenate([src[g, 2 * i + n] for n in range(2)], axis=ROW).T
 
     @pl.loop(0, SUB)
     def _(g):
@@ -205,13 +238,26 @@
 
     for i in range(2):
         load_w(i).start()
+
+    @pl.loop(0, SUB)
+    def _(g):
+        load_q(g).start()
+
     others = range(1, PLANE)
     place.greet([place.plane(r) for r in others])
+
+    zeros[...] = jnp.zeros_like(zeros)
+    for g in range(1, SUB):
+        clear_p(g).start()
 
     def offer(lo, hi):
         @pl.loop(lo, hi)
         def _(g):
             load_p(g).wait()
+            pack(pbuf, ppack, g)
+            store_p(g).start()
+
+        for g in range(lo, hi):
             give_p(g).start()
 
     offer(0, 1)
@@ -239,7 +285,13 @@
         give_stats(r).start()
     offer(1, SUB)
     sbuf[place.slot] = pay[...]
-    ftbuf[...] = signed(base_ref[...], place.y, 1)
+    ftbuf[...] = signed(base_ref, place.y, 1)
+
+    @pl.loop(0, SUB)
+    def _(g):
+        load_q(g).wait()
+        pack(qbuf, qpack, g)
+        store_q(g).start()
 
     for i in range(2):
         load_w(i).wait()
@@ -270,45 +322,60 @@
     def store_z(n):
         t = pl.multiple_of(n % T8 * SUB, SUB)
         lanes = pl.multiple_of(n // T8 * LN, LN)
-        return pltpu.make_async_copy(zbuf.at[n % 2], z_hbm.at[pl.ds(t, SUB), :, pl.ds(lanes, LN)], s_z.at[n % 2])
+        return pltpu.make_async_copy(zbuf.at[n % BUFFERS], z_hbm.at[pl.ds(t, SUB), :, pl.ds(lanes, LN)], s_z.at[n % BUFFERS])
 
     @pl.loop(0, NB * T8)
     def _(n):
-        @pl.when(n >= 2)
+        @pl.when(n >= BUFFERS)
         def _():
-            store_z(n - 2).wait()
+            store_z(n - BUFFERS).wait()
 
         b = n // T8
         xt = turn(xbuf[b, :, pl.ds(pl.multiple_of(n % T8 * SUB, SUB), SUB), :])
         chans = pl.ds(pl.multiple_of(b * CH, CH), CH)
-        xn = (xt - mu_ref[chans, :1]) * inv_ref[chans, :1]
-        zbuf[n % 2] = to_orders(xn.reshape(SUB * CH, NN), ftbuf[...])
+        xn = (xt - col(mu_ref[chans])) * col(inv_ref[chans])
+        zbuf[n % BUFFERS] = to_orders(xn.reshape(SUB * CH, NN), ftbuf[...])
         store_z(n).start()
 
-    for n in range(2):
-        store_z(NB * T8 - 2 + n).wait()
+    for n in range(BUFFERS):
+        store_z(NB * T8 - BUFFERS + n).wait()
     for r in others:
         give_stats(r).wait_send()
 
     @pl.loop(0, SUB)
     def _(g):
+        store_p(g).wait()
+        store_q(g).wait()
+
+    for g in range(SUB):
         give_p(g).wait()
-
-
-def front(x, p_own, spec_w, base, cid):
+        if g > 0:
+            clear_p(g).wait()
+
+
+def used(g):
+    return rows(SUB * g, NL)
+
+
+def unused(g):
+    return rows(0, SUB * g)
+
+
+def front(x, p_raw, q_raw, spec_w, base, cid):
     return call(
         front_kernel,
-        [(NT, NM, LANES), HALF_TABLE, (NB * CH, LN), (NB * CH, LN), (2 * SUB, LN), (2 * SUB, LN, LN)],
+        [(NT, NM, LANES), HALF_TABLE, HALF_TABLE, HALF_TABLE, (NB * CH, LN), (NB * CH, LN), (2 * SUB, LN), (2 * SUB, LN, LN)],
         [
-            vmem(NB, CH, NT, NN), vmem(2, CH, CH, NL), vmem(*HALF_TABLE), vmem(NN, LN), vmem(SUB, NN), vmem(PLANE, SUB, NN),
-            vmem(2, SUB, NM, LN), vmem(NN, NN), vmem(NL, LN), vmem(CH, 2 * SUB, LN),
-            dma_sems(NB * PIECES), dma_sems(2), dma_sems(2), dma_sems(3, SUB), dma_sems(2, PLANE),
+            vmem(NB, CH, NT, NN), vmem(2, CH, CH, NL), vmem(*RAW_TABLE), vmem(*RAW_TABLE), vmem(*HALF_TABLE), vmem(*HALF_TABLE),
+            vmem(PAIRS, CH, LN), vmem(NN, LN), vmem(SUB, NN), vmem(PLANE, SUB, NN),
+            vmem(BUFFERS, SUB, NM, LN), vmem(NN, NN), vmem(NL, LN), vmem(CH, 2 * SUB, LN),
+            dma_sems(NB * PIECES), dma_sems(2), dma_sems(2), dma_sems(3, SUB), dma_sems(4, SUB), dma_sems(2, PLANE),
         ],
         cid=cid,
-        in_specs=[ANY, ANY, ANY, VMEM],
-        out_specs=(ANY, ANY, VMEM, VMEM, VMEM, VMEM),
+        in_specs=[ANY, ANY, ANY, ANY, VMEM],
+        out_specs=(ANY, ANY, ANY, ANY, VMEM, VMEM, VMEM, VMEM),
         name="front",
-    )(x, p_own, spec_w, base)
+    )(x, p_raw, q_raw, spec_w, base)
 
 
 def table_loader(own, peers, tbuf, sems, y):
@@ -368,7 +435,7 @@
     by_degree(a, rows_in)
     near = near_mask(first, count, pair)
 
-    @pl.loop(0, SUB, unroll=UNROLL)
+    @pl.loop(0, SUB)
     def _(l):
         al = a[l, :n]
         b[l, :n] = jnp.where(near, dot(al, kern_ref[l]), dot(al, kern_ref[SUB + l]))
@@ -404,7 +471,7 @@
 
 def analyze_kernel(share, with_q, *refs):
     if with_q:
-        t_own, t_peer, z_hbm, q_own, kern_ref, out_ref, mix_ref, q_peer, a_deg, b_deg, qbuf, *rest = refs
+        t_own, t_peer, z_hbm, q_own, kern_ref, out_ref, mix_ref, q_peer, a_deg, b_deg, qbuf, zeros, s_clear, *rest = refs
         peers = [(t_peer, SUB)]
     else:
         t_own, t_low, t_high, z_hbm, ext_ref, kern_ref, a_ref, c0_ref, mix_ref, dk_ref, a_deg, b_deg, out_ref, s_ref, da_deg, *rest = refs
@@ -413,6 +480,7 @@
         s_ref[...] = jnp.zeros_like(s_ref)
     tbuf, zbuf, turned, part, sib, rx, ry, fx, fy, s_t, s_z, s_q, s_sib, s_x, s_y, s_fx, s_fy = rest
     count = len(SUM_ENDS)
+    mix_after = MIX_AFTER[0 if with_q else 1]
     p = Place()
     x, c, y = p.x, p.c, p.y
     start_t, wait_t = table_loader(t_own, peers, tbuf, s_t, y)
@@ -436,7 +504,12 @@
         return pltpu.make_async_copy(q_own.at[LATE + g], qbuf.at[g], s_q.at[2, g])
 
     def give_q(g):
-        return send(qbuf.at[g], q_peer.at[g], s_q, g, p.yn)
+        at = used(LATE + g)
+        return send(qbuf.at[g, :, at], q_peer.at[g, :, at], s_q, g, p.yn)
+
+    def clear_q(g):
+        at = unused(LATE + g)
+        return pltpu.make_async_copy(zeros.at[:, at], q_peer.at[g, :, at], s_clear.at[g])
 
     def compute(lo, hi, k):
         @pl.loop(lo, hi)
@@ -450,8 +523,8 @@
             @pl.loop(0, SUB, step=at_once)
             def _(some):
                 for m in range(at_once):
-                    m = some + m
-                    r = dot(tbuf[g, m].T[4 * SUB * k:], turned[m])
+                    odd, m = m % 2, some + m
+                    r = dot(tbuf[g, m // 2][4 * SUB * k:, NT * odd:NT * (odd + 1)], turned[m])
                     for n in range(GROUPS - 4 * k):
                         j = 4 * k + n
                         row = sum_position(j, g) * BLOCK + SUB * m
@@ -496,23 +569,33 @@
         if with_q and i < EARLY:
             give_q(i).start()
 
+    def add(lo, hi, *sums):
+        @pl.loop(lo, hi, step=SUB)
+        def _(row):
+            some = pl.ds(pl.multiple_of(row, SUB), SUB)
+            for to, a, b in sums:
+                to[some] = a[some] + b[some]
+
     def half_sum(i):
         lo, mid, hi = chunk(i, share, SUM_ENDS)
         to_x(i).wait_recv()
-        part[x, c, p.oy, rows(lo, mid)] += rx[p.oy, rows(lo, mid)]
+        other = part.at[x, c, p.oy]
+        add(lo, mid, (other, other, rx.at[p.oy]))
         forward_y(i).start()
         to_y(i).wait_recv()
-        part[p.ox, c, y, rows(mid, hi)] += ry[p.ox, rows(mid, hi)]
+        other = part.at[p.ox, c, y]
+        add(mid, hi, (other, other, ry.at[p.ox]))
         forward_x(i).start()
-        out_ref[rows(lo, mid)] = part[x, c, y, rows(lo, mid)] + rx[y, rows(lo, mid)]
-        out_ref[rows(mid, hi)] = part[x, c, y, rows(mid, hi)] + ry[x, rows(mid, hi)]
+        mine = part.at[x, c, y]
+        add(lo, mid, (out_ref, mine, rx.at[y]))
+        add(mid, hi, (out_ref, mine, ry.at[x]))
 
     def last_sum(i):
         lo, mid, hi = chunk(i, share, SUM_ENDS)
         forward_y(i).wait_recv()
-        out_ref[rows(lo, mid)] += fy[rows(lo, mid)]
+        add(lo, mid, (out_ref, out_ref, fy))
         forward_x(i).wait_recv()
-        out_ref[rows(mid, hi)] += fx[rows(mid, hi)]
+        add(mid, hi, (out_ref, out_ref, fx))
 
     def mixed(first, end):
         places = end - first
@@ -522,8 +605,10 @@
             mix_back_places(first, places, p.pair, a_ref, out_ref, kern_ref, c0_ref, mix_ref, dk_ref, s_ref, a_deg, b_deg, da_deg)
 
     if with_q:
+        zeros[...] = jnp.zeros_like(zeros)
         for g in range(EARLY):
             load_q(g).start()
+            clear_q(g).start()
         for g in range(EARLY):
             load_q(g).wait()
     for i in range(count + LAST_LAG):
@@ -537,9 +622,9 @@
             half_sum(i - HALF_LAG)
         if i >= LAST_LAG:
             last_sum(i - LAST_LAG)
-            if i - LAST_LAG in MIX_AFTER:
-                n = MIX_AFTER.index(i - LAST_LAG)
-                mixed(SUM_ENDS[MIX_AFTER[n - 1]] if n > 0 else 0, SUM_ENDS[MIX_AFTER[n]])
+            if i - LAST_LAG in mix_after:
+                n = mix_after.index(i - LAST_LAG)
+                mixed(start_of(n, [SUM_ENDS[m] for m in mix_after]), SUM_ENDS[i - LAST_LAG])
     if with_q:
         mix_ref[STAT:] = jnp.zeros((ROWS - STAT, LANES), F32)
     else:
@@ -551,6 +636,7 @@
     if with_q:
         for g in range(EARLY):
             give_q(g).wait()
+            clear_q(g).wait()
 
 
 HALF_LAG, LAST_LAG = 2, 4
@@ -559,14 +645,14 @@
 
 def analyze(table, z, cid, kern, q_own=None, back=()):
     with_q = q_own is not None
-    share = 7 if with_q else 4
+    share = 13 if with_q else 8
     piece = (EARLY, *HALF_TABLE[1:])
     half = vmem(ROWS, LANES)
     pair = vmem(2, ROWS, LANES)
     degrees = vmem(SUB, NB * MOST * SUB, LN)
     if with_q:
         ins, places, outs = (q_own, kern), [ANY, VMEM], [(ROWS, LANES), (ROWS, LANES), piece]
-        out_places, more = (VMEM, VMEM, ANY), [vmem(*piece)]
+        out_places, more = (VMEM, VMEM, ANY), [vmem(*piece), vmem(PAIRS, CH, LN), dma_sems(EARLY)]
     else:
         ext, a, c0 = back
         ins, places, outs = (ext, kern, a, c0), [VMEM] * 4, [(ROWS, LANES), (2, SUB, CH, LN)]
@@ -575,7 +661,7 @@
         lambda *refs: analyze_kernel(share, with_q, *refs),
         outs,
         [degrees, degrees] + more + [
-            vmem(GROUPS, SUB, NT, NL), vmem(GROUPS, NT, SUB, LANES), vmem(SUB, NT, LANES), vmem(*SLOTS, ROWS + SPARE, LANES),
+            vmem(GROUPS, *HALF_TABLE[1:]), vmem(GROUPS, NT, SUB, LANES), vmem(SUB, NT, LANES), vmem(*SLOTS, ROWS + SPARE, LANES),
             vmem(*SLOTS[1:], ROWS, LANES), pair, pair, half, half,
             dma_sems(GROUPS), dma_sems(GROUPS), dma_sems(3, EARLY),
         ] + [dma_sems(2, len(SUM_ENDS))] * 5,
@@ -652,11 +738,13 @@
             copy(piece).wait_send()
 
 
-def inverse_sums(tbuf, ball, turned, g, k, lanes, at_once):
+def inverse_sums(table, ball, turned, g, k, lanes, at_once):
     @pl.loop(0, SUB, step=at_once)
     def _(some):
         for m in range(at_once):
-            m = some + m
+            odd, m = m % 2, some + m
+            if not odd:
+                both = table(g, m // 2)
             tiles = []
             for n in range(GROUPS - 4 * k):
                 j = 4 * k + n
@@ -665,7 +753,7 @@
                     row = jnp.where(j >= g, row, ROWS)
                 xj, cj, yj = place_of_block(j)
                 tiles.append(ball[xj, cj, yj, pl.ds(pl.multiple_of(row, SUB), SUB), lanes])
-            turned[m] = dot(tbuf[g, m][:, 4 * SUB * k:], jnp.concatenate(tiles, axis=ROW))
+            turned[m] = dot(both[NT * odd:NT * (odd + 1), 4 * SUB * k:], jnp.concatenate(tiles, axis=ROW))
 
 
 ALL = pl.ds(0, LANES)
@@ -685,15 +773,16 @@
     def _(g):
         start_t(g)
 
-    above = [{"dp": (p.z + r) % 4} for r in range(1, 4)]
+    above = [{"dp": (p.z + r) % Z} for r in range(1, Z)]
     partner = [{"h": 3 - p.h}, {"h": 3 - p.h, "w": p.oy}]
     p.greet([p.sibling, p.xn, p.yn, *above, *partner])
 
+    others = range(Z - 1)
     early = Gather(p, own_ref, ball, sems)
     late = Gather(p, ball.at[x, c, y], ball, sems)
 
     def piece(i):
-        return i, *chunk(i, 4, GATHER_ENDS), ALL
+        return i, *chunk(i, SUB, GATHER_ENDS), ALL
 
     def gather(i):
         return late if i == count - 1 else early
@@ -704,7 +793,7 @@
         return send(own_ref.at[GRAD:ROWS], zg.at[r], s_zg, r, above[r])
 
     def dk_z(r):
-        return send(dk_ref.at[:, pl.ds(2 * ((p.z + 1 + r) % 4), 2)], zin.at[r], s_zk, r, above[r])
+        return send(dk_ref.at[:, pl.ds(2 * ((p.z + 1 + r) % Z), 2)], zin.at[r], s_zk, r, above[r])
 
     stay = jnp.where(p.low, 0, 1)
     kept = jnp.where(p.low, p.pair, GROUPS - 1 - p.pair) % 4
@@ -723,11 +812,11 @@
         def _(n):
             g = hi - 1 - n
             wait_t(g)
-            inverse_sums(tbuf, ball, turned, g, k, ALL, AT_ONCE)
+            inverse_sums(lambda g, i: tbuf[g, i].T, ball, turned, g, k, ALL, SUB if k > 0 else AT_ONCE)
             ubuf[g] = turn(turned[...])
             store_u(g).start()
 
-    for r in range(3):
+    for r in others:
         grads_z(r).start()
         dk_z(r).start()
     for i in range(2):
@@ -739,20 +828,20 @@
         if i < count:
             gather(i).pass_on(piece(i))
         if i == 1:
-            for r in range(3):
+            for r in others:
                 grads_z(r).wait_recv()
                 ball[x, c, y, GRAD:ROWS] += zg[r]
         if i == 2:
-            for r in range(3):
+            for r in others:
                 dk_z(r).wait_recv()
             kin[...] = dk_ref[:, quarter] + zin[0] + zin[1] + zin[2]
-            for r in range(3):
+            for r in others:
                 dk_plane(r).start()
             spec_ref[kept, quarter] = kin[stay]
         if i == 3:
-            for r in range(3):
+            for r in others:
                 dk_plane(r).wait_recv()
-            for r in range(3):
+            for r in others:
                 dk_up(r).start()
         if i < count - 2:
             gather(i + 2).give(piece(i + 2))
@@ -768,7 +857,7 @@
         ext_ref[d] = ball[*slot_index(d), STAT:ROWS]
     for i in range(count):
         gather(i).finish(piece(i))
-    for r in range(3):
+    for r in others:
         grads_z(r).wait_send()
         dk_z(r).wait_send()
         dk_plane(r).wait_send()
@@ -785,7 +874,7 @@
         synth_kernel,
         [(NT, NM, LANES), (PLANE, 2 * SUB, LANES), (4, SUB, CH, LN)],
         [
-            vmem(GROUPS, SUB, NT, NL), vmem(GROUPS, NT, SUB, LANES), vmem(SUB, NT, LANES), vmem(*SLOTS, ROWS + SPARE, LANES),
+            vmem(GROUPS, *HALF_TABLE[1:]), vmem(GROUPS, NT, SUB, LANES), vmem(SUB, NT, LANES), vmem(*SLOTS, ROWS + SPARE, LANES),
             vmem(NB, *quarter), vmem(*quarter), vmem(NB, SUB, LANES), dma_sems(GROUPS), dma_sems(GROUPS),
         ] + [dma_sems(2, NB)] * 4 + [dma_sems(2, len(GATHER_ENDS))] * 8,
         cid=cid,
@@ -824,9 +913,9 @@
             h = hid[k][:, columns(t)]
             h2 = h * h
             th = jnp.tanh(h * (GELU_A + (GELU_A * GELU_B) * h2))
-            cdf = 0.5 + 0.5 * th
+            cdf = HALF + HALF * th
             act[k][:, columns(t)] = (h * cdf).astype(BF16)
-            hid[k][:, columns(t)] = cdf + (0.5 * h) * (1.0 - th * th) * (GELU_A + (3.0 * GELU_A * GELU_B) * h2)
+            hid[k][:, columns(t)] = cdf + (HALF * h) * (1.0 - th * th) * (GELU_A + (3.0 * GELU_A * GELU_B) * h2)
     for k in some:
         res = line[k][...] + mxu(w2t_ref[...], act[k][...])
         first = n % PER * BT + SUB * k
@@ -848,7 +937,7 @@
 
 
 def forward_kernel(t_own, t_high, own_ref, x_hbm, tgt_hbm, q_ref, base_ref, w1_ref, w2t_ref, dout_hbm, dz_hbm, q_low, grads_ref,
-                   tbuf, ubuf, turned, ball, xbuf, tgtbuf, dbuf, zbuf, g_ref, gt_ref, line, yb, hid, act, db, dh,
+                   tbuf, across, ubuf, turned, ball, xbuf, tgtbuf, dbuf, zbuf, g_ref, gt_ref, line, yb, hid, act, db, dh,
                    s_t, s_in, s_out, s_q, s_low, *sems):
     p = Place()
     y = p.y
@@ -873,15 +962,15 @@
     def loads(n):
         b, t = block(n)
         return [
-            pltpu.make_async_copy(src.at[b, :, t], dst.at[n % 2], s_in.at[i, n % 2])
+            pltpu.make_async_copy(src.at[b, :, t], dst.at[n % BUFFERS], s_in.at[i, n % BUFFERS])
             for i, (src, dst) in enumerate(((x_hbm, xbuf), (tgt_hbm, tgtbuf)))
         ]
 
     def stores(n):
         b, t = block(n)
         return [
-            pltpu.make_async_copy(dbuf.at[n % 2], dout_hbm.at[b, t], s_out.at[0, n % 2]),
-            pltpu.make_async_copy(zbuf.at[n % 2], dz_hbm.at[t, :, lanes(b)], s_out.at[1, n % 2]),
+            pltpu.make_async_copy(dbuf.at[n % BUFFERS], dout_hbm.at[b, t], s_out.at[0, n % BUFFERS]),
+            pltpu.make_async_copy(zbuf.at[n % BUFFERS], dz_hbm.at[t, :, lanes(b)], s_out.at[1, n % BUFFERS]),
         ]
 
     def give_q(g):
@@ -895,21 +984,31 @@
         start_t(g)
 
     p.greet([p.sibling, p.xn, p.yn])
-    gather.give(piece(0, 0))
-    for g in reversed(range(LATE)):
-        wait_local(SUB * y + g)
-        give_q(g).start()
-        if g == LATE - 1:
-            gather.give(piece(0, 1))
+    each(gather.give, 0)
     for copy in loads(0):
         copy.start()
     ball[p.x, p.c, y, :ROWS] = own_ref[...]
     for d in range(PLANE):
         ball[*slot_index(d), ROWS:] = jnp.zeros((SPARE, LANES), F32)
     grads_ref[...] = jnp.zeros_like(grads_ref)
-    gt_ref[...] = signed(base_ref[...], y, 2)
+    gt_ref[...] = signed(base_ref, y, 2)
     g_ref[...] = gt_ref[...].T
+    def across_table(g):
+        for i in range(PAIRS):
+            across[g, i] = tbuf[g, i].T
+
+    @pl.loop(0, GROUPS)
+    def _(g):
+        at = g % SUB
+
+        @pl.when((at >= LATE) | (g // SUB == y))
+        def _():
+            wait_local(g)
+            across_table(g)
+
     each(gather.pass_on, 0)
+    for g in reversed(range(LATE)):
+        give_q(g).start()
     each(gather.give, 1)
     each(gather.collect, 0)
 
@@ -922,25 +1021,14 @@
                 g = 4 * k + 3 - n
                 at = g % SUB
 
-                @pl.when((s == 0) & (at >= LATE))
-                def _():
-                    wait_local(g)
-
                 @pl.when((s == 0) & (at < LATE) & (g // SUB != y))
                 def _():
                     give_q(at).wait_recv()
                     store_low(at).start()
-
-                inverse_sums(tbuf, ball, turned, g, k, lanes(s), SUB)
+                    across_table(g)
+
+                inverse_sums(lambda g, i: across[g, i], ball, turned, g, k, lanes(s), SUB)
                 ubuf[:, pl.ds(pl.multiple_of(SUB * g, SUB), SUB)] = turn(turned[...])
-
-        @pl.when(s + 1 < NB)
-        def _():
-            each(gather.pass_on, s + 1)
-
-        @pl.when(s + 2 < NB)
-        def _():
-            each(gather.give, s + 2)
 
         @pl.loop(0, PER)
         def _(i):
@@ -953,25 +1041,33 @@
                 for copy in loads(n + 1):
                     copy.start()
 
-            @pl.when(n > 1)
+            @pl.when(n >= BUFFERS)
             def _():
-                for copy in stores(n - 2):
+                for copy in stores(n - BUFFERS):
                     copy.wait()
 
             orders = [ubuf.at[pl.ds(pl.multiple_of(i * BT + SUB * k, SUB), SUB)] for k in range(BT // SUB)]
             grid_stage(
-                n, orders, xbuf.at[n % 2], tgtbuf.at[n % 2], q_ref, (g_ref, gt_ref, w1_ref, w2t_ref),
-                dbuf.at[n % 2], zbuf.at[n % 2], grads_ref, (line, yb, hid, act, db, dh),
+                n, orders, xbuf.at[n % BUFFERS], tgtbuf.at[n % BUFFERS], q_ref, (g_ref, gt_ref, w1_ref, w2t_ref),
+                dbuf.at[n % BUFFERS], zbuf.at[n % BUFFERS], grads_ref, (line, yb, hid, act, db, dh),
             )
             for copy in stores(n):
                 copy.start()
 
-            @pl.when((i == 1) & (s + 1 < NB))
+            @pl.when((i == 0) & (s + 1 < NB))
+            def _():
+                each(gather.pass_on, s + 1)
+
+            @pl.when((i == 0) & (s + 2 < NB))
+            def _():
+                each(gather.give, s + 2)
+
+            @pl.when((i == 2) & (s + 1 < NB))
             def _():
                 each(gather.collect, s + 1)
 
-    for n in range(2):
-        for copy in stores(NB * PER - 2 + n):
+    for n in range(BUFFERS):
+        for copy in stores(NB * PER - BUFFERS + n):
             copy.wait()
 
     @pl.loop(0, NB)
@@ -985,16 +1081,16 @@
 
 def forward(table, own, x, target, q, base, w1, w2t, cid):
     hid = 2 * CH
-    grid, two = (2, CH, BT, NN), BT // SUB
+    grid, two = (BUFFERS, CH, BT, NN), BT // SUB
     return call(
         forward_kernel,
         [(NB, NT, CH, NN), (NT, NM, LANES), (LATE, *HALF_TABLE[1:]), (CH, LANES)],
         [
-            vmem(GROUPS, SUB, NT, NL), vmem(NT, NM, LN), vmem(SUB, NT, LN), vmem(*SLOTS, ROWS + SPARE, LANES),
-            vmem(*grid), vmem(*grid), vmem(2, BT, CH, NN), vmem(2, BT, NM, LN), vmem(NN, NN), vmem(NN, NN),
+            vmem(GROUPS, *HALF_TABLE[1:]), vmem(GROUPS, *HALF_TABLE[1:]), vmem(NT, NM, LN), vmem(SUB, NT, LN), vmem(*SLOTS, ROWS + SPARE, LANES),
+            vmem(*grid), vmem(*grid), vmem(BUFFERS, BT, CH, NN), vmem(BUFFERS, BT, NM, LN), vmem(NN, NN), vmem(NN, NN),
             vmem(two, CH, WIDE), vmem(two, CH, WIDE, dtype=BF16), vmem(two, hid, WIDE), vmem(two, hid, WIDE, dtype=BF16),
             vmem(two, CH, WIDE, dtype=BF16), vmem(two, hid, WIDE, dtype=BF16),
-            dma_sems(GROUPS), dma_sems(2, 2), dma_sems(2, 2), dma_sems(2, LATE), dma_sems(LATE),
+            dma_sems(GROUPS), dma_sems(2, BUFFERS), dma_sems(2, BUFFERS), dma_sems(2, LATE), dma_sems(LATE),
         ] + [dma_sems(2, 2 * NB)] * 8,
         cid=cid,
         in_specs=[ANY, ANY, VMEM, ANY, ANY, SMEM, VMEM, VMEM, VMEM],
@@ -1026,7 +1122,7 @@
                  g_ref, s0_ref, s1_ref):
     @pl.when(first_step())
     def _():
-        g_ref[...] = signed(base_ref[...], Place().y, 1).T
+        g_ref[...] = signed(base_ref, Place().y, 1).T
         gspec_ref[0] = spec_ref[:, :, :CH]
         gspec_ref[1] = spec_ref[:, :, CH:]
         grads = ext_ref[:, SUB:].reshape(CH, LANES)
@@ -1042,14 +1138,14 @@
             s1_ref[chans] = s1[:CH] + s1[CH:]
 
     chans = pl.ds(pl.multiple_of(pl.program_id(0) * CH, CH), CH)
-    inv = inv_ref[:, :1]
+    inv = col(inv_ref[...])
     slope = inv_ref[...] * inv_ref[...] * s1_ref[chans]
 
     @pl.loop(0, FINAL_T // SUB)
     def _(k):
         ts = pl.ds(pl.multiple_of(SUB * k, SUB), SUB)
         dn = to_grid(u_ref[ts], g_ref[...]).reshape(SUB, CH, NN)
-        r = turn(dout_ref[0, ts] + inv * (dn - s0_ref[chans, :1]))
+        r = turn(dout_ref[0, ts] + inv * (dn - col(s0_ref[chans])))
         for c in range(CH):
             for n in range(NN // LN):
                 lanes = slice(LN * n, LN * (n + 1))
@@ -1067,7 +1163,7 @@
         grid=(NB, NT // FINAL_T),
         in_specs=[
             orders, grid, lines, CHAN_SPEC, CHAN_SPEC,
-            whole(PLANE, 2 * SUB, LANES), whole(degrees, CH, LN), whole(NN, NN),
+            whole(PLANE, 2 * SUB, LANES), whole(degrees, CH, LN), whole(4, DFT_STEP, NM),
         ],
         out_specs=(grid, whole(2, degrees, CH, CH), whole(CH, hid), whole(CH, hid), whole(1, 1)),
         name="final",
@@ -1076,9 +1172,9 @@
 
 def solution(mesh):
     def local_step(x, target, q, leg_fwd, leg_inv, spec_w, w1, w2):
-        base = jnp.asarray(dft_matrix())
-        p_own, q_own = (jnp.swapaxes(v, 1, 2).reshape(HALF_TABLE) for v in (leg_fwd, leg_inv))
-        z, p_peer, mu, inv, c0, kern = front(x, p_own, jnp.moveaxis(spec_w, 1, 3), base, 0)
+        base = jnp.asarray(dft_tables())
+        p_raw, q_raw = (jnp.swapaxes(v, 1, 2).reshape(RAW_TABLE) for v in (leg_fwd, leg_inv))
+        z, p_own, p_peer, q_own, mu, inv, c0, kern = front(x, p_raw, q_raw, jnp.moveaxis(spec_w, 1, 3), base, 0)
         a, b, q_high = analyze((p_own, p_peer), z, 1, kern, q_own=q_own)
         dout, dz, q_low, grads = forward((q_own, q_high), b, x, target, q, base, w1, w2.T, 2)
         da, dk = analyze((q_own, q_low, q_high), dz, 3, kern, back=(grads, a, c0))
@@ -1092,6 +1188,6 @@
         local_step,
         mesh=mesh,
         in_specs=(grid_spec, grid_spec, P("h"), table_spec, table_spec, P(), P(), P()),
-        out_specs=(P(), grid_spec, P(None, "h", None, None), P(), P()),
+        out_specs=(P(), grid_spec, P(None, "h"), P(), P()),
         check_vma=False,
     )

time: 449 us -> 429 us (0.955)
  Pallas kernels: 448 us -> 427 us
    pallas_call x1, Pallas kernels: 52.9 us -> 43.4 us  [front(): call(front_kernel, [(NT, NM, LANES), HALF_TABLE, HALF_TABLE, HALF_TABLE,...]
    pallas_call x2, Pallas kernels: 171 us -> 165 us  [analyze(): call(lambda *refs: analyze_kernel(share, with_q, *refs), outs, [degrees,...]
    pallas_call x1, Pallas kernels: 121 us -> 116 us  [forward(): call(forward_kernel, [(NB, NT, CH, NN), (NT, NM, LANES), (LATE, *HALF_TAB...]
where the time goes in v4:
time: 429 us; the launch traced here: 428 us
  Pallas kernels  427 us (100%)
    pallas_call x2, Pallas kernels, analyze(): call(lambda *refs: analyze_kernel(share, with_q, *refs), outs, [degrees,...  165 us
    pallas_call x1, Pallas kernels, forward(): call(forward_kernel, [(NB, NT, CH, NN), (NT, NM, LANES), (LATE, *HALF_TAB...  116 us
    pallas_call x1, Pallas kernels, synth(): call(synth_kernel, [(NT, NM, LANES), (PLANE, 2 * SUB, LANES), (4, SUB, CH...  77.2 us
    pallas_call x1, Pallas kernels, front(): call(front_kernel, [(NT, NM, LANES), HALF_TABLE, HALF_TABLE, HALF_TABLE,...  43.4 us
    pallas_call x1, Pallas kernels, final(): call(final_kernel, [(NB, CH, NT, NN), (2, degrees, CH, CH), (CH, hid), (C...  25.8 us

profile of v4, /device:TPU:1, one launch (start us, length us, event | category | flops | bytes accessed | tf_op | source)
XLA Modules:
  0.0 428.3 jit_solution(9644239057306614103)
XLA Ops:
  0.6 43.4 %front.1 = (f32[64,128,384]{2,1,0:T(8,128)}, f32[8,4,128,128]{3,2,1,0:T(8,128)}, f32[8,4,128,128]{3,2,1,0:T(8,128)}, f32[8,4,128,128]{3,2,1,0:T(8,128)}, f32[192...) custom-call(f32[3,64,64,256]{3,2,1,0:T(8,128)} %x_ref.1, ...), custom_call_target="tpu_custom_call" | custom-call | tf_op jit(solution)/shard_map/front/pallas_call | solution.py:365
  44.0 88.9 %analyze_1.1 = (f32[1104,384]{1,0:T(8,128)}, f32[1104,384]{1,0:T(8,128)}, f32[6,4,128,128]{3,2,1,0:T(8,128)}) custom-call(f32[8,4,128,128]{3,2,1,0:T(8,128)} %get-tuple-element.30.refs_0_.t_own, f32[8,4,128,128]{3,2,1,0:T(8,128)} %get-tuple-element.31.refs_1_.t_peer, f32[64,128,384]{2,1,0:T(8,128)} %get-tuple-element.33.refs_2_, ...), custom_call_target="tpu_custom_call" | custom-call | tf_op jit(solution)/shard_map/analyze_1/pallas_call | solution.py:660
  132.9 116.0 %forward.1 = (f32[3,64,64,256]{3,2,1,0:T(8,128)}, f32[64,128,384]{2,1,0:T(8,128)}, f32[2,4,128,128]{3,2,1,0:T(8,128)}, f32[64,384]{1,0:T(8,128)}) custom-call(f32[8,4,128,128]{3,2,1,0:T(8,128)} %get-tuple-element.32.refs_3_.t_own.refs_0_, f32[6,4,128,128]{3,2,1,0:T(8,128)} %get-tuple-element.35.t_high.refs_2_, f32[1104,384]{1,0:T(8,128)} %get-tuple-element.36.own_ref, ...), custom_call_target="tpu_custom_call" | custom-call | tf_op jit(solution)/shard_map/forward/pallas_call | solution.py:1085
  248.9 76.2 %analyze_3.1 = (f32[1104,384]{1,0:T(8,128)}, f32[2,8,64,128]{3,2,1,0:T(8,128)}) custom-call(f32[8,4,128,128]{3,2,1,0:T(8,128)} %get-tuple-element.32.refs_3_.t_own.refs_0_, f32[2,4,128,128]{3,2,1,0:T(8,128)} %get-tuple-element.37.refs_1_, f32[6,4,128,128]{3,2,1,0:T(8,128)} %get-tuple-element.35.t_high.refs_2_, f32[64,128,384]{2,1,0:T(8,128)} %get-tuple-element.38.refs_3_, ...), custom_call_target="tpu_custom_call" | custom-call | tf_op jit(solution)/shard_map/analyze_3/pallas_call | solution.py:660
  325.1 77.2 %synth_4.1 = (f32[64,128,384]{2,1,0:T(8,128)}, f32[8,16,384]{2,1,0:T(8,128)}, f32[4,8,64,128]{3,2,1,0:T(8,128)}) custom-call(f32[8,4,128,128]{3,2,1,0:T(8,128)} %get-tuple-element.30.refs_0_.t_own, f32[8,4,128,128]{3,2,1,0:T(8,128)} %get-tuple-element.31.refs_1_.t_peer, f32[1104,384]{1,0:T(8,128)} %get-tuple-element.42.own_ref, ...), custom_call_target="tpu_custom_call" | custom-call | tf_op jit(solution)/shard_map/synth_4/pallas_call | solution.py:873
  402.3 25.8 %final.1 = (f32[3,64,64,256]{3,2,1,0:T(8,128)}, f32[2,32,64,64]{3,2,1,0:T(8,128)}, f32[64,128]{1,0:T(8,128)}, f32[64,128]{1,0:T(8,128)}, f32[1,1]{1,0:T(1,128)}) custom-call(f32[64,128,384]{2,1,0:T(8,128)} %get-tuple-element.44.u_ref, f32[3,64,64,256]{3,2,1,0:T(8,128)} %x_ref.1, f32[3,64,64,256]{3,2,1,0:T(8,128)} %get-tuple-element.45.dout_ref, ...), custom_call_target="tpu_custom_call" | custom-call | tf_op jit(solution)/shard_map/final/pallas_call | solution.py:1159

commit v5 on v4

--- a/solution.py
+++ b/solution.py
@@ -30,6 +30,7 @@
 GROUPS = NM // SUB
 PLANE, Z = 8, 4
 PAIRS = SUB // 2
+FIRST_GROUPS = 3
 H_OF_PAIR = (0, 0, 3, 3, 1, 1, 2, 2)
 BLOCK = SUB * SUB
 PLACES = GROUPS + 1
@@ -46,7 +47,7 @@
 NN_DIMS, NT_DIMS, TN_DIMS = ((1,), (0,)), ((1,), (1,)), ((0,), (0,))
 SUM_ENDS = (2, 5, 8, 11, 14, 16, 17)
 GATHER_ENDS = (3, 6, 9, 12, 15, 17)
-MIX_AFTER = (1, 3, 4, 5, 6), (2, 4, 6)
+MIX_AFTER = (2, 3, 4, 6)
 
 SMEM = pl.BlockSpec(memory_space=pltpu.SMEM)
 VMEM = pl.BlockSpec(memory_space=pltpu.VMEM)
@@ -149,9 +150,9 @@
     return ends[i - 1] if i > 0 else 0
 
 
-def chunk(i, share, ends):
+def chunk(i, share, ends, last=ROWS):
     lo = start_of(i, ends) * BLOCK
-    hi = ends[i] * BLOCK if ends[i] < PLACES else ROWS
+    hi = ends[i] * BLOCK if ends[i] < PLACES else last
     return lo, lo + (hi - lo) * share // (2 * BLOCK) * SUB, hi
 
 
@@ -480,7 +481,7 @@
         s_ref[...] = jnp.zeros_like(s_ref)
     tbuf, zbuf, turned, part, sib, rx, ry, fx, fy, s_t, s_z, s_q, s_sib, s_x, s_y, s_fx, s_fy = rest
     count = len(SUM_ENDS)
-    mix_after = MIX_AFTER[0 if with_q else 1]
+    end = DATA if with_q else ROWS
     p = Place()
     x, c, y = p.x, p.c, p.y
     start_t, wait_t = table_loader(t_own, peers, tbuf, s_t, y)
@@ -488,17 +489,19 @@
     def load_z(g):
         return pltpu.make_async_copy(z_hbm.at[:, pl.ds(pl.multiple_of(SUB * g, SUB), SUB)], zbuf.at[g], s_z.at[g])
 
-    @pl.loop(0, GROUPS)
-    def _(g):
-        start_t(g)
-        load_z(g).start()
-
+    def loads(lo, hi):
+        @pl.loop(lo, hi)
+        def _(g):
+            start_t(g)
+            load_z(g).start()
+
+    loads(0, FIRST_GROUPS)
     p.greet([p.sibling, p.xn, p.yn])
+    loads(FIRST_GROUPS, GROUPS)
     for d in range(PLANE):
-        spare = part.at[slot_index(d)]
-        spare[STAT:ROWS] = jnp.zeros((ROWS - STAT, LANES), F32)
         if not with_q:
-            spare[STAT:GRAD] = ext_ref[SUB * d:SUB * (d + 1)]
+            part[*slot_index(d), STAT:GRAD] = ext_ref[SUB * d:SUB * (d + 1)]
+            part[*slot_index(d), GRAD:ROWS] = jnp.zeros((SUB, LANES), F32)
 
     def load_q(g):
         return pltpu.make_async_copy(q_own.at[LATE + g], qbuf.at[g], s_q.at[2, g])
@@ -534,27 +537,27 @@
                         part[xj, cj, yj, pl.ds(pl.multiple_of(row, SUB), SUB), :] = r[SUB * n:SUB * (n + 1)]
 
     def to_sibling(i):
-        lo, _, hi = chunk(i, share, SUM_ENDS)
+        lo, _, hi = chunk(i, share, SUM_ENDS, end)
         return send(part.at[:, 1 - c, :, rows(lo, hi)], sib.at[:, :, rows(lo, hi)], s_sib, i, p.sibling)
 
     def to_x(i):
-        lo, mid, _ = chunk(i, share, SUM_ENDS)
+        lo, mid, _ = chunk(i, share, SUM_ENDS, end)
         return send(part.at[p.ox, c, :, rows(lo, mid)], rx.at[:, rows(lo, mid)], s_x, i, p.xn)
 
     def to_y(i):
-        _, mid, hi = chunk(i, share, SUM_ENDS)
+        _, mid, hi = chunk(i, share, SUM_ENDS, end)
         return send(part.at[:, c, p.oy, rows(mid, hi)], ry.at[:, rows(mid, hi)], s_y, i, p.yn)
 
     def forward_y(i):
-        lo, mid, _ = chunk(i, share, SUM_ENDS)
+        lo, mid, _ = chunk(i, share, SUM_ENDS, end)
         return send(part.at[x, c, p.oy, rows(lo, mid)], fy.at[rows(lo, mid)], s_fy, i, p.yn)
 
     def forward_x(i):
-        _, mid, hi = chunk(i, share, SUM_ENDS)
+        _, mid, hi = chunk(i, share, SUM_ENDS, end)
         return send(part.at[p.ox, c, y, rows(mid, hi)], fx.at[rows(mid, hi)], s_fx, i, p.xn)
 
     def chip_sum(i):
-        lo, _, hi = chunk(i, share, SUM_ENDS)
+        lo, _, hi = chunk(i, share, SUM_ENDS, end)
         to_sibling(i).wait_recv()
 
         @pl.loop(lo, hi, step=2 * SUB)
@@ -567,6 +570,7 @@
         to_x(i).start()
         to_y(i).start()
         if with_q and i < EARLY:
+            load_q(i).wait()
             give_q(i).start()
 
     def add(lo, hi, *sums):
@@ -577,7 +581,7 @@
                 to[some] = a[some] + b[some]
 
     def half_sum(i):
-        lo, mid, hi = chunk(i, share, SUM_ENDS)
+        lo, mid, hi = chunk(i, share, SUM_ENDS, end)
         to_x(i).wait_recv()
         other = part.at[x, c, p.oy]
         add(lo, mid, (other, other, rx.at[p.oy]))
@@ -591,7 +595,7 @@
         add(mid, hi, (out_ref, mine, ry.at[x]))
 
     def last_sum(i):
-        lo, mid, hi = chunk(i, share, SUM_ENDS)
+        lo, mid, hi = chunk(i, share, SUM_ENDS, end)
         forward_y(i).wait_recv()
         add(lo, mid, (out_ref, out_ref, fy))
         forward_x(i).wait_recv()
@@ -609,8 +613,6 @@
         for g in range(EARLY):
             load_q(g).start()
             clear_q(g).start()
-        for g in range(EARLY):
-            load_q(g).wait()
     for i in range(count + LAST_LAG):
         if i < count:
             for step in quarters(max(start_of(i, SUM_ENDS) - 1, 0), SUM_ENDS[i] - 1):
@@ -622,9 +624,9 @@
             half_sum(i - HALF_LAG)
         if i >= LAST_LAG:
             last_sum(i - LAST_LAG)
-            if i - LAST_LAG in mix_after:
-                n = mix_after.index(i - LAST_LAG)
-                mixed(start_of(n, [SUM_ENDS[m] for m in mix_after]), SUM_ENDS[i - LAST_LAG])
+            if i - LAST_LAG in MIX_AFTER:
+                n = MIX_AFTER.index(i - LAST_LAG)
+                mixed(start_of(n, [SUM_ENDS[m] for m in MIX_AFTER]), SUM_ENDS[i - LAST_LAG])
     if with_q:
         mix_ref[STAT:] = jnp.zeros((ROWS - STAT, LANES), F32)
     else:
@@ -949,7 +951,7 @@
         return pl.ds(pl.multiple_of(LN * s, LN), LN)
 
     def piece(s, half):
-        lo, hi = ((0, FIRST), (FIRST, ROWS))[half]
+        lo, hi = ((0, FIRST), (FIRST, DATA))[half]
         return 2 * s + half, lo, lo + (hi - lo) * share // BLOCK * SUB, hi, lanes(s)
 
     def each(step, s):

time: 429 us -> 421 us (0.981)
  Pallas kernels: 427 us -> 419 us
    pallas_call x2, Pallas kernels: 165 us -> 158 us  [analyze(): call(lambda *refs: analyze_kernel(share, with_q, *refs), outs, [degrees,...]
where the time goes in v5:
time: 421 us; the launch traced here: 420 us
  Pallas kernels  419 us (100%)
    pallas_call x2, Pallas kernels, analyze(): call(lambda *refs: analyze_kernel(share, with_q, *refs), outs, [degrees,...  158 us
    pallas_call x1, Pallas kernels, forward(): call(forward_kernel, [(NB, NT, CH, NN), (NT, NM, LANES), (LATE, *HALF_TAB...  115 us
    pallas_call x1, Pallas kernels, synth(): call(synth_kernel, [(NT, NM, LANES), (PLANE, 2 * SUB, LANES), (4, SUB, CH...  77.9 us
    pallas_call x1, Pallas kernels, front(): call(front_kernel, [(NT, NM, LANES), HALF_TABLE, HALF_TABLE, HALF_TABLE,...  43.4 us
    pallas_call x1, Pallas kernels, final(): call(final_kernel, [(NB, CH, NT, NN), (2, degrees, CH, CH), (CH, hid), (C...  25.8 us

profile of v5, /device:TPU:1, one launch (start us, length us, event | category | flops | bytes accessed | tf_op | source)
XLA Modules:
  0.0 420.3 jit_solution(1075150116941216864)
XLA Ops:
  0.6 43.4 %front.1 = (f32[64,128,384]{2,1,0:T(8,128)}, f32[8,4,128,128]{3,2,1,0:T(8,128)}, f32[8,4,128,128]{3,2,1,0:T(8,128)}, f32[8,4,128,128]{3,2,1,0:T(8,128)}, f32[192...) custom-call(f32[3,64,64,256]{3,2,1,0:T(8,128)} %x_ref.1, ...), custom_call_target="tpu_custom_call" | custom-call | tf_op jit(solution)/shard_map/front/pallas_call | solution.py:366
  44.0 83.4 %analyze_1.1 = (f32[1104,384]{1,0:T(8,128)}, f32[1104,384]{1,0:T(8,128)}, f32[6,4,128,128]{3,2,1,0:T(8,128)}) custom-call(f32[8,4,128,128]{3,2,1,0:T(8,128)} %get-tuple-element.30.refs_0_.t_own, f32[8,4,128,128]{3,2,1,0:T(8,128)} %get-tuple-element.31.refs_1_.t_peer, f32[64,128,384]{2,1,0:T(8,128)} %get-tuple-element.33.refs_2_, ...), custom_call_target="tpu_custom_call" | custom-call | tf_op jit(solution)/shard_map/analyze_1/pallas_call | solution.py:662
  127.4 114.5 %forward.1 = (f32[3,64,64,256]{3,2,1,0:T(8,128)}, f32[64,128,384]{2,1,0:T(8,128)}, f32[2,4,128,128]{3,2,1,0:T(8,128)}, f32[64,384]{1,0:T(8,128)}) custom-call(f32[8,4,128,128]{3,2,1,0:T(8,128)} %get-tuple-element.32.refs_3_.t_own.refs_0_, f32[6,4,128,128]{3,2,1,0:T(8,128)} %get-tuple-element.35.t_high.refs_2_, f32[1104,384]{1,0:T(8,128)} %get-tuple-element.36.own_ref, ...), custom_call_target="tpu_custom_call" | custom-call | tf_op jit(solution)/shard_map/forward/pallas_call | solution.py:1087
  241.9 74.5 %analyze_3.1 = (f32[1104,384]{1,0:T(8,128)}, f32[2,8,64,128]{3,2,1,0:T(8,128)}) custom-call(f32[8,4,128,128]{3,2,1,0:T(8,128)} %get-tuple-element.32.refs_3_.t_own.refs_0_, f32[2,4,128,128]{3,2,1,0:T(8,128)} %get-tuple-element.37.refs_1_, f32[6,4,128,128]{3,2,1,0:T(8,128)} %get-tuple-element.35.t_high.refs_2_, f32[64,128,384]{2,1,0:T(8,128)} %get-tuple-element.38.refs_3_, ...), custom_call_target="tpu_custom_call" | custom-call | tf_op jit(solution)/shard_map/analyze_3/pallas_call | solution.py:662
  316.4 77.9 %synth_4.1 = (f32[64,128,384]{2,1,0:T(8,128)}, f32[8,16,384]{2,1,0:T(8,128)}, f32[4,8,64,128]{3,2,1,0:T(8,128)}) custom-call(f32[8,4,128,128]{3,2,1,0:T(8,128)} %get-tuple-element.30.refs_0_.t_own, f32[8,4,128,128]{3,2,1,0:T(8,128)} %get-tuple-element.31.refs_1_.t_peer, f32[1104,384]{1,0:T(8,128)} %get-tuple-element.42.own_ref, ...), custom_call_target="tpu_custom_call" | custom-call | tf_op jit(solution)/shard_map/synth_4/pallas_call | solution.py:875
  394.3 25.8 %final.1 = (f32[3,64,64,256]{3,2,1,0:T(8,128)}, f32[2,32,64,64]{3,2,1,0:T(8,128)}, f32[64,128]{1,0:T(8,128)}, f32[64,128]{1,0:T(8,128)}, f32[1,1]{1,0:T(1,128)}) custom-call(f32[64,128,384]{2,1,0:T(8,128)} %get-tuple-element.44.u_ref, f32[3,64,64,256]{3,2,1,0:T(8,128)} %x_ref.1, f32[3,64,64,256]{3,2,1,0:T(8,128)} %get-tuple-element.45.dout_ref, ...), custom_call_target="tpu_custom_call" | custom-call | tf_op jit(solution)/shard_map/final/pallas_call | solution.py:1161

commit v6 on v5

--- a/solution.py
+++ b/solution.py
@@ -910,9 +910,8 @@
         line[k][...] = wide(r0 + y)
         yb[k][...] = wide(y).astype(BF16)
     for k in some:
-        hid[k][...] = mxu(w1_ref[...], yb[k][...], TN_DIMS)
         for t in range(SUB):
-            h = hid[k][:, columns(t)]
+            h = mxu(w1_ref[...], yb[k][:, columns(t)], TN_DIMS)
             h2 = h * h
             th = jnp.tanh(h * (GELU_A + (GELU_A * GELU_B) * h2))
             cdf = HALF + HALF * th
@@ -930,8 +929,8 @@
             dout[SUB * k + t] = line[k][:, columns(t)]
     for k in some:
         dh[k][...] = (mxu(w2t_ref[...], db[k][...], TN_DIMS) * hid[k][...]).astype(BF16)
-        grads_ref[:, :LN] += mxu(yb[k][...], dh[k][...], NT_DIMS)
-        grads_ref[:, LN:2 * LN] += mxu(db[k][...], act[k][...], NT_DIMS)
+        grads_ref[:, :LN] += mxu(dh[k][...], yb[k][...], NT_DIMS).T
+        grads_ref[:, LN:2 * LN] += mxu(act[k][...], db[k][...], NT_DIMS).T
     for k in some:
         dy = line[k][...] + mxu(w1_ref[...], dh[k][...])
         dys = jnp.concatenate([dy[:, columns(t)] for t in range(SUB)], axis=ROW)

time: 421 us -> 420 us (level)
  no operation moved by 1% of the time
where the time goes in v6:
time: 420 us; the launch traced here: 419 us
  Pallas kernels  419 us (100%)
    pallas_call x2, Pallas kernels, analyze(): call(lambda *refs: analyze_kernel(share, with_q, *refs), outs, [degrees,...  158 us
    pallas_call x1, Pallas kernels, forward(): call(forward_kernel, [(NB, NT, CH, NN), (NT, NM, LANES), (LATE, *HALF_TAB...  114 us
    pallas_call x1, Pallas kernels, synth(): call(synth_kernel, [(NT, NM, LANES), (PLANE, 2 * SUB, LANES), (4, SUB, CH...  77.9 us
    pallas_call x1, Pallas kernels, front(): call(front_kernel, [(NT, NM, LANES), HALF_TABLE, HALF_TABLE, HALF_TABLE,...  43.4 us
    pallas_call x1, Pallas kernels, final(): call(final_kernel, [(NB, CH, NT, NN), (2, degrees, CH, CH), (CH, hid), (C...  25.8 us

profile of v6, /device:TPU:1, one launch (start us, length us, event | category | flops | bytes accessed | tf_op | source)
XLA Modules:
  0.0 419.4 jit_solution(3202389958996456980)
XLA Ops:
  0.6 43.4 %front.1 = (f32[64,128,384]{2,1,0:T(8,128)}, f32[8,4,128,128]{3,2,1,0:T(8,128)}, f32[8,4,128,128]{3,2,1,0:T(8,128)}, f32[8,4,128,128]{3,2,1,0:T(8,128)}, f32[192...) custom-call(f32[3,64,64,256]{3,2,1,0:T(8,128)} %x_ref.1, ...), custom_call_target="tpu_custom_call" | custom-call | tf_op jit(solution)/shard_map/front/pallas_call | solution.py:366
  44.0 83.4 %analyze_1.1 = (f32[1104,384]{1,0:T(8,128)}, f32[1104,384]{1,0:T(8,128)}, f32[6,4,128,128]{3,2,1,0:T(8,128)}) custom-call(f32[8,4,128,128]{3,2,1,0:T(8,128)} %get-tuple-element.30.refs_0_.t_own, f32[8,4,128,128]{3,2,1,0:T(8,128)} %get-tuple-element.31.refs_1_.t_peer, f32[64,128,384]{2,1,0:T(8,128)} %get-tuple-element.33.refs_2_, ...), custom_call_target="tpu_custom_call" | custom-call | tf_op jit(solution)/shard_map/analyze_1/pallas_call | solution.py:662
  127.4 113.8 %forward.1 = (f32[3,64,64,256]{3,2,1,0:T(8,128)}, f32[64,128,384]{2,1,0:T(8,128)}, f32[2,4,128,128]{3,2,1,0:T(8,128)}, f32[64,384]{1,0:T(8,128)}) custom-call(f32[8,4,128,128]{3,2,1,0:T(8,128)} %get-tuple-element.32.refs_3_.t_own.refs_0_, f32[6,4,128,128]{3,2,1,0:T(8,128)} %get-tuple-element.35.t_high.refs_2_, f32[1104,384]{1,0:T(8,128)} %get-tuple-element.36.own_ref, ...), custom_call_target="tpu_custom_call" | custom-call | tf_op jit(solution)/shard_map/forward/pallas_call | solution.py:1086
  241.2 74.4 %analyze_3.1 = (f32[1104,384]{1,0:T(8,128)}, f32[2,8,64,128]{3,2,1,0:T(8,128)}) custom-call(f32[8,4,128,128]{3,2,1,0:T(8,128)} %get-tuple-element.32.refs_3_.t_own.refs_0_, f32[2,4,128,128]{3,2,1,0:T(8,128)} %get-tuple-element.37.refs_1_, f32[6,4,128,128]{3,2,1,0:T(8,128)} %get-tuple-element.35.t_high.refs_2_, f32[64,128,384]{2,1,0:T(8,128)} %get-tuple-element.38.refs_3_, ...), custom_call_target="tpu_custom_call" | custom-call | tf_op jit(solution)/shard_map/analyze_3/pallas_call | solution.py:662
  315.6 77.9 %synth_4.1 = (f32[64,128,384]{2,1,0:T(8,128)}, f32[8,16,384]{2,1,0:T(8,128)}, f32[4,8,64,128]{3,2,1,0:T(8,128)}) custom-call(f32[8,4,128,128]{3,2,1,0:T(8,128)} %get-tuple-element.30.refs_0_.t_own, f32[8,4,128,128]{3,2,1,0:T(8,128)} %get-tuple-element.31.refs_1_.t_peer, f32[1104,384]{1,0:T(8,128)} %get-tuple-element.42.own_ref, ...), custom_call_target="tpu_custom_call" | custom-call | tf_op jit(solution)/shard_map/synth_4/pallas_call | solution.py:875
  393.5 25.8 %final.1 = (f32[3,64,64,256]{3,2,1,0:T(8,128)}, f32[2,32,64,64]{3,2,1,0:T(8,128)}, f32[64,128]{1,0:T(8,128)}, f32[64,128]{1,0:T(8,128)}, f32[1,1]{1,0:T(1,128)}) custom-call(f32[64,128,384]{2,1,0:T(8,128)} %get-tuple-element.44.u_ref, f32[3,64,64,256]{3,2,1,0:T(8,128)} %x_ref.1, f32[3,64,64,256]{3,2,1,0:T(8,128)} %get-tuple-element.45.dout_ref, ...), custom_call_target="tpu_custom_call" | custom-call | tf_op jit(solution)/shard_map/final/pallas_call | solution.py:1160
